TPU v7x, 8 devices: a whole 2x2x1 slice. The times are simulated.
8 devices in a mesh: dp: 1 (over z), ep_b: 2 (over y), ep_a: 4 (over x, core).
Axes of the slice: x: 2, y: 2, z: 1, core: 2. Of those that a mesh axis runs over, the one named last changes fastest.
Arguments:
- tokens: bfloat16 [8, 8192, 384], P(('dp', 'ep_b', 'ep_a'))
- expert_ids: int32 [8, 8192], P(('dp', 'ep_b', 'ep_a'))
- route_order: int32 [8, 8192], P(('dp', 'ep_b', 'ep_a'))
- w_route: bfloat16 [384, 256], replicated
- expert_keys: bfloat16 [8, 256], replicated
- temperature: float32 [], replicated
- w_in: bfloat16 [8, 384, 1536], P(('ep_b', 'ep_a'))
- b_in: bfloat16 [8, 1536], P(('ep_b', 'ep_a'))
- w_out: bfloat16 [8, 1536, 384], P(('ep_b', 'ep_a'))
- b_out: bfloat16 [8, 384], P(('ep_b', 'ep_a'))
Outputs:
- output: bfloat16 [8, 8192, 384], P(('dp', 'ep_b', 'ep_a'))
All inputs are finite; a program needn't handle non-finite values.
Results may differ from a plain program's by a relative error of at most 0.002588.
Values are sent between devices in bfloat16 or wider.
A program may use at most 1 GiB of HBM per device.

v0:
```python
import functools

import jax
import jax.numpy as jnp
from jax import lax
from jax.experimental import pallas as pl
from jax.experimental.pallas import tpu as pltpu
from jax.sharding import PartitionSpec as P


EXPERT_AXES = ("ep_b", "ep_a")

LANES = 128
BLOCK_ROWS = 4
GRAN = 16
BF16 = jnp.bfloat16
F32 = jnp.float32
NT = (((1,), (1,)), ((), ()))


def iota(shape, dim):
    return lax.broadcasted_iota(jnp.int32, shape, dim)


def plan_step(num_experts, capacity, ids_ref, ord_ref, wr_ref, keys_ref, pos_ref, start_ref, count_ref, wt_ref):
    rows = ids_ref.shape[0]
    blocks = rows // BLOCK_ROWS
    place = jnp.zeros((2 * rows, LANES), F32)
    hi_iota = iota((rows, LANES), 0)
    lo_iota = iota((LANES, LANES), 0)
    lane_val = iota((rows, LANES), 1).astype(F32)
    for chunk in range(rows // 8):
        left, right = [], []
        for r in range(8 * chunk, 8 * chunk + 8):
            order_row = ord_ref[r : r + 1, :]
            hit = hi_iota == (order_row >> 7)
            upper = jnp.where(hit, F32(r), 0.0).astype(BF16)
            lower = jnp.where(hit, lane_val, 0.0).astype(BF16)
            left.append(jnp.concatenate([upper, lower], axis=0))
            right.append(jnp.where(lo_iota == (order_row & 127), 1.0, 0.0).astype(BF16))
        place += lax.dot_general(jnp.concatenate(left, axis=1), jnp.concatenate(right, axis=1), NT, preferred_element_type=F32)
    place = (place[:rows] * LANES + place[rows:]).astype(jnp.int32)
    ids = ids_ref[...]
    mask = (ids[None] == iota((num_experts, rows, LANES), 0)).astype(F32)

    def narrow(step, bound):
        trial = bound + (2 * rows * LANES >> (step + 1))
        admitted = jnp.where(place[None] < trial, mask, 0.0)
        total = jnp.sum(jnp.sum(admitted, axis=1, keepdims=True), axis=2, keepdims=True)
        return jnp.where(total <= capacity, trial, bound)

    steps = (rows * LANES).bit_length()
    bound = lax.fori_loop(0, steps, narrow, jnp.zeros((num_experts, 1, 1), jnp.int32))
    kept = jnp.where(place[None] < bound, mask, 0.0)
    kept2 = kept.reshape(num_experts * rows, LANES).astype(BF16)
    before = (iota((LANES, LANES), 0) < iota((LANES, LANES), 1)).astype(BF16)
    lane_prefix = jnp.dot(kept2, before, preferred_element_type=F32)
    row_total = jnp.dot(kept2, jnp.ones((LANES, LANES), BF16), preferred_element_type=F32).astype(BF16)
    row_a, row_b = iota((rows, rows), 0), iota((rows, rows), 1)
    same = row_a // BLOCK_ROWS == row_b // BLOCK_ROWS
    earlier = (same & (row_b < row_a)).astype(BF16)
    same = same.astype(BF16)
    pick = (iota((blocks, rows), 1) == iota((blocks, rows), 0) * BLOCK_ROWS).astype(BF16)
    lane = iota((blocks, LANES), 1)
    slot = jnp.full((rows, LANES), -1, jnp.int32)
    first = jnp.zeros((rows, LANES), jnp.int32)
    starts = jnp.zeros((blocks, LANES), F32)
    counts = jnp.zeros((blocks, LANES), F32)
    for e in range(num_experts):
        part = slice(e * rows, (e + 1) * rows)
        row_prefix = jnp.dot(earlier, row_total[part], preferred_element_type=F32)
        in_block = jnp.dot(same, row_total[part], preferred_element_type=F32).astype(jnp.int32)
        grans = (in_block + (GRAN - 1)) >> 4
        here = first * GRAN + (row_prefix + lane_prefix[part]).astype(jnp.int32)
        slot = jnp.where(kept[e] > 0.0, here, slot)
        starts += jnp.where(lane == e, jnp.dot(pick, first.astype(F32).astype(BF16), preferred_element_type=F32), 0.0)
        counts += jnp.where(lane == e, jnp.dot(pick, grans.astype(F32).astype(BF16), preferred_element_type=F32), 0.0)
        first = first + grans
    pos_ref[...] = slot
    start_ref[...] = starts.astype(jnp.int32)
    count_ref[...] = counts.astype(jnp.int32)
    wr = wr_ref[...]
    router = wr.shape[1]
    eye = (iota((router, router), 0) == iota((router, router), 1)).astype(BF16)
    keys = keys_ref[...].astype(F32)
    unit = keys / jnp.sqrt(jnp.sum(keys * keys, axis=1, keepdims=True))
    folded = lax.dot_general(unit, wr.astype(F32), NT, preferred_element_type=F32, precision=lax.Precision.HIGHEST)
    part_a = folded.astype(BF16)
    rest = folded - part_a.astype(F32)
    part_b = rest.astype(BF16)
    part_c = (rest - part_b.astype(F32)).astype(BF16)
    wt_ref[0:router, :] = lax.dot_general(eye, wr, NT, preferred_element_type=F32).astype(BF16)
    tail = jnp.concatenate([part_a.astype(F32), part_b.astype(F32), part_c.astype(F32), jnp.zeros_like(folded)], axis=0)
    wt_ref[router:, :] = tail.astype(BF16)


def dispatch_kernel(
    router, num_experts, capacity, slots, tau_ref, ids_ref, ord_ref, wr_ref, keys_ref, x_ref,
    pos_ref, start_ref, count_ref, gate_ref, xs_ref, wt_ref,
):
    @pl.when(pl.program_id(0) == 0)
    def _():
        plan_step(num_experts, capacity, ids_ref, ord_ref, wr_ref, keys_ref, pos_ref, start_ref, count_ref, wt_ref)

    rows = x_ref.shape[0] // LANES
    part = pl.ds(pl.multiple_of(pl.program_id(0) * rows, rows), rows)
    ids, pos = ids_ref[part, :], pos_ref[part, :]
    tau = tau_ref[0, 0]
    for sub in range(rows // BLOCK_ROWS):
        row0 = sub * BLOCK_ROWS
        x = x_ref[row0 * LANES : (row0 + BLOCK_ROWS) * LANES, :]
        proj = lax.dot_general(wt_ref[...], x, NT, preferred_element_type=F32)
        square = jnp.sum(proj[:router] * proj[:router], axis=0, keepdims=True)
        ne = num_experts
        logits = proj[router : router + ne] + proj[router + ne : router + 2 * ne] + proj[router + 2 * ne : router + 3 * ne]
        logits = logits / jnp.sqrt(square) / tau
        expo = jnp.exp(logits - jnp.max(logits, axis=0, keepdims=True))
        prob = expo / jnp.sum(expo, axis=0, keepdims=True)
        id_row = jnp.concatenate([ids[r : r + 1] for r in range(row0, row0 + BLOCK_ROWS)], axis=1)
        gate = jnp.sum(jnp.where(iota(prob.shape, 0) == id_row, prob, 0.0), axis=0, keepdims=True)
        for r in range(BLOCK_ROWS):
            gate_ref[row0 + r : row0 + r + 1, :] = gate[:, r * LANES : (r + 1) * LANES]
        slot_iota = iota((slots, LANES), 0)
        hot = [(slot_iota == pos[r : r + 1]).astype(F32).astype(BF16) for r in range(row0, row0 + BLOCK_ROWS)]
        picked = jnp.dot(jnp.concatenate(hot, axis=1), x, preferred_element_type=F32).astype(BF16)
        grans = slots // GRAN
        xs_ref[sub * grans : (sub + 1) * grans] = picked.reshape(grans, GRAN, picked.shape[1])


def load_expert(i, span, eid_ref, start_ref, count_ref, xs_ref, w1_refs, w2_refs, w1_buf, w2_buf, x_buf, w_sem, x_sem):
    pltpu.make_async_copy(w1_refs[i], w1_buf.at[i], w_sem.at[2 * i]).start()
    e = eid_ref[0, i]

    def per_block(b, n):
        size = count_ref[b, e]

        @pl.when(size > 0)
        def _():
            run = xs_ref.at[pl.ds(b * span + start_ref[b, e], size)]
            pltpu.make_async_copy(run, x_buf.at[i, pl.ds(n, size)], x_sem.at[i]).start()

        return n + size

    total = lax.fori_loop(0, start_ref.shape[0], per_block, 0)
    pltpu.make_async_copy(w2_refs[i], w2_buf.at[i], w_sem.at[2 * i + 1]).start()
    return total


def run_expert(i, total, tile, b_ref, w1_refs, w2_refs, xs_ref, w1_buf, w2_buf, x_buf, h_buf, w_sem, x_sem):
    width, hidden = w1_buf.shape[1], w1_buf.shape[2]
    pltpu.make_async_copy(w1_refs[i], w1_buf.at[i], w_sem.at[2 * i]).wait()

    @pl.when(total > 0)
    def _():
        pltpu.make_async_copy(xs_ref.at[pl.ds(0, total)], x_buf.at[i, pl.ds(0, total)], x_sem.at[i]).wait()

    pltpu.make_async_copy(w2_refs[i], w2_buf.at[i], w_sem.at[2 * i + 1]).wait()
    b1 = b_ref[:, 0:hidden].astype(F32)
    b2 = b_ref[:, hidden : hidden + width].astype(F32)

    def per_tile(t, _):
        g0 = t * tile
        x = x_buf[i, pl.ds(g0, tile)].reshape(tile * GRAN, width)
        step = 256
        for c in range(0, hidden, step):
            pre = jnp.dot(x, w1_buf[i, :, c : c + step], preferred_element_type=F32) + b1[:, c : c + step]
            act = 0.5 * pre * (1.0 + lax.erf(pre * F32(0.5**0.5)))
            h_buf[:, c : c + step] = act.astype(BF16)
        y = jnp.dot(h_buf[...], w2_buf[i], preferred_element_type=F32) + b2
        x_buf[i, pl.ds(g0, tile)] = y.astype(BF16).reshape(tile, GRAN, width)
        return 0

    lax.fori_loop(0, (total + tile - 1) // tile, per_tile, 0)


def expert_kernel(count, tile, span, eid_ref, start_ref, count_ref, xs_ref, *refs):
    w1_refs, w2_refs, b_refs = refs[:count], refs[count : 2 * count], refs[2 * count : 3 * count]
    out_ref = refs[3 * count]
    w1_buf, w2_buf, x_buf, h_buf, w_sem, x_sem, y_sem = refs[3 * count + 1 :]

    def load(i):
        return load_expert(i, span, eid_ref, start_ref, count_ref, xs_ref, w1_refs, w2_refs, w1_buf, w2_buf, x_buf, w_sem, x_sem)

    totals = [load(0)]
    for i in range(count):
        if i + 1 < count:
            totals.append(load(i + 1))
        run_expert(i, totals[i], tile, b_refs[i], w1_refs, w2_refs, xs_ref, w1_buf, w2_buf, x_buf, h_buf, w_sem, x_sem)
        e = eid_ref[0, i]

        def per_block(b, n):
            size = count_ref[b, e]

            @pl.when(size > 0)
            def _():
                run = out_ref.at[pl.ds(b * span + start_ref[b, e], size)]
                pltpu.make_async_copy(x_buf.at[i, pl.ds(n, size)], run, y_sem.at[i]).start()

            return n + size

        lax.fori_loop(0, start_ref.shape[0], per_block, 0)
    for i in range(count):

        @pl.when(totals[i] > 0)
        def _():
            pltpu.make_async_copy(x_buf.at[i, pl.ds(0, totals[i])], out_ref.at[pl.ds(0, totals[i])], y_sem.at[i]).wait()


def final_kernel(count, tile, span, window, eid_ref, start_ref, count_ref, pos_ref, gate_ref, ids_ref, xs_ref, part_ref, *refs):
    w1_refs, w2_refs, b_refs = refs[:count], refs[count : 2 * count], refs[2 * count : 3 * count]
    out_ref = refs[3 * count]
    w1_buf, w2_buf, x_buf, h_buf, w_sem, x_sem, o_buf, p_sem, o_sem = refs[3 * count + 1 :]
    blocks = start_ref.shape[0]
    width = w1_buf.shape[1]
    block_tok = BLOCK_ROWS * LANES

    def load(i):
        return load_expert(i, span, eid_ref, start_ref, count_ref, xs_ref, w1_refs, w2_refs, w1_buf, w2_buf, x_buf, w_sem, x_sem)

    totals = [load(i) for i in range(count)]
    part_in = pltpu.make_async_copy(part_ref, o_buf, p_sem)
    part_in.start()
    pad = jnp.zeros((tile + window, GRAN, width), BF16)
    for i in range(count):
        x_buf[i, pl.ds(totals[i], tile + window)] = pad
    for i in range(count):
        run_expert(i, totals[i], tile, b_refs[i], w1_refs, w2_refs, xs_ref, w1_buf, w2_buf, x_buf, h_buf, w_sem, x_sem)
    part_in.wait()
    lane = iota((LANES, window * GRAN), 1).astype(F32)

    def out_copy(b):
        rows = pl.ds(pl.multiple_of(b * block_tok, block_tok), block_tok)
        return pltpu.make_async_copy(o_buf.at[rows], out_ref.at[rows], o_sem)

    def per_pair(pair, offsets):
        row0 = pl.multiple_of(pair * 2 * BLOCK_ROWS, 2 * BLOCK_ROWS)
        rows8 = pl.ds(row0, 2 * BLOCK_ROWS)
        pos8, gate8, ids8 = pos_ref[rows8, :], gate_ref[rows8, :], ids_ref[rows8, :]
        gate_cols = jnp.transpose(gate8)
        upper = iota(pos8.shape, 0) < BLOCK_ROWS
        local = []
        for i in range(count):
            e = eid_ref[0, i]
            origin = jnp.where(upper, start_ref[2 * pair, e], start_ref[2 * pair + 1, e]) * GRAN
            mine = (ids8 == e) & (pos8 >= 0)
            local.append(jnp.transpose(jnp.where(mine, pos8 - origin, -1).astype(F32)))

        def window_rows(sub, w, offsets):
            ys = jnp.concatenate(
                [x_buf[i, pl.ds(jnp.minimum(offsets[i] + w * window, totals[i]), window)].reshape(window * GRAN, width) for i in range(count)],
                axis=0,
            )
            shift = jnp.asarray(w * (window * GRAN)).astype(F32)
            hot = []
            for r in range(sub * BLOCK_ROWS, (sub + 1) * BLOCK_ROWS):
                hot.append(jnp.concatenate([(lane == local[i][:, r : r + 1] - shift).astype(F32).astype(BF16) for i in range(count)], axis=1))
            return jnp.dot(jnp.concatenate(hot, axis=0), ys, preferred_element_type=F32)

        def add(sub, back):
            for r in range(BLOCK_ROWS):
                at = pl.ds(pl.multiple_of((2 * pair + sub) * block_tok + r * LANES, LANES), LANES)
                scaled = back[r * LANES : (r + 1) * LANES] * gate_cols[:, sub * BLOCK_ROWS + r : sub * BLOCK_ROWS + r + 1]
                o_buf[at, :] = (o_buf[at, :].astype(F32) + scaled).astype(BF16)

        starts = [offsets]
        for sub in range(2):
            starts.append(tuple(starts[sub][i] + count_ref[2 * pair + sub, eid_ref[0, i]] for i in range(count)))
        for sub in range(2):
            add(sub, window_rows(sub, 0, starts[sub]))
        for sub in range(2):
            longest = starts[sub + 1][0] - starts[sub][0]
            for i in range(1, count):
                longest = jnp.maximum(longest, starts[sub + 1][i] - starts[sub][i])

            def more(w, _):
                add(sub, window_rows(sub, w, starts[sub]))
                return 0

            lax.fori_loop(1, (longest + window - 1) // window, more, 0)
            out_copy(2 * pair + sub).start()
        return starts[2]

    lax.fori_loop(0, blocks // 2, per_pair, (jnp.int32(0),) * count)
    pltpu.make_async_copy(o_buf, out_ref, o_sem).wait()


def combine_kernel(slots, eid_ref, ys_ref, pos_ref, gate_ref, ids_ref, out_ref):
    rows = pos_ref.shape[0]
    pos_cols = jnp.transpose(pos_ref[...].astype(F32))
    later = (ids_ref[...] == eid_ref[0, 0]) | (ids_ref[...] == eid_ref[0, 1])
    gate_cols = jnp.transpose(jnp.where(later, 0.0, gate_ref[...]))
    grans = slots // GRAN
    slot_iota = iota((LANES, slots), 1).astype(F32)
    for sub in range(rows // BLOCK_ROWS):
        row0 = sub * BLOCK_ROWS
        y = ys_ref[sub * grans : (sub + 1) * grans].reshape(slots, ys_ref.shape[2])
        hot = [(slot_iota == pos_cols[:, r : r + 1]).astype(F32).astype(BF16) for r in range(row0, row0 + BLOCK_ROWS)]
        back = jnp.dot(jnp.concatenate(hot, axis=0), y, preferred_element_type=F32)
        for r in range(BLOCK_ROWS):
            at = (row0 + r) * LANES
            scaled = back[r * LANES : (r + 1) * LANES] * gate_cols[:, row0 + r : row0 + r + 1]
            out_ref[at : at + LANES, :] = scaled.astype(BF16)


def vmem():
    return pl.BlockSpec(memory_space=pltpu.VMEM)


def smem():
    return pl.BlockSpec(memory_space=pltpu.SMEM)


def hbm():
    return pl.BlockSpec(memory_space=pl.ANY)


def solution(mesh):
    num_experts = mesh.shape["ep_b"] * mesh.shape["ep_a"]
    tok_spec = P(("dp",) + EXPERT_AXES)
    expert_spec = P(EXPERT_AXES)

    def swap(value, bit):
        return lax.ppermute(value, EXPERT_AXES, [(e, e ^ bit) for e in range(num_experts)])

    def inner_step(tokens, expert_ids, route_order, w_route, expert_keys, value_a11, w_in, b_in, w_out, b_out):
        tok_dev, width = tokens.shape[1], tokens.shape[2]
        hidden = w_in.shape[2]
        router = w_route.shape[1]
        capacity = (5 * tok_dev + 4 * num_experts - 1) // (4 * num_experts)
        rows = tok_dev // LANES
        blocks = rows // BLOCK_ROWS
        slots = -(-(BLOCK_ROWS * LANES + num_experts * (GRAN - 1)) // LANES) * LANES
        span = slots // GRAN
        me = lax.axis_index(EXPERT_AXES)

        first, second = w_in[0], w_out[0]
        x_first, y_second = swap(first, 2), swap(second, 4)
        x_second, y_first = swap(second, 2), swap(first, 4)
        c_first, c_second = swap(first, 1), swap(second, 1)
        own_bias = jnp.concatenate([b_in, b_out], axis=1)
        bias = [own_bias] + [swap(own_bias, bit) for bit in range(1, num_experts)]

        ids, order = expert_ids.reshape(rows, LANES), route_order.reshape(rows, LANES)
        unit = 2 * BLOCK_ROWS
        whole = pl.BlockSpec((rows, LANES), lambda i: (0, 0))
        table = pl.BlockSpec((blocks, LANES), lambda i: (0, 0))
        pos, starts, counts, gate, xs = pl.pallas_call(
            functools.partial(dispatch_kernel, router, num_experts, capacity, slots),
            out_shape=(
                jax.ShapeDtypeStruct((rows, LANES), jnp.int32),
                jax.ShapeDtypeStruct((blocks, LANES), jnp.int32),
                jax.ShapeDtypeStruct((blocks, LANES), jnp.int32),
                jax.ShapeDtypeStruct((rows, LANES), F32),
                jax.ShapeDtypeStruct((blocks * span, GRAN, width), BF16),
            ),
            grid=(rows // unit,),
            in_specs=[
                smem(),
                whole,
                whole,
                pl.BlockSpec((width, router), lambda i: (0, 0)),
                pl.BlockSpec((num_experts, router), lambda i: (0, 0)),
                pl.BlockSpec((unit * LANES, width), lambda i: (i, 0)),
            ],
            out_specs=(
                whole,
                table,
                table,
                pl.BlockSpec((unit, LANES), lambda i: (i, 0)),
                pl.BlockSpec((2 * span, GRAN, width), lambda i: (i, 0, 0)),
            ),
            scratch_shapes=[pltpu.VMEM((router + 4 * num_experts, width), BF16)],
            cost_estimate=pl.CostEstimate(flops=9 * 10**9, bytes_accessed=14 * 10**6, transcendentals=0),
            name="dispatch",
        )(value_a11.reshape(1, 1), ids, order, w_route, expert_keys, tokens[0])

        most = -(-(capacity + blocks * (GRAN - 1)) // (16 * GRAN)) * 16
        tile, window = 16, 8

        def eids(bits):
            return jnp.stack([me ^ bits, me ^ bits ^ 1]).reshape(1, 2).astype(jnp.int32)

        def scratch(n, extra):
            return [
                pltpu.VMEM((n,) + first.shape, BF16),
                pltpu.VMEM((n,) + second.shape, BF16),
                pltpu.VMEM((n, most + extra, GRAN, width), BF16),
                pltpu.VMEM((tile * GRAN, hidden), BF16),
                pltpu.SemaphoreType.DMA((2 * n,)),
                pltpu.SemaphoreType.DMA((n,)),
            ]

        def eids(*bits):
            return jnp.stack([me ^ bit for bit in bits]).reshape(1, len(bits)).astype(jnp.int32)

        def experts(bits, xs, firsts, seconds):
            n = len(bits)
            return pl.pallas_call(
                functools.partial(expert_kernel, n, tile, span),
                out_shape=jax.ShapeDtypeStruct(xs.shape, BF16),
                in_specs=[smem()] * 3 + [hbm()] * (1 + 2 * n) + [vmem()] * n,
                out_specs=hbm(),
                scratch_shapes=scratch(n, 0) + [pltpu.SemaphoreType.DMA((n,))],
                input_output_aliases={3: 0},
                cost_estimate=pl.CostEstimate(flops=3 * n * 10**9, bytes_accessed=4 * n * 10**6, transcendentals=0),
            )(eids(*bits), starts, counts, xs, *firsts, *seconds, *[bias[bit] for bit in bits])

        xs = experts((0, 1), xs, (first, c_first), (second, c_second))
        x_first, y_second, xs = lax.optimization_barrier((x_first, y_second, xs))
        d_first, d_second = swap(x_first, 4), swap(y_second, 2)
        cx_first, cy_second = swap(x_first, 1), swap(y_second, 1)
        cx_second, cy_first = swap(x_second, 1), swap(y_first, 1)
        xs = experts((2, 3, 4, 5), xs, (x_first, cx_first, y_first, cy_first), (x_second, cx_second, y_second, cy_second))
        part = pl.pallas_call(
            functools.partial(combine_kernel, slots),
            out_shape=jax.ShapeDtypeStruct((tok_dev, width), BF16),
            grid=(rows // unit,),
            in_specs=[
                smem(),
                pl.BlockSpec((2 * span, GRAN, width), lambda i: (i, 0, 0)),
                pl.BlockSpec((unit, LANES), lambda i: (i, 0)),
                pl.BlockSpec((unit, LANES), lambda i: (i, 0)),
                pl.BlockSpec((unit, LANES), lambda i: (i, 0)),
            ],
            out_specs=pl.BlockSpec((unit * LANES, width), lambda i: (i, 0)),
            cost_estimate=pl.CostEstimate(flops=5 * 10**9, bytes_accessed=14 * 10**6, transcendentals=0),
            name="combine",
        )(eids(6, 7), xs, pos, gate, ids)
        d_first, d_second, part = lax.optimization_barrier((d_first, d_second, part))
        out = pl.pallas_call(
            functools.partial(final_kernel, 2, tile, span, window),
            out_shape=jax.ShapeDtypeStruct((tok_dev, width), BF16),
            in_specs=[smem()] * 3 + [vmem()] * 3 + [hbm()] * 6 + [vmem()] * 2,
            out_specs=hbm(),
            scratch_shapes=scratch(2, tile + window)
            + [pltpu.VMEM((tok_dev, width), BF16), pltpu.SemaphoreType.DMA, pltpu.SemaphoreType.DMA],
            cost_estimate=pl.CostEstimate(flops=7 * 10**9, bytes_accessed=8 * 10**6, transcendentals=0),
            name="final",
        )(
            eids(6, 7), starts, counts, pos, gate, ids, xs, part,
            d_first, swap(d_first, 1), d_second, swap(d_second, 1), bias[6], bias[7],
        )
        return out[None]

    return jax.shard_map(
        inner_step,
        mesh=mesh,
        in_specs=(tok_spec, tok_spec, tok_spec, P(), P(), P(), expert_spec, expert_spec, expert_spec, expert_spec),
        out_specs=tok_spec,
        check_vma=False,
    )
```

profile of v0, /device:TPU:0, one launch (start us, length us, event | category | flops | bytes accessed | tf_op | source)
XLA Modules:
  0.0 136.4 jit_solution(2301736904717823282)
XLA Ops:
  0.0 0.8 collective-permute-start.2
  0.8 2.5 %collective-permute-start = (bf16[384,1536]{1,0:T(8,128)(2,1)}, bf16[384,1536]{1,0:T(8,128)(2,1)S(1)}, u32[]{:S(2)}, u32[]{:S(2)}) collective-permute-start(bf16[384,1536]{1,0:T(8,128)(2,1)} %bitcast.24), channel_id=1, source_target_pairs={{0,2},{1,3},{2,0},{3,1},{4,6},{5,7},{6,4},{7,5}} | collective-permute-start | bytes 3538952 | tf_op jit(solution)/shard_map/ppermute | solution.py:323
  3.3 1.5 %collective-permute-start.1 = (bf16[1536,384]{1,0:T(8,128)(2,1)}, bf16[1536,384]{1,0:T(8,128)(2,1)S(1)}, u32[]{:S(2)}, u32[]{:S(2)}) collective-permute-start(bf16[1536,384]{1,0:T(8,128)(2,1)} %bitcast.27), channel_id=1, source_target_pairs={{0,4},{1,5},{2,6},{3,7},{4,0},{5,1},{6,2},{7,3}} | collective-permute-start | bytes 3538952 | tf_op jit(solution)/shard_map/ppermute | solution.py:323
  4.8 0.7 constant_dynamic-update-slice_fusion.1
  5.5 0.7 constant_dynamic-update-slice_fusion.refs_4_
  8.6 1.1 collective-permute-start.8
  9.7 17.9 %dispatch.1 = (s32[64,128]{1,0:T(8,128)}, s32[16,128]{1,0:T(8,128)}, s32[16,128]{1,0:T(8,128)}, f32[64,128]{1,0:T(8,128)}, bf16[640,16,384]{2,1,0:T(8,128)(2,1)}) custom-call(f32[1,1]{1,0:T(1,128)} %bitcast.21.tau_ref, s32[64,128]{1,0:T(8,128)} %bitcast.32, s32[64,128]{1,0:T(8,128)} %bitcast.31, bf16[384,256]{1,0:T(8,128)(2,1)} %wr_ref.1, ...), custom_call_target="tpu_custom_call" | custom-call | flops 8999999488 | bytes 14000000 | tf_op jit(solution)/shard_map/dispatch/pallas_call | solution.py:347
  27.6 14.3 %shard_map.100.xs_ref = bf16[640,16,384]{2,1,0:T(8,128)(2,1)} custom-call(s32[1,2]{1,0:T(1,128)} %add_bitcast_fusion.2.eid_ref, s32[16,128]{1,0:T(8,128)} %get-tuple-element.16.start_ref, s32[16,128]{1,0:T(8,128)} %get-tuple-element.17.count_ref, bf16[640,16,384]{2,1,0:T(8,128)(2,1)} %get-tuple-element.20.xs_ref, ...), custom_call_target="tpu_custom_call", output_to_operand_aliasing={{}: (3, {})} | custom-call | flops 6000000000 | bytes 8000000 | tf_op jit(solution)/shard_map/pallas_call | solution.py:398
  42.0 14.9 %collective-permute-done.6.refs_2_ = bf16[384,1536]{1,0:T(8,128)(2,1)S(1)} collective-permute-done((bf16[384,1536]{1,0:T(8,128)(2,1)}, bf16[384,1536]{1,0:T(8,128)(2,1)S(1)}, u32[]{:S(2)}, u32[]{:S(2)}) %collective-permute-start.6) | collective-permute-done | bytes 1179680 | tf_op jit(solution)/shard_map/ppermute | solution.py:323
  57.8 3.3 %collective-permute-done.11.refs_8_ = bf16[1,1920]{1,0:T(2,128)(2,1)S(1)} collective-permute-done((bf16[1,1920]{1,0:T(2,128)(2,1)S(1)}, bf16[1,1920]{1,0:T(2,128)(2,1)S(1)}, u32[]{:S(2)}, u32[]{:S(2)}) %collective-permute-start.11) | collective-permute-done | bytes 3872 | tf_op jit(solution)/shard_map/ppermute | solution.py:323
  61.1 3.2 %collective-permute-done.12.refs_9_ = bf16[1,1920]{1,0:T(2,128)(2,1)} collective-permute-done((bf16[1,1920]{1,0:T(2,128)(2,1)S(1)}, bf16[1,1920]{1,0:T(2,128)(2,1)}, u32[]{:S(2)}, u32[]{:S(2)}) %collective-permute-start.12) | collective-permute-done | bytes 3872 | tf_op jit(solution)/shard_map/ppermute | solution.py:323
  64.3 1.5 %collective-permute-start.13 = (bf16[1,1920]{1,0:T(2,128)(2,1)S(1)}, bf16[1,1920]{1,0:T(2,128)(2,1)}, u32[]{:S(2)}, u32[]{:S(2)}) collective-permute-start(bf16[1,1920]{1,0:T(2,128)(2,1)S(1)} %copy-done.1), channel_id=1, source_target_pairs={{0,4},{1,5},{2,6},{3,7},{4,0},{5,1},{6,2},{7,3}} | collective-permute-start | bytes 11528 | tf_op jit(solution)/shard_map/ppermute | solution.py:323
  65.8 0.7 add_bitcast_fusion.eid_ref
  66.5 1.6 %collective-permute-done.13.refs_10_ = bf16[1,1920]{1,0:T(2,128)(2,1)} collective-permute-done((bf16[1,1920]{1,0:T(2,128)(2,1)S(1)}, bf16[1,1920]{1,0:T(2,128)(2,1)}, u32[]{:S(2)}, u32[]{:S(2)}) %collective-permute-start.13) | collective-permute-done | bytes 3872 | tf_op jit(solution)/shard_map/ppermute | solution.py:323
  68.0 0.6 add_bitcast_fusion.1.eid_ref
  68.7 2.4 %collective-permute-done.14.refs_11_ = bf16[1,1920]{1,0:T(2,128)(2,1)S(1)} collective-permute-done((bf16[1,1920]{1,0:T(2,128)(2,1)S(1)}, bf16[1,1920]{1,0:T(2,128)(2,1)S(1)}, u32[]{:S(2)}, u32[]{:S(2)}) %collective-permute-start.14) | collective-permute-done | bytes 3872 | tf_op jit(solution)/shard_map/ppermute | solution.py:323
  71.1 1.5 %collective-permute-start.15 = (bf16[384,1536]{1,0:T(8,128)(2,1)S(1)}, bf16[384,1536]{1,0:T(8,128)(2,1)}, u32[]{:S(2)}, u32[]{:S(2)}) collective-permute-start(bf16[384,1536]{1,0:T(8,128)(2,1)S(1)} %collective-permute-done.refs_0_), channel_id=1, source_target_pairs={{0,4},{1,5},{2,6},{3,7},{4,0},{5,1},{6,2},{7,3}} | collective-permute-start | bytes 3538952 | tf_op jit(solution)/shard_map/ppermute | solution.py:323
  73.3 23.5 %shard_map.101.ys_ref.xs_ref = bf16[640,16,384]{2,1,0:T(8,128)(2,1)} custom-call(s32[1,4]{1,0:T(1,128)} %add_bitcast_fusion.1.eid_ref, s32[16,128]{1,0:T(8,128)} %get-tuple-element.16.start_ref, s32[16,128]{1,0:T(8,128)} %get-tuple-element.17.count_ref, bf16[640,16,384]{2,1,0:T(8,128)(2,1)} %shard_map.100.xs_ref, ...), custom_call_target="tpu_custom_call", output_to_operand_aliasing={{}: (3, {})} | custom-call | flops 12000000000 | bytes 16000000 | tf_op jit(solution)/shard_map/pallas_call | solution.py:398
  96.8 12.4 %combine.1.part_ref = bf16[8192,384]{1,0:T(8,128)(2,1)} custom-call(s32[1,2]{1,0:T(1,128)} %add_bitcast_fusion.eid_ref, bf16[640,16,384]{2,1,0:T(8,128)(2,1)} %shard_map.101.ys_ref.xs_ref, s32[64,128]{1,0:T(8,128)} %get-tuple-element.18.pos_ref, f32[64,128]{1,0:T(8,128)} %get-tuple-element.19.gate_ref, s32[64,128]{1,0:T(8,128)} %bitcast.33), custom_call_target="tpu_custom_call" | custom-call | flops 5000000000 | bytes 14000000 | tf_op jit(solution)/shard_map/combine/pallas_call | solution.py:414
  109.7 2.2 %collective-permute-start.19 = (bf16[1,1920]{1,0:T(2,128)(2,1)S(1)}, bf16[1,1920]{1,0:T(2,128)(2,1)S(1)}, u32[]{:S(2)}, u32[]{:S(2)}) collective-permute-start(bf16[1,1920]{1,0:T(2,128)(2,1)S(1)} %copy-done.1), channel_id=1, source_target_pairs={{0,6},{1,7},{2,4},{3,5},{4,2},{5,3},{6,0},{7,1}} | collective-permute-start | bytes 11528 | tf_op jit(solution)/shard_map/ppermute | solution.py:323
  111.9 2.3 %collective-permute-done.19.refs_4_ = bf16[1,1920]{1,0:T(2,128)(2,1)S(1)} collective-permute-done((bf16[1,1920]{1,0:T(2,128)(2,1)S(1)}, bf16[1,1920]{1,0:T(2,128)(2,1)S(1)}, u32[]{:S(2)}, u32[]{:S(2)}) %collective-permute-start.19) | collective-permute-done | bytes 3872 | tf_op jit(solution)/shard_map/ppermute | solution.py:323
  114.2 1.6 %collective-permute-done.20.refs_5_ = bf16[1,1920]{1,0:T(2,128)(2,1)S(1)} collective-permute-done((bf16[1,1920]{1,0:T(2,128)(2,1)S(1)}, bf16[1,1920]{1,0:T(2,128)(2,1)S(1)}, u32[]{:S(2)}, u32[]{:S(2)}) %collective-permute-start.20) | collective-permute-done | bytes 3872 | tf_op jit(solution)/shard_map/ppermute | solution.py:323
  116.8 1.0 copy-done.6
  117.8 18.6 %final.1 = bf16[8192,384]{1,0:T(8,128)(2,1)} custom-call(s32[1,2]{1,0:T(1,128)} %add_bitcast_fusion.eid_ref, s32[16,128]{1,0:T(8,128)} %get-tuple-element.16.start_ref, s32[16,128]{1,0:T(8,128)} %get-tuple-element.17.count_ref, s32[64,128]{1,0:T(8,128)} %get-tuple-element.18.pos_ref, f32[64,128]{1,0:T(8,128)} %get-tuple-element.19.gate_ref, ...), custom_call_target="tpu_custom_call" | custom-call | flops 7000000000 | bytes 8000000 | tf_op jit(solution)/shard_map/final/pallas_call | solution.py:430
  (52 shorter events, 4.9 us)
Async XLA Ops:
  0.0 8.6 %collective-permute-start.2 = (bf16[384,1536]{1,0:T(8,128)(2,1)}, bf16[384,1536]{1,0:T(8,128)(2,1)}, u32[]{:S(2)}, u32[]{:S(2)}) collective-permute-start(bf16[384,1536]{1,0:T(8,128)(2,1)} %bitcast.23), channel_id=1, source_target_pairs={{0,1},{1,0},{2,3},{3,2},{4,5},{5,4},{6,7},{7,6}} | collective-permute-start | bytes 3538952 | tf_op jit(solution)/shard_map/ppermute | solution.py:323
  0.8 41.1 %collective-permute-start = (bf16[384,1536]{1,0:T(8,128)(2,1)}, bf16[384,1536]{1,0:T(8,128)(2,1)S(1)}, u32[]{:S(2)}, u32[]{:S(2)}) collective-permute-start(bf16[384,1536]{1,0:T(8,128)(2,1)} %bitcast.24), channel_id=1, source_target_pairs={{0,2},{1,3},{2,0},{3,1},{4,6},{5,7},{6,4},{7,5}} | collective-permute-start | bytes 3538952 | tf_op jit(solution)/shard_map/ppermute | solution.py:323
  3.3 38.6 %collective-permute-start.1 = (bf16[1536,384]{1,0:T(8,128)(2,1)}, bf16[1536,384]{1,0:T(8,128)(2,1)S(1)}, u32[]{:S(2)}, u32[]{:S(2)}) collective-permute-start(bf16[1536,384]{1,0:T(8,128)(2,1)} %bitcast.27), channel_id=1, source_target_pairs={{0,4},{1,5},{2,6},{3,7},{4,0},{5,1},{6,2},{7,3}} | collective-permute-start | bytes 3538952 | tf_op jit(solution)/shard_map/ppermute | solution.py:323
  4.8 22.8 %collective-permute-start.3 = (bf16[1536,384]{1,0:T(8,128)(2,1)}, bf16[1536,384]{1,0:T(8,128)(2,1)}, u32[]{:S(2)}, u32[]{:S(2)}) collective-permute-start(bf16[1536,384]{1,0:T(8,128)(2,1)} %bitcast.28), channel_id=1, source_target_pairs={{0,1},{1,0},{2,3},{3,2},{4,5},{5,4},{6,7},{7,6}} | collective-permute-start | bytes 3538952 | tf_op jit(solution)/shard_map/ppermute | solution.py:323
  6.2 1.8 %collective-permute-start.4 = (bf16[1,1920]{1,0:T(2,128)(2,1)S(1)}, bf16[1,1920]{1,0:T(2,128)(2,1)S(1)}, u32[]{:S(2)}, u32[]{:S(2)}) collective-permute-start(bf16[1,1920]{1,0:T(2,128)(2,1)S(1)} %constant_dynamic-update-slice_fusion.refs_4_), channel_id=1, source_target_pairs={{0,1},{1,0},{2,3},{3,2},{4,5},{5,4},{6,7},{7,6}} | collective-permute-start | bytes 11528 | tf_op jit(solution)/shard_map/ppermute | solution.py:323
  8.0 48.9 %collective-permute-start.6 = (bf16[384,1536]{1,0:T(8,128)(2,1)}, bf16[384,1536]{1,0:T(8,128)(2,1)S(1)}, u32[]{:S(2)}, u32[]{:S(2)}) collective-permute-start(bf16[384,1536]{1,0:T(8,128)(2,1)} %bitcast.25), channel_id=1, source_target_pairs={{0,4},{1,5},{2,6},{3,7},{4,0},{5,1},{6,2},{7,3}} | collective-permute-start | bytes 3538952 | tf_op jit(solution)/shard_map/ppermute | solution.py:323
  8.6 48.3 %collective-permute-start.8 = (bf16[1536,384]{1,0:T(8,128)(2,1)}, bf16[1536,384]{1,0:T(8,128)(2,1)}, u32[]{:S(2)}, u32[]{:S(2)}) collective-permute-start(bf16[1536,384]{1,0:T(8,128)(2,1)} %bitcast.29), channel_id=1, source_target_pairs={{0,2},{1,3},{2,0},{3,1},{4,6},{5,7},{6,4},{7,5}} | collective-permute-start | bytes 3538952 | tf_op jit(solution)/shard_map/ppermute | solution.py:323
  27.6 29.8 %copy-start.1 = (bf16[1,1920]{1,0:T(2,128)(2,1)S(1)}, bf16[1,1920]{1,0:T(2,128)(2,1)}, u32[]{:S(2)}) copy-start(bf16[1,1920]{1,0:T(2,128)(2,1)} %copy-done) | copy-start | bytes 11524
  41.9 31.3 %copy-start.2 = (bf16[384,1536]{1,0:T(8,128)(2,1)}, bf16[384,1536]{1,0:T(8,128)(2,1)S(1)}, u32[]{:S(2)}) copy-start(bf16[384,1536]{1,0:T(8,128)(2,1)S(1)} %collective-permute-done.refs_0_) | copy-start | bytes 3538948
  42.0 31.3 %copy-start.3 = (bf16[1536,384]{1,0:T(8,128)(2,1)}, bf16[1536,384]{1,0:T(8,128)(2,1)S(1)}, u32[]{:S(2)}) copy-start(bf16[1536,384]{1,0:T(8,128)(2,1)S(1)} %collective-permute-done.1.refs_6_) | copy-start | bytes 3538948
  42.0 30.7 %collective-permute-start.5 = (bf16[384,1536]{1,0:T(8,128)(2,1)S(1)}, bf16[384,1536]{1,0:T(8,128)(2,1)}, u32[]{:S(2)}, u32[]{:S(2)}) collective-permute-start(bf16[384,1536]{1,0:T(8,128)(2,1)S(1)} %collective-permute-done.refs_0_), channel_id=1, source_target_pairs={{0,1},{1,0},{2,3},{3,2},{4,5},{5,4},{6,7},{7,6}} | collective-permute-start | bytes 3538952 | tf_op jit(solution)/shard_map/ppermute | solution.py:323
  56.9 16.3 %collective-permute-start.7 = (bf16[384,1536]{1,0:T(8,128)(2,1)S(1)}, bf16[384,1536]{1,0:T(8,128)(2,1)}, u32[]{:S(2)}, u32[]{:S(2)}) collective-permute-start(bf16[384,1536]{1,0:T(8,128)(2,1)S(1)} %collective-permute-done.6.refs_2_), channel_id=1, source_target_pairs={{0,1},{1,0},{2,3},{3,2},{4,5},{5,4},{6,7},{7,6}} | collective-permute-start | bytes 3538952 | tf_op jit(solution)/shard_map/ppermute | solution.py:323
  56.9 16.3 %collective-permute-start.9 = (bf16[1536,384]{1,0:T(8,128)(2,1)}, bf16[1536,384]{1,0:T(8,128)(2,1)}, u32[]{:S(2)}, u32[]{:S(2)}) collective-permute-start(bf16[1536,384]{1,0:T(8,128)(2,1)} %collective-permute-done.8.refs_4_), channel_id=1, source_target_pairs={{0,1},{1,0},{2,3},{3,2},{4,5},{5,4},{6,7},{7,6}} | collective-permute-start | bytes 3538952 | tf_op jit(solution)/shard_map/ppermute | solution.py:323
  57.4 15.8 %collective-permute-start.10 = (bf16[1536,384]{1,0:T(8,128)(2,1)S(1)}, bf16[1536,384]{1,0:T(8,128)(2,1)}, u32[]{:S(2)}, u32[]{:S(2)}) collective-permute-start(bf16[1536,384]{1,0:T(8,128)(2,1)S(1)} %collective-permute-done.1.refs_6_), channel_id=1, source_target_pairs={{0,1},{1,0},{2,3},{3,2},{4,5},{5,4},{6,7},{7,6}} | collective-permute-start | bytes 3538952 | tf_op jit(solution)/shard_map/ppermute | solution.py:323
  57.4 3.6 %collective-permute-start.11 = (bf16[1,1920]{1,0:T(2,128)(2,1)S(1)}, bf16[1,1920]{1,0:T(2,128)(2,1)S(1)}, u32[]{:S(2)}, u32[]{:S(2)}) collective-permute-start(bf16[1,1920]{1,0:T(2,128)(2,1)S(1)} %copy-done.1), channel_id=1, source_target_pairs={{0,2},{1,3},{2,0},{3,1},{4,6},{5,7},{6,4},{7,5}} | collective-permute-start | bytes 11528 | tf_op jit(solution)/shard_map/ppermute | solution.py:323
  61.1 3.2 %collective-permute-start.12 = (bf16[1,1920]{1,0:T(2,128)(2,1)S(1)}, bf16[1,1920]{1,0:T(2,128)(2,1)}, u32[]{:S(2)}, u32[]{:S(2)}) collective-permute-start(bf16[1,1920]{1,0:T(2,128)(2,1)S(1)} %copy-done.1), channel_id=1, source_target_pairs={{0,3},{1,2},{2,1},{3,0},{4,7},{5,6},{6,5},{7,4}} | collective-permute-start | bytes 11528 | tf_op jit(solution)/shard_map/ppermute | solution.py:323
  64.3 3.8 %collective-permute-start.13 = (bf16[1,1920]{1,0:T(2,128)(2,1)S(1)}, bf16[1,1920]{1,0:T(2,128)(2,1)}, u32[]{:S(2)}, u32[]{:S(2)}) collective-permute-start(bf16[1,1920]{1,0:T(2,128)(2,1)S(1)} %copy-done.1), channel_id=1, source_target_pairs={{0,4},{1,5},{2,6},{3,7},{4,0},{5,1},{6,2},{7,3}} | collective-permute-start | bytes 11528 | tf_op jit(solution)/shard_map/ppermute | solution.py:323
  68.0 3.1 %collective-permute-start.14 = (bf16[1,1920]{1,0:T(2,128)(2,1)S(1)}, bf16[1,1920]{1,0:T(2,128)(2,1)S(1)}, u32[]{:S(2)}, u32[]{:S(2)}) collective-permute-start(bf16[1,1920]{1,0:T(2,128)(2,1)S(1)} %copy-done.1), channel_id=1, source_target_pairs={{0,5},{1,4},{2,7},{3,6},{4,1},{5,0},{6,3},{7,2}} | collective-permute-start | bytes 11528 | tf_op jit(solution)/shard_map/ppermute | solution.py:323
  71.1 38.0 %collective-permute-start.15 = (bf16[384,1536]{1,0:T(8,128)(2,1)S(1)}, bf16[384,1536]{1,0:T(8,128)(2,1)}, u32[]{:S(2)}, u32[]{:S(2)}) collective-permute-start(bf16[384,1536]{1,0:T(8,128)(2,1)S(1)} %collective-permute-done.refs_0_), channel_id=1, source_target_pairs={{0,4},{1,5},{2,6},{3,7},{4,0},{5,1},{6,2},{7,3}} | collective-permute-start | bytes 3538952 | tf_op jit(solution)/shard_map/ppermute | solution.py:323
  72.6 36.5 %collective-permute-start.16 = (bf16[1536,384]{1,0:T(8,128)(2,1)S(1)}, bf16[1536,384]{1,0:T(8,128)(2,1)}, u32[]{:S(2)}, u32[]{:S(2)}) collective-permute-start(bf16[1536,384]{1,0:T(8,128)(2,1)S(1)} %collective-permute-done.1.refs_6_), channel_id=1, source_target_pairs={{0,2},{1,3},{2,0},{3,1},{4,6},{5,7},{6,4},{7,5}} | collective-permute-start | bytes 3538952 | tf_op jit(solution)/shard_map/ppermute | solution.py:323
  109.1 6.7 %collective-permute-start.17 = (bf16[384,1536]{1,0:T(8,128)(2,1)}, bf16[384,1536]{1,0:T(8,128)(2,1)S(1)}, u32[]{:S(2)}, u32[]{:S(2)}) collective-permute-start(bf16[384,1536]{1,0:T(8,128)(2,1)} %collective-permute-done.15.refs_0_), channel_id=1, source_target_pairs={{0,1},{1,0},{2,3},{3,2},{4,5},{5,4},{6,7},{7,6}} | collective-permute-start | bytes 3538952 | tf_op jit(solution)/shard_map/ppermute | solution.py:323
  109.2 6.6 %collective-permute-start.18 = (bf16[1536,384]{1,0:T(8,128)(2,1)}, bf16[1536,384]{1,0:T(8,128)(2,1)S(1)}, u32[]{:S(2)}, u32[]{:S(2)}) collective-permute-start(bf16[1536,384]{1,0:T(8,128)(2,1)} %collective-permute-done.16.refs_2_), channel_id=1, source_target_pairs={{0,1},{1,0},{2,3},{3,2},{4,5},{5,4},{6,7},{7,6}} | collective-permute-start | bytes 3538952 | tf_op jit(solution)/shard_map/ppermute | solution.py:323
  109.7 4.5 %collective-permute-start.19 = (bf16[1,1920]{1,0:T(2,128)(2,1)S(1)}, bf16[1,1920]{1,0:T(2,128)(2,1)S(1)}, u32[]{:S(2)}, u32[]{:S(2)}) collective-permute-start(bf16[1,1920]{1,0:T(2,128)(2,1)S(1)} %copy-done.1), channel_id=1, source_target_pairs={{0,6},{1,7},{2,4},{3,5},{4,2},{5,3},{6,0},{7,1}} | collective-permute-start | bytes 11528 | tf_op jit(solution)/shard_map/ppermute | solution.py:323
  111.8 4.0 %collective-permute-start.20 = (bf16[1,1920]{1,0:T(2,128)(2,1)S(1)}, bf16[1,1920]{1,0:T(2,128)(2,1)S(1)}, u32[]{:S(2)}, u32[]{:S(2)}) collective-permute-start(bf16[1,1920]{1,0:T(2,128)(2,1)S(1)} %copy-done.1), channel_id=1, source_target_pairs={{0,7},{1,6},{2,5},{3,4},{4,3},{5,2},{6,1},{7,0}} | collective-permute-start | bytes 11528 | tf_op jit(solution)/shard_map/ppermute | solution.py:323
  (9 other events, 75.8 us)
where the time goes:
time: 139 us; the launch traced here: 136 us
  Pallas kernels  86.6 us (62%)
  waiting for transfers between devices  29.2 us (21%)
  starting transfers between devices  14.3 us (10%)
  local copies, waits for them, and re-layouts  3.45 us (2%)
  other arithmetic  1.94 us (1%)
    pallas_call x2, Pallas kernels, experts(): pl.pallas_call(functools.partial(expert_kernel, n, tile, span), out_shape...  37.8 us
    ppermute x21, waiting for transfers between devices, swap(): lax.ppermute(value, EXPERT_AXES, [(e, e ^ bit) for e in range(num_experts)])  29.2 us
    pallas_call x1, Pallas kernels, inner_step(): pl.pallas_call(functools.partial(final_kernel, 2, tile, span, window), ou...  18.6 us
    pallas_call x1, Pallas kernels, inner_step(): pl.pallas_call(functools.partial(dispatch_kernel, router, num_experts, ca...  17.9 us
    ppermute x21, starting transfers between devices, swap(): lax.ppermute(value, EXPERT_AXES, [(e, e ^ bit) for e in range(num_experts)])  14.3 us
    pallas_call x1, Pallas kernels, inner_step(): pl.pallas_call(functools.partial(combine_kernel, slots), out_shape=jax.Sh...  12.4 us
  transfers between devices with their start and end apart: 21, of which 7 were waited for; matrix products, arithmetic and copies ran while one was open for 2% of the time, Pallas kernels for 50%

commit v1 on v0

v1 whole, which is shorter than its diff:
```python
import functools

import jax
import jax.numpy as jnp
from jax import lax
from jax.experimental import pallas as pl
from jax.experimental.pallas import tpu as pltpu
from jax.sharding import PartitionSpec as P


EXPERT_AXES = ("ep_b", "ep_a")

LANES = 128
BLOCK_ROWS = 4
GRAN = 16
BF16 = jnp.bfloat16
F32 = jnp.float32
NT = (((1,), (1,)), ((), ()))


def iota(shape, dim):
    return lax.broadcasted_iota(jnp.int32, shape, dim)


def plan_step(num_experts, capacity, span, ids_ref, ord_ref, wr_ref, keys_ref, pos_ref, start_ref, count_ref, offset_ref, list_ref, wt_ref):
    rows = ids_ref.shape[0]
    blocks = rows // BLOCK_ROWS
    place = jnp.zeros((2 * rows, LANES), F32)
    hi_iota = iota((rows, LANES), 0)
    lo_iota = iota((LANES, LANES), 0)
    lane_val = iota((rows, LANES), 1).astype(F32)
    for chunk in range(rows // 8):
        left, right = [], []
        for r in range(8 * chunk, 8 * chunk + 8):
            order_row = ord_ref[r : r + 1, :]
            hit = hi_iota == (order_row >> 7)
            upper = jnp.where(hit, F32(r), 0.0).astype(BF16)
            lower = jnp.where(hit, lane_val, 0.0).astype(BF16)
            left.append(jnp.concatenate([upper, lower], axis=0))
            right.append(jnp.where(lo_iota == (order_row & 127), 1.0, 0.0).astype(BF16))
        place += lax.dot_general(jnp.concatenate(left, axis=1), jnp.concatenate(right, axis=1), NT, preferred_element_type=F32)
    place = (place[:rows] * LANES + place[rows:]).astype(jnp.int32)
    ids = ids_ref[...]
    mask = (ids[None] == iota((num_experts, rows, LANES), 0)).astype(F32)

    def narrow(step, bound):
        trial = bound + (2 * rows * LANES >> (step + 1))
        admitted = jnp.where(place[None] < trial, mask, 0.0)
        total = jnp.sum(jnp.sum(admitted, axis=1, keepdims=True), axis=2, keepdims=True)
        return jnp.where(total <= capacity, trial, bound)

    steps = (rows * LANES).bit_length()
    bound = lax.fori_loop(0, steps, narrow, jnp.zeros((num_experts, 1, 1), jnp.int32))
    kept = jnp.where(place[None] < bound, mask, 0.0)
    kept2 = kept.reshape(num_experts * rows, LANES).astype(BF16)
    before = (iota((LANES, LANES), 0) < iota((LANES, LANES), 1)).astype(BF16)
    lane_prefix = jnp.dot(kept2, before, preferred_element_type=F32)
    row_total = jnp.dot(kept2, jnp.ones((LANES, LANES), BF16), preferred_element_type=F32).astype(BF16)
    row_a, row_b = iota((rows, rows), 0), iota((rows, rows), 1)
    same = row_a // BLOCK_ROWS == row_b // BLOCK_ROWS
    earlier = (same & (row_b < row_a)).astype(BF16)
    same = same.astype(BF16)
    pick = (iota((blocks, rows), 1) == iota((blocks, rows), 0) * BLOCK_ROWS).astype(BF16)
    lane = iota((blocks, LANES), 1)
    slot = jnp.full((rows, LANES), -1, jnp.int32)
    first = jnp.zeros((rows, LANES), jnp.int32)
    starts = jnp.zeros((blocks, LANES), F32)
    counts = jnp.zeros((blocks, LANES), F32)
    offsets = jnp.zeros((blocks, LANES), F32)
    block_iota = iota((blocks, LANES), 0)
    past = (iota((blocks, blocks), 1) < iota((blocks, blocks), 0)).astype(BF16)
    for e in range(num_experts):
        part = slice(e * rows, (e + 1) * rows)
        row_prefix = jnp.dot(earlier, row_total[part], preferred_element_type=F32)
        in_block = jnp.dot(same, row_total[part], preferred_element_type=F32).astype(jnp.int32)
        grans = (in_block + (GRAN - 1)) >> 4
        here = first * GRAN + (row_prefix + lane_prefix[part]).astype(jnp.int32)
        slot = jnp.where(kept[e] > 0.0, here, slot)
        first_b = jnp.dot(pick, first.astype(F32).astype(BF16), preferred_element_type=F32)
        count_b = jnp.dot(pick, grans.astype(F32).astype(BF16), preferred_element_type=F32)
        offset_b = jnp.dot(past, count_b.astype(BF16), preferred_element_type=F32)
        starts += jnp.where(lane == e, first_b, 0.0)
        counts += jnp.where(lane == e, count_b, 0.0)
        offsets += jnp.where(lane == e, offset_b, 0.0)
        index = (lane - offset_b.astype(jnp.int32) + first_b.astype(jnp.int32) + block_iota * span).astype(F32)
        inside = (lane.astype(F32) >= offset_b) & (lane.astype(F32) < offset_b + count_b)
        index = jnp.sum(jnp.where(inside, index - blocks * span, 0.0), axis=0, keepdims=True)
        list_ref[e : e + 1, :] = index.astype(jnp.int32) + blocks * span
        first = first + grans
    pos_ref[...] = slot
    start_ref[...] = starts.astype(jnp.int32)
    offset_ref[...] = offsets.astype(jnp.int32)
    count_ref[...] = counts.astype(jnp.int32)
    wr = wr_ref[...]
    router = wr.shape[1]
    eye = (iota((router, router), 0) == iota((router, router), 1)).astype(BF16)
    keys = keys_ref[...].astype(F32)
    unit = keys / jnp.sqrt(jnp.sum(keys * keys, axis=1, keepdims=True))
    folded = lax.dot_general(unit, wr.astype(F32), NT, preferred_element_type=F32, precision=lax.Precision.HIGHEST)
    part_a = folded.astype(BF16)
    rest = folded - part_a.astype(F32)
    part_b = rest.astype(BF16)
    part_c = (rest - part_b.astype(F32)).astype(BF16)
    wt_ref[0:router, :] = lax.dot_general(eye, wr, NT, preferred_element_type=F32).astype(BF16)
    tail = jnp.concatenate([part_a.astype(F32), part_b.astype(F32), part_c.astype(F32), jnp.zeros_like(folded)], axis=0)
    wt_ref[router:, :] = tail.astype(BF16)


def dispatch_kernel(
    router, num_experts, capacity, slots, tau_ref, ids_ref, ord_ref, wr_ref, keys_ref, x_ref,
    pos_ref, start_ref, count_ref, offset_ref, list_ref, gate_ref, xs_ref, wt_ref,
):
    grans = slots // GRAN
    spare = start_ref.shape[0] * grans

    @pl.when(pl.program_id(0) == 0)
    def _():
        plan_step(
            num_experts, capacity, grans, ids_ref, ord_ref, wr_ref, keys_ref,
            pos_ref, start_ref, count_ref, offset_ref, list_ref, wt_ref,
        )
        xs_ref[spare : spare + 2] = jnp.zeros((2,) + xs_ref.shape[1:], BF16)

    rows = x_ref.shape[0] // LANES
    part = pl.ds(pl.multiple_of(pl.program_id(0) * rows, rows), rows)
    ids, pos = ids_ref[part, :], pos_ref[part, :]
    tau = tau_ref[0, 0]
    for sub in range(rows // BLOCK_ROWS):
        row0 = sub * BLOCK_ROWS
        x = x_ref[row0 * LANES : (row0 + BLOCK_ROWS) * LANES, :]
        proj = lax.dot_general(wt_ref[...], x, NT, preferred_element_type=F32)
        square = jnp.sum(proj[:router] * proj[:router], axis=0, keepdims=True)
        ne = num_experts
        logits = proj[router : router + ne] + proj[router + ne : router + 2 * ne] + proj[router + 2 * ne : router + 3 * ne]
        logits = logits / jnp.sqrt(square) / tau
        expo = jnp.exp(logits - jnp.max(logits, axis=0, keepdims=True))
        prob = expo / jnp.sum(expo, axis=0, keepdims=True)
        id_row = jnp.concatenate([ids[r : r + 1] for r in range(row0, row0 + BLOCK_ROWS)], axis=1)
        gate = jnp.sum(jnp.where(iota(prob.shape, 0) == id_row, prob, 0.0), axis=0, keepdims=True)
        for r in range(BLOCK_ROWS):
            gate_ref[row0 + r : row0 + r + 1, :] = gate[:, r * LANES : (r + 1) * LANES]
        slot_iota = iota((slots, LANES), 0)
        hot = [(slot_iota == pos[r : r + 1]).astype(F32).astype(BF16) for r in range(row0, row0 + BLOCK_ROWS)]
        picked = jnp.dot(jnp.concatenate(hot, axis=1), x, preferred_element_type=F32).astype(BF16)
        at = pl.ds((pl.program_id(0) * (rows // BLOCK_ROWS) + sub) * grans, grans)
        xs_ref[at] = picked.reshape(grans, GRAN, picked.shape[1])


def expert_names(bits):
    me = lax.axis_index("ep_b") * lax.axis_size("ep_a") + lax.axis_index("ep_a")
    return [me ^ bit for bit in bits]


def run_expert(e, tile, list_ref, start_count, b_ref, w1_ref, w2_ref, xs_ref, h_buf, put):
    width, hidden = w1_ref.shape
    total = start_count
    b1 = b_ref[:, 0:hidden].astype(F32)
    b2 = b_ref[:, hidden : hidden + width].astype(F32)

    def per_tile(t, _):
        names = [list_ref[e, t * tile + k] for k in range(tile)]
        x = jnp.concatenate([xs_ref[name] for name in names], axis=0)
        step = 256
        for c in range(0, hidden, step):
            pre = jnp.dot(x, w1_ref[:, c : c + step], preferred_element_type=F32) + b1[:, c : c + step]
            act = 0.5 * pre * (1.0 + lax.erf(pre * F32(0.5**0.5)))
            h_buf[:, c : c + step] = act.astype(BF16)
        y = jnp.dot(h_buf[...], w2_ref[...], preferred_element_type=F32) + b2
        put(t, names, y.astype(BF16))
        return 0

    lax.fori_loop(0, (total + tile - 1) // tile, per_tile, 0)


def expert_kernel(bits, tile, spare, count_ref, offset_ref, list_ref, xs_ref, *refs):
    count, experts = len(bits), expert_names(bits)
    w1_refs, w2_refs, b_refs = refs[:count], refs[count : 2 * count], refs[2 * count : 3 * count]
    out_ref, h_buf = refs[3 * count :]
    last = count_ref.shape[0] - 1

    def put(t, names, y):
        for k, name in enumerate(names):
            out_ref[jnp.where(name == spare, spare + 1, name)] = y[k * GRAN : (k + 1) * GRAN]

    for i in range(count):
        e = experts[i]
        run_expert(e, tile, list_ref, offset_ref[last, e] + count_ref[last, e], b_refs[i], w1_refs[i], w2_refs[i], xs_ref, h_buf, put)


def final_kernel(
    bits, tile, window, start_ref, count_ref, offset_ref, list_ref, pos_ref, gate_ref, ids_ref, xs_ref, part_ref, *refs
):
    count, experts = len(bits), expert_names(bits)
    w1_refs, w2_refs, b_refs = refs[:count], refs[count : 2 * count], refs[2 * count : 3 * count]
    out_ref, h_buf, y_buf, o_buf, o_sem = refs[3 * count :]
    blocks = start_ref.shape[0]
    width = w1_refs[0].shape[0]
    block_tok = BLOCK_ROWS * LANES
    totals = [offset_ref[blocks - 1, experts[i]] + count_ref[blocks - 1, experts[i]] for i in range(count)]
    for i in range(count):

        def put(t, names, y):
            y_buf[i, pl.ds(t * tile, tile)] = y.reshape(tile, GRAN, width)

        run_expert(experts[i], tile, list_ref, totals[i], b_refs[i], w1_refs[i], w2_refs[i], xs_ref, h_buf, put)
        y_buf[i, pl.ds((totals[i] + tile - 1) // tile * tile, window)] = jnp.zeros((window, GRAN, width), BF16)
    lane = iota((LANES, window * GRAN), 1).astype(F32)

    def out_copy(pair, slot):
        rows = pl.ds(pl.multiple_of(pair * 2 * block_tok, 2 * block_tok), 2 * block_tok)
        return pltpu.make_async_copy(o_buf.at[slot], out_ref.at[rows], o_sem.at[slot])

    def per_pair(pair, _):
        slot = pair % 2
        row0 = pl.multiple_of(pair * 2 * BLOCK_ROWS, 2 * BLOCK_ROWS)
        rows8 = pl.ds(row0, 2 * BLOCK_ROWS)
        pos8, gate8, ids8 = pos_ref[rows8, :], gate_ref[rows8, :], ids_ref[rows8, :]
        gate_cols = jnp.transpose(gate8)
        upper = iota(pos8.shape, 0) < BLOCK_ROWS
        local = []
        for i in range(count):
            e = experts[i]
            origin = jnp.where(upper, start_ref[2 * pair, e], start_ref[2 * pair + 1, e]) * GRAN
            mine = (ids8 == e) & (pos8 >= 0)
            local.append(jnp.transpose(jnp.where(mine, pos8 - origin, -1).astype(F32)))

        def window_rows(sub, w, offsets):
            ys = jnp.concatenate(
                [y_buf[i, pl.ds(jnp.minimum(offsets[i] + w * window, totals[i]), window)].reshape(window * GRAN, width) for i in range(count)],
                axis=0,
            )
            shift = jnp.asarray(w * (window * GRAN)).astype(F32)
            hot = []
            for r in range(sub * BLOCK_ROWS, (sub + 1) * BLOCK_ROWS):
                hot.append(jnp.concatenate([(lane == local[i][:, r : r + 1] - shift).astype(F32).astype(BF16) for i in range(count)], axis=1))
            return jnp.dot(jnp.concatenate(hot, axis=0), ys, preferred_element_type=F32)

        def scaled(sub, back, r):
            return back[r * LANES : (r + 1) * LANES] * gate_cols[:, sub * BLOCK_ROWS + r : sub * BLOCK_ROWS + r + 1]

        @pl.when(pair >= 2)
        def _():
            out_copy(pair, slot).wait()

        for sub in range(2):
            b = 2 * pair + sub
            sizes = [count_ref[b, experts[i]] for i in range(count)]
            starts = [offset_ref[b, experts[i]] for i in range(count)]
            back = window_rows(sub, 0, starts)
            for r in range(BLOCK_ROWS):
                source = pl.ds(pl.multiple_of(b * block_tok + r * LANES, LANES), LANES)
                at = slice((sub * BLOCK_ROWS + r) * LANES, (sub * BLOCK_ROWS + r + 1) * LANES)
                o_buf[slot, at, :] = (part_ref[source, :].astype(F32) + scaled(sub, back, r)).astype(BF16)

        for sub in range(2):
            b = 2 * pair + sub
            sizes = [count_ref[b, experts[i]] for i in range(count)]
            starts = [offset_ref[b, experts[i]] for i in range(count)]
            longest = sizes[0]
            for size in sizes[1:]:
                longest = jnp.maximum(longest, size)

            def more(w, _):
                back = window_rows(sub, w, starts)
                for r in range(BLOCK_ROWS):
                    at = slice((sub * BLOCK_ROWS + r) * LANES, (sub * BLOCK_ROWS + r + 1) * LANES)
                    o_buf[slot, at, :] = (o_buf[slot, at, :].astype(F32) + scaled(sub, back, r)).astype(BF16)
                return 0

            lax.fori_loop(1, (longest + window - 1) // window, more, 0)
        out_copy(pair, slot).start()
        return 0

    lax.fori_loop(0, blocks // 2, per_pair, 0)
    for slot in range(2):
        out_copy(0, slot).wait()


def combine_kernel(slots, bits, ys_ref, pos_ref, gate_ref, ids_ref, out_ref):
    experts = expert_names(bits)
    rows = pos_ref.shape[0]
    pos_cols = jnp.transpose(pos_ref[...].astype(F32))
    later = (ids_ref[...] == experts[0]) | (ids_ref[...] == experts[1])
    gate_cols = jnp.transpose(jnp.where(later, 0.0, gate_ref[...]))
    grans = slots // GRAN
    slot_iota = iota((LANES, slots), 1).astype(F32)
    for sub in range(rows // BLOCK_ROWS):
        row0 = sub * BLOCK_ROWS
        y = ys_ref[pl.ds((pl.program_id(0) * (rows // BLOCK_ROWS) + sub) * grans, grans)].reshape(slots, ys_ref.shape[2])
        hot = [(slot_iota == pos_cols[:, r : r + 1]).astype(F32).astype(BF16) for r in range(row0, row0 + BLOCK_ROWS)]
        back = jnp.dot(jnp.concatenate(hot, axis=0), y, preferred_element_type=F32)
        for r in range(BLOCK_ROWS):
            at = pl.ds(pl.multiple_of(((pl.program_id(0) * rows) + row0 + r) * LANES, LANES), LANES)
            scaled = back[r * LANES : (r + 1) * LANES] * gate_cols[:, row0 + r : row0 + r + 1]
            out_ref[at, :] = scaled.astype(BF16)


def vmem():
    return pl.BlockSpec(memory_space=pltpu.VMEM)


def smem():
    return pl.BlockSpec(memory_space=pltpu.SMEM)


def hbm():
    return pl.BlockSpec(memory_space=pl.ANY)


def solution(mesh):
    num_experts = mesh.shape["ep_b"] * mesh.shape["ep_a"]
    tok_spec = P(("dp",) + EXPERT_AXES)
    expert_spec = P(EXPERT_AXES)

    def swap(value, bit):
        return lax.ppermute(value, EXPERT_AXES, [(e, e ^ bit) for e in range(num_experts)])

    def inner_step(tokens, expert_ids, route_order, w_route, expert_keys, value_a11, w_in, b_in, w_out, b_out):
        tok_dev, width = tokens.shape[1], tokens.shape[2]
        hidden = w_in.shape[2]
        router = w_route.shape[1]
        capacity = (5 * tok_dev + 4 * num_experts - 1) // (4 * num_experts)
        rows = tok_dev // LANES
        blocks = rows // BLOCK_ROWS
        slots = -(-(BLOCK_ROWS * LANES + num_experts * (GRAN - 1)) // LANES) * LANES
        span = slots // GRAN

        first, second = w_in[0], w_out[0]
        x_first, y_second = swap(first, 2), swap(second, 4)
        x_second, y_first = swap(second, 2), swap(first, 4)
        c_first, c_second = swap(first, 1), swap(second, 1)
        own_bias = jnp.concatenate([b_in, b_out], axis=1)
        bias = [own_bias] + [swap(own_bias, bit) for bit in range(1, num_experts)]

        ids, order = expert_ids.reshape(rows, LANES), route_order.reshape(rows, LANES)
        unit = 2 * BLOCK_ROWS
        small = functools.partial(pl.BlockSpec, index_map=lambda i: (0, 0))
        whole = small((rows, LANES))
        table = small((blocks, LANES))
        xs_shape = (blocks * span + 8, GRAN, width)
        pos, starts, counts, offsets, lists, gate, xs = pl.pallas_call(
            functools.partial(dispatch_kernel, router, num_experts, capacity, slots),
            out_shape=(
                jax.ShapeDtypeStruct((rows, LANES), jnp.int32),
                jax.ShapeDtypeStruct((blocks, LANES), jnp.int32),
                jax.ShapeDtypeStruct((blocks, LANES), jnp.int32),
                jax.ShapeDtypeStruct((blocks, LANES), jnp.int32),
                jax.ShapeDtypeStruct((num_experts, LANES), jnp.int32),
                jax.ShapeDtypeStruct((rows, LANES), F32),
                pltpu.VMEM(xs_shape, BF16),
            ),
            grid=(rows // unit,),
            in_specs=[
                smem(),
                whole,
                whole,
                small((width, router)),
                small((num_experts, router)),
                pl.BlockSpec((unit * LANES, width), lambda i: (i, 0)),
            ],
            out_specs=(
                whole,
                table,
                table,
                table,
                small((num_experts, LANES)),
                pl.BlockSpec((unit, LANES), lambda i: (i, 0)),
                vmem(),
            ),
            scratch_shapes=[pltpu.VMEM((router + 4 * num_experts, width), BF16)],
            cost_estimate=pl.CostEstimate(flops=9 * 10**9, bytes_accessed=14 * 10**6, transcendentals=0),
            compiler_params=pltpu.CompilerParams(vmem_limit_bytes=12 * 2**20),
            name="dispatch",
        )(value_a11.reshape(1, 1), ids, order, w_route, expert_keys, tokens[0])

        most = -(-(capacity + blocks * (GRAN - 1)) // (16 * GRAN)) * 16
        tile, window = 16, 8
        held = lambda array: pltpu.with_memory_space_constraint(array, pltpu.VMEM)

        def experts(bits, xs, firsts, seconds):
            n = len(bits)
            return pl.pallas_call(
                functools.partial(expert_kernel, bits, tile, blocks * span),
                out_shape=pltpu.VMEM(xs.shape, BF16),
                in_specs=[smem()] * 3 + [vmem()] * (1 + 3 * n),
                out_specs=vmem(),
                scratch_shapes=[pltpu.VMEM((tile * GRAN, hidden), BF16)],
                input_output_aliases={3: 0},
                cost_estimate=pl.CostEstimate(flops=3 * n * 10**9, bytes_accessed=4 * n * 10**6, transcendentals=0),
                compiler_params=pltpu.CompilerParams(vmem_limit_bytes=8 * 2**20),
            )(counts, offsets, lists, held(xs), *map(held, firsts), *map(held, seconds), *[bias[bit] for bit in bits])

        xs = experts((0, 1), xs, (first, c_first), (second, c_second))
        x_first, y_second, xs = lax.optimization_barrier((x_first, y_second, xs))
        d_first, d_second = swap(x_first, 4), swap(y_second, 2)
        cx_first, cy_second = swap(x_first, 1), swap(y_second, 1)
        cx_second, cy_first = swap(x_second, 1), swap(y_first, 1)
        xs = experts((2, 3, 4, 5), xs, (x_first, cx_first, y_first, cy_first), (x_second, cx_second, y_second, cy_second))
        part = pl.pallas_call(
            functools.partial(combine_kernel, slots, (6, 7)),
            out_shape=pltpu.VMEM((tok_dev, width), BF16),
            grid=(rows // unit,),
            in_specs=[
                vmem(),
                pl.BlockSpec((unit, LANES), lambda i: (i, 0)),
                pl.BlockSpec((unit, LANES), lambda i: (i, 0)),
                pl.BlockSpec((unit, LANES), lambda i: (i, 0)),
            ],
            out_specs=vmem(),
            cost_estimate=pl.CostEstimate(flops=5 * 10**9, bytes_accessed=14 * 10**6, transcendentals=0),
            compiler_params=pltpu.CompilerParams(vmem_limit_bytes=8 * 2**20),
            name="combine",
        )(held(xs), pos, gate, ids)
        d_first, d_second, part = lax.optimization_barrier((d_first, d_second, part))
        firsts = (d_first, swap(d_first, 1))
        seconds = (d_second, swap(d_second, 1))
        out = pl.pallas_call(
            functools.partial(final_kernel, (6, 7), tile, window),
            out_shape=jax.ShapeDtypeStruct((tok_dev, width), BF16),
            in_specs=[smem()] * 4 + [vmem()] * (5 + 6),
            out_specs=hbm(),
            scratch_shapes=[
                pltpu.VMEM((tile * GRAN, hidden), BF16),
                pltpu.VMEM((2, most + tile, GRAN, width), BF16),
                pltpu.VMEM((2, 2 * BLOCK_ROWS * LANES, width), BF16),
                pltpu.SemaphoreType.DMA((2,)),
            ],
            cost_estimate=pl.CostEstimate(flops=7 * 10**9, bytes_accessed=8 * 10**6, transcendentals=0),
            compiler_params=pltpu.CompilerParams(vmem_limit_bytes=12 * 2**20),
            name="final",
        )(
            starts, counts, offsets, lists, pos, gate, ids, held(xs), held(part),
            *map(held, firsts), *map(held, seconds), bias[6], bias[7],
        )
        return out[None]

    return jax.shard_map(
        inner_step,
        mesh=mesh,
        in_specs=(tok_spec, tok_spec, tok_spec, P(), P(), P(), expert_spec, expert_spec, expert_spec, expert_spec),
        out_specs=tok_spec,
        check_vma=False,
    )
```

time: 139 us -> 128 us (0.921)
  Pallas kernels: 86.6 us -> 71.2 us
  local copies, waits for them, and re-layouts: 3.45 us -> 7.31 us
  waiting for transfers between devices: 29.2 us -> 31.8 us
  other arithmetic: 1.94 us -> 0 us
    pallas_call x4, Pallas kernels: 68.7 us -> 55.7 us  [the longest x2 30.2 us: experts(): pl.pallas_call(functools.partial(expert_kernel, bits, tile, blocks * span...]
    unnamed x25 -> x17, local copies, waits for them, and re-layouts: 2.76 us -> 6.62 us
    ppermute x21, waiting for transfers between devices: 29.2 us -> 31.8 us  [swap(): lax.ppermute(value, EXPERT_AXES, [(e, e ^ bit) for e in range(num_experts)])]
    pallas_call x1, Pallas kernels: 17.9 us -> 15.5 us  [inner_step(): pl.pallas_call(functools.partial(dispatch_kernel, router, num_experts, ca...]
    reshape x3 -> x0, other arithmetic: 1.94 us -> none  [eids(): jnp.stack([me ^ bit for bit in bits]).reshape(1, len(bits))]
  transfers between devices with their start and end apart: 21 -> 21, of which waited for: 7 -> 7; matrix products, arithmetic and copies ran while one was open for 2% -> 1% of each run, Pallas kernels for 50% -> 43%
where the time goes in v1:
time: 128 us; the launch traced here: 126 us
  Pallas kernels  71.2 us (56%)
  waiting for transfers between devices  31.8 us (25%)
  starting transfers between devices  15.2 us (12%)
  local copies, waits for them, and re-layouts  7.31 us (6%)
    ppermute x21, waiting for transfers between devices, swap(): lax.ppermute(value, EXPERT_AXES, [(e, e ^ bit) for e in range(num_experts)])  31.8 us
    pallas_call x2, Pallas kernels, experts(): pl.pallas_call(functools.partial(expert_kernel, bits, tile, blocks * span...  30.2 us
    pallas_call x1, Pallas kernels, inner_step(): pl.pallas_call(functools.partial(final_kernel, (6, 7), tile, window), out...  16.6 us
    pallas_call x1, Pallas kernels, inner_step(): pl.pallas_call(functools.partial(dispatch_kernel, router, num_experts, ca...  15.5 us
    ppermute x21, starting transfers between devices, swap(): lax.ppermute(value, EXPERT_AXES, [(e, e ^ bit) for e in range(num_experts)])  15.2 us
    pallas_call x1, Pallas kernels, inner_step(): pl.pallas_call(functools.partial(combine_kernel, slots, (6, 7)), out_shap...  8.83 us
    unnamed x17, local copies, waits for them, and re-layouts  6.62 us
  transfers between devices with their start and end apart: 21, of which 7 were waited for; matrix products, arithmetic and copies ran while one was open for 1% of the time, Pallas kernels for 43%

profile of v1, /device:TPU:0, one launch (start us, length us, event | category | flops | bytes accessed | tf_op | source)
XLA Modules:
  0.0 126.3 jit_solution(5510766654648062052)
XLA Ops:
  0.0 0.8 collective-permute-start.2
  2.7 2.5 %collective-permute-start = (bf16[384,1536]{1,0:T(8,128)(2,1)}, bf16[384,1536]{1,0:T(8,128)(2,1)S(1)}, u32[]{:S(2)}, u32[]{:S(2)}) collective-permute-start(bf16[384,1536]{1,0:T(8,128)(2,1)} %bitcast.10), channel_id=1, source_target_pairs={{0,2},{1,3},{2,0},{3,1},{4,6},{5,7},{6,4},{7,5}} | collective-permute-start | bytes 3538952 | tf_op jit(solution)/shard_map/ppermute | solution.py:316
  5.2 1.5 %collective-permute-start.1 = (bf16[1536,384]{1,0:T(8,128)(2,1)}, bf16[1536,384]{1,0:T(8,128)(2,1)S(1)}, u32[]{:S(2)}, u32[]{:S(2)}) collective-permute-start(bf16[1536,384]{1,0:T(8,128)(2,1)} %bitcast.14), channel_id=1, source_target_pairs={{0,4},{1,5},{2,6},{3,7},{4,0},{5,1},{6,2},{7,3}} | collective-permute-start | bytes 3538952 | tf_op jit(solution)/shard_map/ppermute | solution.py:316
  7.4 0.8 collective-permute-start.6
  8.2 1.5 %collective-permute-start.8 = (bf16[1536,384]{1,0:T(8,128)(2,1)}, bf16[1536,384]{1,0:T(8,128)(2,1)S(1)}, u32[]{:S(2)}, u32[]{:S(2)}) collective-permute-start(bf16[1536,384]{1,0:T(8,128)(2,1)} %bitcast.15), channel_id=1, source_target_pairs={{0,2},{1,3},{2,0},{3,1},{4,6},{5,7},{6,4},{7,5}} | collective-permute-start | bytes 3538952 | tf_op jit(solution)/shard_map/ppermute | solution.py:316
  9.7 2.8 %copy-done = bf16[1,8192,384]{2,1,0:T(8,128)(2,1)S(1)} copy-done((bf16[1,8192,384]{2,1,0:T(8,128)(2,1)S(1)}, bf16[1,8192,384]{2,1,0:T(8,128)(2,1)}, u32[]{:S(2)}) %copy-start) | copy-done | bytes 6291480
  12.5 0.9 copy-done.3
  13.4 0.8 copy-done.4
  14.2 0.8 copy-done.5
  15.6 15.5 %dispatch.1 = (s32[64,128]{1,0:T(8,128)S(1)}, s32[16,128]{1,0:T(8,128)S(1)}, s32[16,128]{1,0:T(8,128)S(1)}, s32[16,128]{1,0:T(8,128)S(1)}, s32[8,128]{1,0:T(8,12...) custom-call(f32[1,1]{1,0:T(1,128)} %bitcast.7.tau_ref, s32[64,128]{1,0:T(8,128)S(1)} %bitcast.18, ...), custom_call_target="tpu_custom_call" | custom-call | flops 8999999488 | bytes 14000000 | tf_op jit(solution)/shard_map/dispatch/pallas_call | solution.py:341
  31.2 11.2 %shard_map.100.xs_ref = bf16[648,16,384]{2,1,0:T(8,128)(2,1)S(1)} custom-call(s32[16,128]{1,0:T(8,128)S(1)} %get-tuple-element.19.count_ref, s32[16,128]{1,0:T(8,128)S(1)} %get-tuple-element.20.offset_ref, s32[8,128]{1,0:T(8,128)S(1)} %get-tuple-element.21.list_ref, ...), custom_call_target="tpu_custom_call", output_to_operand_aliasing={{}: (3, {})} | custom-call | flops 6000000000 | bytes 8000000 | tf_op jit(solution)/shard_map/pallas_call | solution.py:382
  42.5 16.3 %collective-permute-done.6.refs_2_ = bf16[384,1536]{1,0:T(8,128)(2,1)S(1)} collective-permute-done((bf16[384,1536]{1,0:T(8,128)(2,1)}, bf16[384,1536]{1,0:T(8,128)(2,1)S(1)}, u32[]{:S(2)}, u32[]{:S(2)}) %collective-permute-start.6) | collective-permute-done | bytes 1179680 | tf_op jit(solution)/shard_map/ppermute | solution.py:316
  59.6 3.3 %collective-permute-done.11.refs_8_ = bf16[1,1920]{1,0:T(2,128)(2,1)S(1)} collective-permute-done((bf16[1,1920]{1,0:T(2,128)(2,1)S(1)}, bf16[1,1920]{1,0:T(2,128)(2,1)S(1)}, u32[]{:S(2)}, u32[]{:S(2)}) %collective-permute-start.11) | collective-permute-done | bytes 3872 | tf_op jit(solution)/shard_map/ppermute | solution.py:316
  63.0 3.1 %collective-permute-done.12.refs_9_ = bf16[1,1920]{1,0:T(2,128)(2,1)S(1)} collective-permute-done((bf16[1,1920]{1,0:T(2,128)(2,1)S(1)}, bf16[1,1920]{1,0:T(2,128)(2,1)S(1)}, u32[]{:S(2)}, u32[]{:S(2)}) %collective-permute-start.12) | collective-permute-done | bytes 3872 | tf_op jit(solution)/shard_map/ppermute | solution.py:316
  66.0 1.5 %collective-permute-start.13 = (bf16[1,1920]{1,0:T(2,128)(2,1)S(1)}, bf16[1,1920]{1,0:T(2,128)(2,1)S(1)}, u32[]{:S(2)}, u32[]{:S(2)}) collective-permute-start(bf16[1,1920]{1,0:T(2,128)(2,1)S(1)} %constant_dynamic-update-slice_fusion.refs_4_), channel_id=1, source_target_pairs={{0,4},{1,5},{2,6},{3,7},{4,0},{5,1},{6,2},{7,3}} | collective-permute-start | bytes 11528 | tf_op jit(solution)/shard_map/ppermute | solution.py:316
  67.6 2.1 %collective-permute-done.13.refs_10_ = bf16[1,1920]{1,0:T(2,128)(2,1)S(1)} collective-permute-done((bf16[1,1920]{1,0:T(2,128)(2,1)S(1)}, bf16[1,1920]{1,0:T(2,128)(2,1)S(1)}, u32[]{:S(2)}, u32[]{:S(2)}) %collective-permute-start.13) | collective-permute-done | bytes 3872 | tf_op jit(solution)/shard_map/ppermute | solution.py:316
  69.7 3.1 %collective-permute-done.14.refs_11_ = bf16[1,1920]{1,0:T(2,128)(2,1)S(1)} collective-permute-done((bf16[1,1920]{1,0:T(2,128)(2,1)S(1)}, bf16[1,1920]{1,0:T(2,128)(2,1)S(1)}, u32[]{:S(2)}, u32[]{:S(2)}) %collective-permute-start.14) | collective-permute-done | bytes 3872 | tf_op jit(solution)/shard_map/ppermute | solution.py:316
  72.8 1.5 %collective-permute-start.15 = (bf16[384,1536]{1,0:T(8,128)(2,1)S(1)}, bf16[384,1536]{1,0:T(8,128)(2,1)S(1)}, u32[]{:S(2)}, u32[]{:S(2)}) collective-permute-start(bf16[384,1536]{1,0:T(8,128)(2,1)S(1)} %collective-permute-done.refs_0_), channel_id=1, source_target_pairs={{0,4},{1,5},{2,6},{3,7},{4,0},{5,1},{6,2},{7,3}} | collective-permute-start | bytes 3538952 | tf_op jit(solution)/shard_map/ppermute | solution.py:316
  74.9 19.0 %shard_map.101.ys_ref.xs_ref = bf16[648,16,384]{2,1,0:T(8,128)(2,1)S(1)} custom-call(s32[16,128]{1,0:T(8,128)S(1)} %get-tuple-element.19.count_ref, s32[16,128]{1,0:T(8,128)S(1)} %get-tuple-element.20.offset_ref, s32[8,128]{1,0:T(8,128)S(1)} %get-tuple-element.21.list_ref, ...), custom_call_target="tpu_custom_call", output_to_operand_aliasing={{}: (3, {})} | custom-call | flops 12000000000 | bytes 16000000 | tf_op jit(solution)/shard_map/pallas_call | solution.py:382
  93.8 8.8 %combine.1.part_ref = bf16[8192,384]{1,0:T(8,128)(2,1)S(1)} custom-call(bf16[648,16,384]{2,1,0:T(8,128)(2,1)S(1)} %shard_map.101.ys_ref.xs_ref, s32[64,128]{1,0:T(8,128)S(1)} %get-tuple-element.22.pos_ref, f32[64,128]{1,0:T(8,128)S(1)} %get-tuple-element.23.gate_ref, s32[64,128]{1,0:T(8,128)S(1)} %bitcast.19), custom_call_target="tpu_custom_call" | custom-call | flops 5000000000 | bytes 14000000 | tf_op jit(solution)/shard_map/combine/pallas_call | solution.py:399
  103.2 2.5 %collective-permute-start.19 = (bf16[1,1920]{1,0:T(2,128)(2,1)S(1)}, bf16[1,1920]{1,0:T(2,128)(2,1)S(1)}, u32[]{:S(2)}, u32[]{:S(2)}) collective-permute-start(bf16[1,1920]{1,0:T(2,128)(2,1)S(1)} %constant_dynamic-update-slice_fusion.refs_4_), channel_id=1, source_target_pairs={{0,6},{1,7},{2,4},{3,5},{4,2},{5,3},{6,0},{7,1}} | collective-permute-start | bytes 11528 | tf_op jit(solution)/shard_map/ppermute | solution.py:316
  105.8 2.0 %collective-permute-done.19.refs_4_ = bf16[1,1920]{1,0:T(2,128)(2,1)S(1)} collective-permute-done((bf16[1,1920]{1,0:T(2,128)(2,1)S(1)}, bf16[1,1920]{1,0:T(2,128)(2,1)S(1)}, u32[]{:S(2)}, u32[]{:S(2)}) %collective-permute-start.19) | collective-permute-done | bytes 3872 | tf_op jit(solution)/shard_map/ppermute | solution.py:316
  107.8 1.9 %collective-permute-done.20.refs_5_ = bf16[1,1920]{1,0:T(2,128)(2,1)S(1)} collective-permute-done((bf16[1,1920]{1,0:T(2,128)(2,1)S(1)}, bf16[1,1920]{1,0:T(2,128)(2,1)S(1)}, u32[]{:S(2)}, u32[]{:S(2)}) %collective-permute-start.20) | collective-permute-done | bytes 3872 | tf_op jit(solution)/shard_map/ppermute | solution.py:316
  109.7 16.6 %final.1 = bf16[8192,384]{1,0:T(8,128)(2,1)} custom-call(s32[16,128]{1,0:T(8,128)S(1)} %get-tuple-element.18.start_ref, s32[16,128]{1,0:T(8,128)S(1)} %get-tuple-element.19.count_ref, s32[16,128]{1,0:T(8,128)S(1)} %get-tuple-element.20.offset_ref, s32[8,128]{1,0:T(8,128)S(1)} %get-tuple-element.21.list_ref, s32[64,128]{1,0:T(8,128)S(1)} %get-tuple-element.22.pos_ref, ...), custom_call_target="tpu_custom_call" | custom-call | flops 7000000000 | bytes 8000000 | tf_op jit(solution)/shard_map/final/pallas_call | solution.py:417
  (41 shorter events, 4.7 us)
Async XLA Ops:
  0.0 8.2 %collective-permute-start.2 = (bf16[384,1536]{1,0:T(8,128)(2,1)}, bf16[384,1536]{1,0:T(8,128)(2,1)S(1)}, u32[]{:S(2)}, u32[]{:S(2)}) collective-permute-start(bf16[384,1536]{1,0:T(8,128)(2,1)} %bitcast.9), channel_id=1, source_target_pairs={{0,1},{1,0},{2,3},{3,2},{4,5},{5,4},{6,7},{7,6}} | collective-permute-start | bytes 3538952 | tf_op jit(solution)/shard_map/ppermute | solution.py:316
  0.8 30.3 %collective-permute-start.3 = (bf16[1536,384]{1,0:T(8,128)(2,1)}, bf16[1536,384]{1,0:T(8,128)(2,1)}, u32[]{:S(2)}, u32[]{:S(2)}) collective-permute-start(bf16[1536,384]{1,0:T(8,128)(2,1)} %bitcast.13), channel_id=1, source_target_pairs={{0,1},{1,0},{2,3},{3,2},{4,5},{5,4},{6,7},{7,6}} | collective-permute-start | bytes 3538952 | tf_op jit(solution)/shard_map/ppermute | solution.py:316
  2.2 5.2 %collective-permute-start.4 = (bf16[1,1920]{1,0:T(2,128)(2,1)S(1)}, bf16[1,1920]{1,0:T(2,128)(2,1)S(1)}, u32[]{:S(2)}, u32[]{:S(2)}) collective-permute-start(bf16[1,1920]{1,0:T(2,128)(2,1)S(1)} %constant_dynamic-update-slice_fusion.refs_4_), channel_id=1, source_target_pairs={{0,1},{1,0},{2,3},{3,2},{4,5},{5,4},{6,7},{7,6}} | collective-permute-start | bytes 11528 | tf_op jit(solution)/shard_map/ppermute | solution.py:316
  2.7 39.7 %collective-permute-start = (bf16[384,1536]{1,0:T(8,128)(2,1)}, bf16[384,1536]{1,0:T(8,128)(2,1)S(1)}, u32[]{:S(2)}, u32[]{:S(2)}) collective-permute-start(bf16[384,1536]{1,0:T(8,128)(2,1)} %bitcast.10), channel_id=1, source_target_pairs={{0,2},{1,3},{2,0},{3,1},{4,6},{5,7},{6,4},{7,5}} | collective-permute-start | bytes 3538952 | tf_op jit(solution)/shard_map/ppermute | solution.py:316
  5.2 37.3 %collective-permute-start.1 = (bf16[1536,384]{1,0:T(8,128)(2,1)}, bf16[1536,384]{1,0:T(8,128)(2,1)S(1)}, u32[]{:S(2)}, u32[]{:S(2)}) collective-permute-start(bf16[1536,384]{1,0:T(8,128)(2,1)} %bitcast.14), channel_id=1, source_target_pairs={{0,4},{1,5},{2,6},{3,7},{4,0},{5,1},{6,2},{7,3}} | collective-permute-start | bytes 3538952 | tf_op jit(solution)/shard_map/ppermute | solution.py:316
  7.4 51.4 %collective-permute-start.6 = (bf16[384,1536]{1,0:T(8,128)(2,1)}, bf16[384,1536]{1,0:T(8,128)(2,1)S(1)}, u32[]{:S(2)}, u32[]{:S(2)}) collective-permute-start(bf16[384,1536]{1,0:T(8,128)(2,1)} %bitcast.11), channel_id=1, source_target_pairs={{0,4},{1,5},{2,6},{3,7},{4,0},{5,1},{6,2},{7,3}} | collective-permute-start | bytes 3538952 | tf_op jit(solution)/shard_map/ppermute | solution.py:316
  8.2 50.6 %collective-permute-start.8 = (bf16[1536,384]{1,0:T(8,128)(2,1)}, bf16[1536,384]{1,0:T(8,128)(2,1)S(1)}, u32[]{:S(2)}, u32[]{:S(2)}) collective-permute-start(bf16[1536,384]{1,0:T(8,128)(2,1)} %bitcast.15), channel_id=1, source_target_pairs={{0,2},{1,3},{2,0},{3,1},{4,6},{5,7},{6,4},{7,5}} | collective-permute-start | bytes 3538952 | tf_op jit(solution)/shard_map/ppermute | solution.py:316
  15.6 15.5 %copy-start.1 = (bf16[1,384,1536]{2,1,0:T(8,128)(2,1)S(1)}, bf16[1,384,1536]{2,1,0:T(8,128)(2,1)}, u32[]{:S(2)}) copy-start(bf16[1,384,1536]{2,1,0:T(8,128)(2,1)} %param.16) | copy-start | bytes 3538948
  15.6 15.5 %copy-start.2 = (bf16[1,1536,384]{2,1,0:T(8,128)(2,1)S(1)}, bf16[1,1536,384]{2,1,0:T(8,128)(2,1)}, u32[]{:S(2)}) copy-start(bf16[1,1536,384]{2,1,0:T(8,128)(2,1)} %param.18) | copy-start | bytes 3538948
  42.4 51.4 %copy-start.6 = (s32[1,8192]{1,0:T(1,128)S(1)}, s32[1,8192]{1,0:T(1,128)}, u32[]{:S(2)}) copy-start(s32[1,8192]{1,0:T(1,128)} %param.11) | copy-start | bytes 98308
  42.5 31.8 %collective-permute-start.5 = (bf16[384,1536]{1,0:T(8,128)(2,1)S(1)}, bf16[384,1536]{1,0:T(8,128)(2,1)S(1)}, u32[]{:S(2)}, u32[]{:S(2)}) collective-permute-start(bf16[384,1536]{1,0:T(8,128)(2,1)S(1)} %collective-permute-done.refs_0_), channel_id=1, source_target_pairs={{0,1},{1,0},{2,3},{3,2},{4,5},{5,4},{6,7},{7,6}} | collective-permute-start | bytes 3538952 | tf_op jit(solution)/shard_map/ppermute | solution.py:316
  58.8 16.1 %collective-permute-start.7 = (bf16[384,1536]{1,0:T(8,128)(2,1)S(1)}, bf16[384,1536]{1,0:T(8,128)(2,1)S(1)}, u32[]{:S(2)}, u32[]{:S(2)}) collective-permute-start(bf16[384,1536]{1,0:T(8,128)(2,1)S(1)} %collective-permute-done.6.refs_2_), channel_id=1, source_target_pairs={{0,1},{1,0},{2,3},{3,2},{4,5},{5,4},{6,7},{7,6}} | collective-permute-start | bytes 3538952 | tf_op jit(solution)/shard_map/ppermute | solution.py:316
  58.8 16.1 %collective-permute-start.9 = (bf16[1536,384]{1,0:T(8,128)(2,1)S(1)}, bf16[1536,384]{1,0:T(8,128)(2,1)S(1)}, u32[]{:S(2)}, u32[]{:S(2)}) collective-permute-start(bf16[1536,384]{1,0:T(8,128)(2,1)S(1)} %collective-permute-done.8.refs_4_), channel_id=1, source_target_pairs={{0,1},{1,0},{2,3},{3,2},{4,5},{5,4},{6,7},{7,6}} | collective-permute-start | bytes 3538952 | tf_op jit(solution)/shard_map/ppermute | solution.py:316
  59.3 15.5 %collective-permute-start.10 = (bf16[1536,384]{1,0:T(8,128)(2,1)S(1)}, bf16[1536,384]{1,0:T(8,128)(2,1)S(1)}, u32[]{:S(2)}, u32[]{:S(2)}) collective-permute-start(bf16[1536,384]{1,0:T(8,128)(2,1)S(1)} %collective-permute-done.1.refs_6_), channel_id=1, source_target_pairs={{0,1},{1,0},{2,3},{3,2},{4,5},{5,4},{6,7},{7,6}} | collective-permute-start | bytes 3538952 | tf_op jit(solution)/shard_map/ppermute | solution.py:316
  59.3 3.6 %collective-permute-start.11 = (bf16[1,1920]{1,0:T(2,128)(2,1)S(1)}, bf16[1,1920]{1,0:T(2,128)(2,1)S(1)}, u32[]{:S(2)}, u32[]{:S(2)}) collective-permute-start(bf16[1,1920]{1,0:T(2,128)(2,1)S(1)} %constant_dynamic-update-slice_fusion.refs_4_), channel_id=1, source_target_pairs={{0,2},{1,3},{2,0},{3,1},{4,6},{5,7},{6,4},{7,5}} | collective-permute-start | bytes 11528 | tf_op jit(solution)/shard_map/ppermute | solution.py:316
  63.0 3.1 %collective-permute-start.12 = (bf16[1,1920]{1,0:T(2,128)(2,1)S(1)}, bf16[1,1920]{1,0:T(2,128)(2,1)S(1)}, u32[]{:S(2)}, u32[]{:S(2)}) collective-permute-start(bf16[1,1920]{1,0:T(2,128)(2,1)S(1)} %constant_dynamic-update-slice_fusion.refs_4_), channel_id=1, source_target_pairs={{0,3},{1,2},{2,1},{3,0},{4,7},{5,6},{6,5},{7,4}} | collective-permute-start | bytes 11528 | tf_op jit(solution)/shard_map/ppermute | solution.py:316
  66.0 3.6 %collective-permute-start.13 = (bf16[1,1920]{1,0:T(2,128)(2,1)S(1)}, bf16[1,1920]{1,0:T(2,128)(2,1)S(1)}, u32[]{:S(2)}, u32[]{:S(2)}) collective-permute-start(bf16[1,1920]{1,0:T(2,128)(2,1)S(1)} %constant_dynamic-update-slice_fusion.refs_4_), channel_id=1, source_target_pairs={{0,4},{1,5},{2,6},{3,7},{4,0},{5,1},{6,2},{7,3}} | collective-permute-start | bytes 11528 | tf_op jit(solution)/shard_map/ppermute | solution.py:316
  69.7 3.1 %collective-permute-start.14 = (bf16[1,1920]{1,0:T(2,128)(2,1)S(1)}, bf16[1,1920]{1,0:T(2,128)(2,1)S(1)}, u32[]{:S(2)}, u32[]{:S(2)}) collective-permute-start(bf16[1,1920]{1,0:T(2,128)(2,1)S(1)} %constant_dynamic-update-slice_fusion.refs_4_), channel_id=1, source_target_pairs={{0,5},{1,4},{2,7},{3,6},{4,1},{5,0},{6,3},{7,2}} | collective-permute-start | bytes 11528 | tf_op jit(solution)/shard_map/ppermute | solution.py:316
  72.8 29.9 %collective-permute-start.15 = (bf16[384,1536]{1,0:T(8,128)(2,1)S(1)}, bf16[384,1536]{1,0:T(8,128)(2,1)S(1)}, u32[]{:S(2)}, u32[]{:S(2)}) collective-permute-start(bf16[384,1536]{1,0:T(8,128)(2,1)S(1)} %collective-permute-done.refs_0_), channel_id=1, source_target_pairs={{0,4},{1,5},{2,6},{3,7},{4,0},{5,1},{6,2},{7,3}} | collective-permute-start | bytes 3538952 | tf_op jit(solution)/shard_map/ppermute | solution.py:316
  74.3 28.4 %collective-permute-start.16 = (bf16[1536,384]{1,0:T(8,128)(2,1)S(1)}, bf16[1536,384]{1,0:T(8,128)(2,1)S(1)}, u32[]{:S(2)}, u32[]{:S(2)}) collective-permute-start(bf16[1536,384]{1,0:T(8,128)(2,1)S(1)} %collective-permute-done.1.refs_6_), channel_id=1, source_target_pairs={{0,2},{1,3},{2,0},{3,1},{4,6},{5,7},{6,4},{7,5}} | collective-permute-start | bytes 3538952 | tf_op jit(solution)/shard_map/ppermute | solution.py:316
  102.7 7.0 %collective-permute-start.17 = (bf16[384,1536]{1,0:T(8,128)(2,1)S(1)}, bf16[384,1536]{1,0:T(8,128)(2,1)S(1)}, u32[]{:S(2)}, u32[]{:S(2)}) collective-permute-start(bf16[384,1536]{1,0:T(8,128)(2,1)S(1)} %collective-permute-done.15.refs_0_), channel_id=1, source_target_pairs={{0,1},{1,0},{2,3},{3,2},{4,5},{5,4},{6,7},{7,6}} | collective-permute-start | bytes 3538952 | tf_op jit(solution)/shard_map/ppermute | solution.py:316
  102.7 7.0 %collective-permute-start.18 = (bf16[1536,384]{1,0:T(8,128)(2,1)S(1)}, bf16[1536,384]{1,0:T(8,128)(2,1)S(1)}, u32[]{:S(2)}, u32[]{:S(2)}) collective-permute-start(bf16[1536,384]{1,0:T(8,128)(2,1)S(1)} %collective-permute-done.16.refs_2_), channel_id=1, source_target_pairs={{0,1},{1,0},{2,3},{3,2},{4,5},{5,4},{6,7},{7,6}} | collective-permute-start | bytes 3538952 | tf_op jit(solution)/shard_map/ppermute | solution.py:316
  103.2 4.5 %collective-permute-start.19 = (bf16[1,1920]{1,0:T(2,128)(2,1)S(1)}, bf16[1,1920]{1,0:T(2,128)(2,1)S(1)}, u32[]{:S(2)}, u32[]{:S(2)}) collective-permute-start(bf16[1,1920]{1,0:T(2,128)(2,1)S(1)} %constant_dynamic-update-slice_fusion.refs_4_), channel_id=1, source_target_pairs={{0,6},{1,7},{2,4},{3,5},{4,2},{5,3},{6,0},{7,1}} | collective-permute-start | bytes 11528 | tf_op jit(solution)/shard_map/ppermute | solution.py:316
  105.7 4.0 %collective-permute-start.20 = (bf16[1,1920]{1,0:T(2,128)(2,1)S(1)}, bf16[1,1920]{1,0:T(2,128)(2,1)S(1)}, u32[]{:S(2)}, u32[]{:S(2)}) collective-permute-start(bf16[1,1920]{1,0:T(2,128)(2,1)S(1)} %constant_dynamic-update-slice_fusion.refs_4_), channel_id=1, source_target_pairs={{0,7},{1,6},{2,5},{3,4},{4,3},{5,2},{6,1},{7,0}} | collective-permute-start | bytes 11528 | tf_op jit(solution)/shard_map/ppermute | solution.py:316
  (5 other events, 5.9 us)

commit v2 on v1

--- a/solution.py
+++ b/solution.py
@@ -151,60 +151,127 @@
     return [me ^ bit for bit in bits]
 
 
-def run_expert(e, tile, list_ref, start_count, b_ref, w1_ref, w2_ref, xs_ref, h_buf, put):
-    width, hidden = w1_ref.shape
-    total = start_count
-    b1 = b_ref[:, 0:hidden].astype(F32)
-    b2 = b_ref[:, hidden : hidden + width].astype(F32)
-
-    def per_tile(t, _):
-        names = [list_ref[e, t * tile + k] for k in range(tile)]
-        x = jnp.concatenate([xs_ref[name] for name in names], axis=0)
-        step = 256
-        for c in range(0, hidden, step):
-            pre = jnp.dot(x, w1_ref[:, c : c + step], preferred_element_type=F32) + b1[:, c : c + step]
-            act = 0.5 * pre * (1.0 + lax.erf(pre * F32(0.5**0.5)))
-            h_buf[:, c : c + step] = act.astype(BF16)
-        y = jnp.dot(h_buf[...], w2_ref[...], preferred_element_type=F32) + b2
-        put(t, names, y.astype(BF16))
-        return 0
-
-    lax.fori_loop(0, (total + tile - 1) // tile, per_tile, 0)
+def stacked_dot(left, refs, columns):
+    total, at = None, 0
+    for ref in refs:
+        depth = ref.shape[0]
+        part = jnp.dot(left[:, at : at + depth], ref[:, columns], preferred_element_type=F32)
+        total = part if total is None else total + part
+        at += depth
+    return total
+
+
+def split_bias(ref, hidden):
+    return ref[:, 0:hidden].astype(F32), ref[:, hidden:].astype(F32)
+
+
+def up_tile(x, refs, b1, h_ref, at):
+    hidden = refs[0].shape[1]
+    step = 256
+    for c in range(0, hidden, step):
+        pre = stacked_dot(x, refs, slice(c, c + step)) + b1[:, c : c + step]
+        act = 0.5 * pre * (1.0 + lax.erf(pre * F32(0.5**0.5)))
+        h_ref[at, c : c + step] = act.astype(BF16)
+
+
+def granules(e, count_ref, offset_ref):
+    last = count_ref.shape[0] - 1
+    return offset_ref[last, e] + count_ref[last, e]
+
+
+def tile_names(e, t, tile, list_ref):
+    return [list_ref[e, t * tile + k] for k in range(tile)]
+
+
+def put_rows(names, spare, y, out_ref):
+    for k, name in enumerate(names):
+        out_ref[jnp.where(name == spare, spare + 1, name)] = y[k * GRAN : (k + 1) * GRAN]
 
 
 def expert_kernel(bits, tile, spare, count_ref, offset_ref, list_ref, xs_ref, *refs):
-    count, experts = len(bits), expert_names(bits)
+    count = len(bits)
     w1_refs, w2_refs, b_refs = refs[:count], refs[count : 2 * count], refs[2 * count : 3 * count]
     out_ref, h_buf = refs[3 * count :]
-    last = count_ref.shape[0] - 1
-
-    def put(t, names, y):
-        for k, name in enumerate(names):
-            out_ref[jnp.where(name == spare, spare + 1, name)] = y[k * GRAN : (k + 1) * GRAN]
-
-    for i in range(count):
-        e = experts[i]
-        run_expert(e, tile, list_ref, offset_ref[last, e] + count_ref[last, e], b_refs[i], w1_refs[i], w2_refs[i], xs_ref, h_buf, put)
+    hidden = h_buf.shape[1]
+    for i, e in enumerate(expert_names(bits)):
+        b1, b2 = split_bias(b_refs[i], hidden)
+
+        def per_tile(t, _):
+            names = tile_names(e, t, tile, list_ref)
+            up_tile(jnp.concatenate([xs_ref[name] for name in names], axis=0), [w1_refs[i]], b1, h_buf, slice(None))
+            y = stacked_dot(h_buf[...], [w2_refs[i]], slice(None)) + b2
+            put_rows(names, spare, y.astype(BF16), out_ref)
+            return 0
+
+        lax.fori_loop(0, (granules(e, count_ref, offset_ref) + tile - 1) // tile, per_tile, 0)
+
+
+def up_kernel(bits, pieces, tile, most, count_ref, offset_ref, list_ref, xs_ref, *refs):
+    count = len(bits)
+    w1_refs = [refs[i * pieces : (i + 1) * pieces] for i in range(count)]
+    b_refs = refs[count * pieces : count * pieces + count]
+    h_ref = refs[count * pieces + count]
+    hidden = h_ref.shape[1]
+    for i, e in enumerate(expert_names(bits)):
+        b1, _ = split_bias(b_refs[i], hidden)
+
+        def per_tile(t, _):
+            names = tile_names(e, t, tile, list_ref)
+            at = pl.ds(pl.multiple_of((i * most + t * tile) * GRAN, tile * GRAN), tile * GRAN)
+            up_tile(jnp.concatenate([xs_ref[name] for name in names], axis=0), w1_refs[i], b1, h_ref, at)
+            return 0
+
+        lax.fori_loop(0, (granules(e, count_ref, offset_ref) + tile - 1) // tile, per_tile, 0)
+
+
+def down_kernel(bits, first, tile, most, spare, count_ref, offset_ref, list_ref, xs_ref, h_ref, *refs):
+    count = len(bits)
+    w2_refs, b_refs, out_ref = refs[:count], refs[count : 2 * count], refs[2 * count]
+    del xs_ref
+    for i, e in enumerate(expert_names(bits)):
+        _, b2 = split_bias(b_refs[i], h_ref.shape[1])
+
+        def per_tile(t, _):
+            names = tile_names(e, t, tile, list_ref)
+            at = pl.ds(pl.multiple_of(((first + i) * most + t * tile) * GRAN, tile * GRAN), tile * GRAN)
+            y = stacked_dot(h_ref[at, :], [w2_refs[i]], slice(None)) + b2
+            put_rows(names, spare, y.astype(BF16), out_ref)
+            return 0
+
+        lax.fori_loop(0, (granules(e, count_ref, offset_ref) + tile - 1) // tile, per_tile, 0)
+
+
+def compact_down(place, total, tile, most, window, w2_refs, b_ref, h_ref, y_ref):
+    width = y_ref.shape[2]
+    _, b2 = split_bias(b_ref, h_ref.shape[1])
+
+    def per_tile(t, _):
+        at = pl.ds(pl.multiple_of((place * most + t * tile) * GRAN, tile * GRAN), tile * GRAN)
+        y = stacked_dot(h_ref[at, :], w2_refs, slice(None)) + b2
+        y_ref[pl.ds(t * tile, tile)] = y.astype(BF16).reshape(tile, GRAN, width)
+        return 0
+
+    tiles = (total + tile - 1) // tile
+    lax.fori_loop(0, tiles, per_tile, 0)
+    y_ref[pl.ds(tiles * tile, window)] = jnp.zeros((window, GRAN, width), BF16)
+
+
+def half_kernel(bits, tile, most, window, count_ref, offset_ref, h_ref, *refs):
+    total = granules(expert_names(bits)[0], count_ref, offset_ref)
+    compact_down(0, total, tile, most, window, refs[:-2], refs[-2], h_ref, refs[-1])
 
 
 def final_kernel(
-    bits, tile, window, start_ref, count_ref, offset_ref, list_ref, pos_ref, gate_ref, ids_ref, xs_ref, part_ref, *refs
+    bits, tile, most, window, start_ref, count_ref, offset_ref, pos_ref, gate_ref, ids_ref, hot_ref, h_ref, part_ref, y_ref, *refs
 ):
     count, experts = len(bits), expert_names(bits)
-    w1_refs, w2_refs, b_refs = refs[:count], refs[count : 2 * count], refs[2 * count : 3 * count]
-    out_ref, h_buf, y_buf, o_buf, o_sem = refs[3 * count :]
+    out_ref, y_buf, o_buf, o_sem = refs[-4:]
+    y_refs = (y_ref, y_buf)
     blocks = start_ref.shape[0]
-    width = w1_refs[0].shape[0]
+    width = part_ref.shape[1]
     block_tok = BLOCK_ROWS * LANES
-    totals = [offset_ref[blocks - 1, experts[i]] + count_ref[blocks - 1, experts[i]] for i in range(count)]
-    for i in range(count):
-
-        def put(t, names, y):
-            y_buf[i, pl.ds(t * tile, tile)] = y.reshape(tile, GRAN, width)
-
-        run_expert(experts[i], tile, list_ref, totals[i], b_refs[i], w1_refs[i], w2_refs[i], xs_ref, h_buf, put)
-        y_buf[i, pl.ds((totals[i] + tile - 1) // tile * tile, window)] = jnp.zeros((window, GRAN, width), BF16)
-    lane = iota((LANES, window * GRAN), 1).astype(F32)
+    totals = [granules(e, count_ref, offset_ref) for e in experts]
+    compact_down(1, totals[1], tile, most, window, refs[:-5], refs[-5], h_ref, y_buf)
 
     def out_copy(pair, slot):
         rows = pl.ds(pl.multiple_of(pair * 2 * block_tok, 2 * block_tok), 2 * block_tok)
@@ -214,26 +281,14 @@
         slot = pair % 2
         row0 = pl.multiple_of(pair * 2 * BLOCK_ROWS, 2 * BLOCK_ROWS)
         rows8 = pl.ds(row0, 2 * BLOCK_ROWS)
-        pos8, gate8, ids8 = pos_ref[rows8, :], gate_ref[rows8, :], ids_ref[rows8, :]
-        gate_cols = jnp.transpose(gate8)
-        upper = iota(pos8.shape, 0) < BLOCK_ROWS
-        local = []
-        for i in range(count):
-            e = experts[i]
-            origin = jnp.where(upper, start_ref[2 * pair, e], start_ref[2 * pair + 1, e]) * GRAN
-            mine = (ids8 == e) & (pos8 >= 0)
-            local.append(jnp.transpose(jnp.where(mine, pos8 - origin, -1).astype(F32)))
-
-        def window_rows(sub, w, offsets):
-            ys = jnp.concatenate(
-                [y_buf[i, pl.ds(jnp.minimum(offsets[i] + w * window, totals[i]), window)].reshape(window * GRAN, width) for i in range(count)],
-                axis=0,
-            )
-            shift = jnp.asarray(w * (window * GRAN)).astype(F32)
-            hot = []
-            for r in range(sub * BLOCK_ROWS, (sub + 1) * BLOCK_ROWS):
-                hot.append(jnp.concatenate([(lane == local[i][:, r : r + 1] - shift).astype(F32).astype(BF16) for i in range(count)], axis=1))
-            return jnp.dot(jnp.concatenate(hot, axis=0), ys, preferred_element_type=F32)
+        gate_cols = jnp.transpose(gate_ref[rows8, :])
+
+        def window_rows(sub, w, hot):
+            ys = []
+            for i in range(count):
+                at = jnp.minimum(offset_ref[2 * pair + sub, experts[i]] + w * window, totals[i])
+                ys.append(y_refs[i][pl.ds(at, window)].reshape(window * GRAN, width))
+            return jnp.dot(hot, jnp.concatenate(ys, axis=0), preferred_element_type=F32)
 
         def scaled(sub, back, r):
             return back[r * LANES : (r + 1) * LANES] * gate_cols[:, sub * BLOCK_ROWS + r : sub * BLOCK_ROWS + r + 1]
@@ -244,9 +299,8 @@
 
         for sub in range(2):
             b = 2 * pair + sub
-            sizes = [count_ref[b, experts[i]] for i in range(count)]
-            starts = [offset_ref[b, experts[i]] for i in range(count)]
-            back = window_rows(sub, 0, starts)
+            hot = hot_ref[pl.ds(pl.multiple_of(b * block_tok, block_tok), block_tok), :]
+            back = window_rows(sub, 0, hot)
             for r in range(BLOCK_ROWS):
                 source = pl.ds(pl.multiple_of(b * block_tok + r * LANES, LANES), LANES)
                 at = slice((sub * BLOCK_ROWS + r) * LANES, (sub * BLOCK_ROWS + r + 1) * LANES)
@@ -254,14 +308,13 @@
 
         for sub in range(2):
             b = 2 * pair + sub
-            sizes = [count_ref[b, experts[i]] for i in range(count)]
-            starts = [offset_ref[b, experts[i]] for i in range(count)]
-            longest = sizes[0]
-            for size in sizes[1:]:
-                longest = jnp.maximum(longest, size)
+            longest = count_ref[b, experts[0]]
+            for e in experts[1:]:
+                longest = jnp.maximum(longest, count_ref[b, e])
 
             def more(w, _):
-                back = window_rows(sub, w, starts)
+                local = local_slots(experts, pos_ref[rows8, :], ids_ref[rows8, :], [start_ref[b, e] + w * window for e in experts])
+                back = window_rows(sub, w, hot_rows(local, window, sub))
                 for r in range(BLOCK_ROWS):
                     at = slice((sub * BLOCK_ROWS + r) * LANES, (sub * BLOCK_ROWS + r + 1) * LANES)
                     o_buf[slot, at, :] = (o_buf[slot, at, :].astype(F32) + scaled(sub, back, r)).astype(BF16)
@@ -276,13 +329,33 @@
         out_copy(0, slot).wait()
 
 
-def combine_kernel(slots, bits, ys_ref, pos_ref, gate_ref, ids_ref, out_ref):
+def local_slots(experts, pos8, ids8, firsts):
+    local = []
+    for e, first in zip(experts, firsts):
+        mine = (ids8 == e) & (pos8 >= 0)
+        local.append(jnp.transpose(jnp.where(mine, pos8 - first * GRAN, -1).astype(F32)))
+    return local
+
+
+def hot_rows(local, window, sub):
+    lane = iota((LANES, window * GRAN), 1).astype(F32)
+    hot = []
+    for r in range(sub * BLOCK_ROWS, (sub + 1) * BLOCK_ROWS):
+        hot.append(jnp.concatenate([(lane == cols[:, r : r + 1]).astype(F32).astype(BF16) for cols in local], axis=1))
+    return jnp.concatenate(hot, axis=0)
+
+
+def combine_kernel(slots, bits, window, start_ref, ys_ref, pos_ref, gate_ref, ids_ref, out_ref, hot_ref):
     experts = expert_names(bits)
     rows = pos_ref.shape[0]
     pos_cols = jnp.transpose(pos_ref[...].astype(F32))
     later = (ids_ref[...] == experts[0]) | (ids_ref[...] == experts[1])
     gate_cols = jnp.transpose(jnp.where(later, 0.0, gate_ref[...]))
     grans = slots // GRAN
+    upper = iota(pos_ref.shape, 0) < BLOCK_ROWS
+    pair = pl.program_id(0)
+    firsts = [jnp.where(upper, start_ref[2 * pair, e], start_ref[2 * pair + 1, e]) for e in experts]
+    local = local_slots(experts, pos_ref[...], ids_ref[...], firsts)
     slot_iota = iota((LANES, slots), 1).astype(F32)
     for sub in range(rows // BLOCK_ROWS):
         row0 = sub * BLOCK_ROWS
@@ -293,6 +366,8 @@
             at = pl.ds(pl.multiple_of(((pl.program_id(0) * rows) + row0 + r) * LANES, LANES), LANES)
             scaled = back[r * LANES : (r + 1) * LANES] * gate_cols[:, row0 + r : row0 + r + 1]
             out_ref[at, :] = scaled.astype(BF16)
+        block = pl.ds(pl.multiple_of((2 * pair + sub) * BLOCK_ROWS * LANES, BLOCK_ROWS * LANES), BLOCK_ROWS * LANES)
+        hot_ref[block, :] = hot_rows(local, window, sub)
 
 
 def vmem():
@@ -326,8 +401,8 @@
         span = slots // GRAN
 
         first, second = w_in[0], w_out[0]
-        x_first, y_second = swap(first, 2), swap(second, 4)
-        x_second, y_first = swap(second, 2), swap(first, 4)
+        x_first, y_first = swap(first, 2), swap(first, 4)
+        x_second, y_second = swap(second, 2), swap(second, 4)
         c_first, c_second = swap(first, 1), swap(second, 1)
         own_bias = jnp.concatenate([b_in, b_out], axis=1)
         bias = [own_bias] + [swap(own_bias, bit) for bit in range(1, num_experts)]
@@ -371,67 +446,109 @@
             cost_estimate=pl.CostEstimate(flops=9 * 10**9, bytes_accessed=14 * 10**6, transcendentals=0),
             compiler_params=pltpu.CompilerParams(vmem_limit_bytes=12 * 2**20),
             name="dispatch",
-        )(value_a11.reshape(1, 1), ids, order, w_route, expert_keys, tokens[0])
-
-        most = -(-(capacity + blocks * (GRAN - 1)) // (16 * GRAN)) * 16
-        tile, window = 16, 8
+        )(value_a11.reshape(1, 1), *[pltpu.with_memory_space_constraint(array, pltpu.HBM) for array in (ids, order, w_route, expert_keys, tokens[0])])
+
+        most = -(-(capacity + blocks * (GRAN - 1)) // (32 * GRAN)) * 32
+        tile, window = 32, 8
         held = lambda array: pltpu.with_memory_space_constraint(array, pltpu.VMEM)
 
-        def experts(bits, xs, firsts, seconds):
+        spare = blocks * span
+        limit = pltpu.CompilerParams(vmem_limit_bytes=8 * 2**20)
+        tables = (counts, offsets, lists)
+
+        def cost(flops):
+            return pl.CostEstimate(flops=flops, bytes_accessed=10**6, transcendentals=0)
+
+        def up(bits, xs, firsts):
             n = len(bits)
+            pieces = len(firsts[0])
             return pl.pallas_call(
-                functools.partial(expert_kernel, bits, tile, blocks * span),
+                functools.partial(up_kernel, bits, pieces, tile, most),
+                out_shape=pltpu.VMEM((n * most * GRAN, hidden), BF16),
+                in_specs=[smem()] * 3 + [vmem()] * (1 + n * pieces + n),
+                out_specs=vmem(),
+                cost_estimate=cost(2 * n * 10**9),
+                compiler_params=limit,
+            )(*tables, held(xs), *[held(piece) for expert in firsts for piece in expert], *[bias[bit] for bit in bits])
+
+        def down(bits, place, xs, h, seconds):
+            return pl.pallas_call(
+                functools.partial(down_kernel, bits, place, tile, most, spare),
                 out_shape=pltpu.VMEM(xs.shape, BF16),
-                in_specs=[smem()] * 3 + [vmem()] * (1 + 3 * n),
+                in_specs=[smem()] * 3 + [vmem()] * (2 + 2 * len(bits)),
                 out_specs=vmem(),
-                scratch_shapes=[pltpu.VMEM((tile * GRAN, hidden), BF16)],
                 input_output_aliases={3: 0},
-                cost_estimate=pl.CostEstimate(flops=3 * n * 10**9, bytes_accessed=4 * n * 10**6, transcendentals=0),
-                compiler_params=pltpu.CompilerParams(vmem_limit_bytes=8 * 2**20),
-            )(counts, offsets, lists, held(xs), *map(held, firsts), *map(held, seconds), *[bias[bit] for bit in bits])
-
-        xs = experts((0, 1), xs, (first, c_first), (second, c_second))
-        x_first, y_second, xs = lax.optimization_barrier((x_first, y_second, xs))
-        d_first, d_second = swap(x_first, 4), swap(y_second, 2)
-        cx_first, cy_second = swap(x_first, 1), swap(y_second, 1)
-        cx_second, cy_first = swap(x_second, 1), swap(y_first, 1)
-        xs = experts((2, 3, 4, 5), xs, (x_first, cx_first, y_first, cy_first), (x_second, cx_second, y_second, cy_second))
-        part = pl.pallas_call(
-            functools.partial(combine_kernel, slots, (6, 7)),
-            out_shape=pltpu.VMEM((tok_dev, width), BF16),
+                cost_estimate=cost(2 * len(bits) * 10**9),
+                compiler_params=limit,
+            )(*tables, held(xs), held(h), *map(held, seconds), *[bias[bit] for bit in bits])
+
+        xs = pl.pallas_call(
+            functools.partial(expert_kernel, (0, 1), tile, spare),
+            out_shape=pltpu.VMEM(xs.shape, BF16),
+            in_specs=[smem()] * 3 + [vmem()] * 7,
+            out_specs=vmem(),
+            scratch_shapes=[pltpu.VMEM((tile * GRAN, hidden), BF16)],
+            input_output_aliases={3: 0},
+            cost_estimate=cost(6 * 10**9),
+            compiler_params=limit,
+            name="experts0",
+        )(*tables, held(xs), held(first), held(c_first), held(second), held(c_second), bias[0], bias[1])
+
+        x_first, y_first, xs = lax.optimization_barrier((x_first, y_first, xs))
+        cut = width - LANES
+        d_top, d_low = swap(x_first[:cut], 4), swap(y_first[cut:], 2)
+        cx_first, cy_first = swap(x_first, 1), swap(y_first, 1)
+        h = up((2, 4, 3, 5), xs, ((x_first,), (y_first,), (cx_first,), (cy_first,)))
+        x_second, y_second, h = lax.optimization_barrier((x_second, y_second, h))
+        edge = hidden // 3
+        e_top, e_low = swap(x_second[:edge], 4), swap(y_second[edge:], 2)
+        cx_second, cy_second = swap(x_second, 1), swap(y_second, 1)
+        xs = down((2, 4), 0, xs, h, (x_second, y_second))
+        xs = down((3, 5), 2, xs, h, (cx_second, cy_second))
+        part, hot = pl.pallas_call(
+            functools.partial(combine_kernel, slots, (6, 7), window),
+            out_shape=(pltpu.VMEM((tok_dev, width), BF16), pltpu.VMEM((tok_dev, 2 * window * GRAN), BF16)),
             grid=(rows // unit,),
             in_specs=[
+                smem(),
                 vmem(),
                 pl.BlockSpec((unit, LANES), lambda i: (i, 0)),
                 pl.BlockSpec((unit, LANES), lambda i: (i, 0)),
                 pl.BlockSpec((unit, LANES), lambda i: (i, 0)),
             ],
+            out_specs=(vmem(), vmem()),
+            cost_estimate=cost(5 * 10**9),
+            compiler_params=limit,
+            name="combine",
+        )(starts, held(xs), pos, gate, ids)
+        d_top, d_low, part, hot = lax.optimization_barrier((d_top, d_low, part, hot))
+        firsts = ((d_top, d_low), (swap(d_top, 1), swap(d_low, 1)))
+        h = up((6, 7), xs, firsts)
+        e_top, e_low, h = lax.optimization_barrier((e_top, e_low, h))
+        ce_top, ce_low = swap(e_top, 1), swap(e_low, 1)
+        y = pl.pallas_call(
+            functools.partial(half_kernel, (6, 7), tile, most, window),
+            out_shape=pltpu.VMEM((most + window, GRAN, width), BF16),
+            in_specs=[smem()] * 2 + [vmem()] * 4,
             out_specs=vmem(),
-            cost_estimate=pl.CostEstimate(flops=5 * 10**9, bytes_accessed=14 * 10**6, transcendentals=0),
-            compiler_params=pltpu.CompilerParams(vmem_limit_bytes=8 * 2**20),
-            name="combine",
-        )(held(xs), pos, gate, ids)
-        d_first, d_second, part = lax.optimization_barrier((d_first, d_second, part))
-        firsts = (d_first, swap(d_first, 1))
-        seconds = (d_second, swap(d_second, 1))
+            cost_estimate=cost(2 * 10**9),
+            compiler_params=limit,
+            name="half",
+        )(counts, offsets, held(h), held(e_top), held(e_low), bias[6])
         out = pl.pallas_call(
-            functools.partial(final_kernel, (6, 7), tile, window),
+            functools.partial(final_kernel, (6, 7), tile, most, window),
             out_shape=jax.ShapeDtypeStruct((tok_dev, width), BF16),
-            in_specs=[smem()] * 4 + [vmem()] * (5 + 6),
+            in_specs=[smem()] * 3 + [vmem()] * (7 + 3),
             out_specs=hbm(),
             scratch_shapes=[
-                pltpu.VMEM((tile * GRAN, hidden), BF16),
-                pltpu.VMEM((2, most + tile, GRAN, width), BF16),
+                pltpu.VMEM((most + window, GRAN, width), BF16),
                 pltpu.VMEM((2, 2 * BLOCK_ROWS * LANES, width), BF16),
                 pltpu.SemaphoreType.DMA((2,)),
             ],
-            cost_estimate=pl.CostEstimate(flops=7 * 10**9, bytes_accessed=8 * 10**6, transcendentals=0),
-            compiler_params=pltpu.CompilerParams(vmem_limit_bytes=12 * 2**20),
+            cost_estimate=cost(5 * 10**9),
+            compiler_params=limit,
             name="final",
-        )(
-            starts, counts, offsets, lists, pos, gate, ids, held(xs), held(part),
-            *map(held, firsts), *map(held, seconds), bias[6], bias[7],
-        )
+        )(starts, counts, offsets, pos, gate, ids, held(hot), held(h), held(part), held(y), held(ce_top), held(ce_low), bias[7])
         return out[None]
 
     return jax.shard_map(

time: 128 us -> 153 us (1.20)
  waiting for transfers between devices: 31.8 us -> 52.1 us
  starting transfers between devices: 15.2 us -> 21 us
  local copies, waits for them, and re-layouts: 7.31 us -> 1.61 us
  Pallas kernels: 71.2 us -> 76.4 us
    ppermute x21 -> x25, waiting for transfers between devices: 31.8 us -> 52.1 us  [swap(): lax.ppermute(value, EXPERT_AXES, [(e, e ^ bit) for e in range(num_experts)])]
    unnamed x17 -> x7, local copies, waits for them, and re-layouts: 6.62 us -> 0.72 us
    ppermute x21 -> x25, starting transfers between devices: 15.2 us -> 21 us  [swap(): lax.ppermute(value, EXPERT_AXES, [(e, e ^ bit) for e in range(num_experts)])]
    pallas_call x4 -> x8, Pallas kernels: 55.7 us -> 59.4 us  [the longest x2 16.2 us: up(): pl.pallas_call(functools.partial(up_kernel, bits, pieces, tile, most), ou...]
  transfers between devices with their start and end apart: 21 -> 25, of which waited for: 7 -> 6; matrix products, arithmetic and copies ran while one was open for 1% -> 1% of each run, Pallas kernels for 43% -> 44%
where the time goes in v2:
time: 153 us; the launch traced here: 152 us
  Pallas kernels  76.4 us (50%)
  waiting for transfers between devices  52.1 us (34%)
  starting transfers between devices  21 us (14%)
  local copies, waits for them, and re-layouts  1.61 us (1%)
    ppermute x25, waiting for transfers between devices, swap(): lax.ppermute(value, EXPERT_AXES, [(e, e ^ bit) for e in range(num_experts)])  52.1 us
    ppermute x25, starting transfers between devices, swap(): lax.ppermute(value, EXPERT_AXES, [(e, e ^ bit) for e in range(num_experts)])  21 us
    pallas_call x1, Pallas kernels, inner_step(): pl.pallas_call(functools.partial(dispatch_kernel, router, num_experts, ca...  17 us
    pallas_call x2, Pallas kernels, up(): pl.pallas_call(functools.partial(up_kernel, bits, pieces, tile, most), ou...  16.2 us
    pallas_call x1, Pallas kernels, inner_step(): pl.pallas_call(functools.partial(expert_kernel, (0, 1), tile, spare), out...  10.8 us
    pallas_call x2, Pallas kernels, down(): pl.pallas_call(functools.partial(down_kernel, bits, place, tile, most, sp...  10.8 us
    pallas_call x1, Pallas kernels, inner_step(): pl.pallas_call(functools.partial(combine_kernel, slots, (6, 7), window),...  9.71 us
    pallas_call x1, Pallas kernels, inner_step(): pl.pallas_call(functools.partial(final_kernel, (6, 7), tile, most, window...  9.05 us
  transfers between devices with their start and end apart: 25, of which 6 were waited for; matrix products, arithmetic and copies ran while one was open for 1% of the time, Pallas kernels for 44%

profile of v2, /device:TPU:0, one launch (start us, length us, event | category | flops | bytes accessed | tf_op | source)
XLA Modules:
  0.0 152.3 jit_solution(16488724666593002788)
XLA Ops:
  0.0 0.8 collective-permute-start.2
  0.8 2.5 %collective-permute-start.1 = (bf16[384,1536]{1,0:T(8,128)(2,1)}, bf16[384,1536]{1,0:T(8,128)(2,1)S(1)}, u32[]{:S(2)}, u32[]{:S(2)}) collective-permute-start(bf16[384,1536]{1,0:T(8,128)(2,1)} %bitcast.12), channel_id=1, source_target_pairs={{0,4},{1,5},{2,6},{3,7},{4,0},{5,1},{6,2},{7,3}} | collective-permute-start | bytes 3538952 | tf_op jit(solution)/shard_map/ppermute | solution.py:391
  3.3 1.5 collective-permute-start
  7.4 17.0 %dispatch.1 = (s32[64,128]{1,0:T(8,128)S(1)}, s32[16,128]{1,0:T(8,128)S(1)}, s32[16,128]{1,0:T(8,128)S(1)}, s32[16,128]{1,0:T(8,128)S(1)}, s32[8,128]{1,0:T(8,12...) custom-call(f32[1,1]{1,0:T(1,128)} %bitcast.7.tau_ref, s32[64,128]{1,0:T(8,128)} %bitcast.8, ...), custom_call_target="tpu_custom_call" | custom-call | flops 8999999488 | bytes 14000000 | tf_op jit(solution)/shard_map/dispatch/pallas_call | solution.py:416
  24.5 10.8 %experts0.1.xs_ref = bf16[648,16,384]{2,1,0:T(8,128)(2,1)S(1)} custom-call(s32[16,128]{1,0:T(8,128)S(1)} %get-tuple-element.28.count_ref, s32[16,128]{1,0:T(8,128)S(1)} %get-tuple-element.29.offset_ref, s32[8,128]{1,0:T(8,128)S(1)} %get-tuple-element.32.list_ref, bf16[648,16,384]{2,1,0:T(8,128)(2,1)S(1)} %get-tuple-element.33.xs_ref, ...), custom_call_target="tpu_custom_call", output_to_operand_aliasing={{}: (3, {})} | custom-call | flops 6000000000 | bytes 1000000 | tf_op jit(solution)/shard_map/experts0/pallas_call | solution.py:485
  35.9 2.4 %collective-permute-start.7 = (bf16[1536,384]{1,0:T(8,128)(2,1)S(1)}, bf16[1536,384]{1,0:T(8,128)(2,1)S(1)}, u32[]{:S(2)}, u32[]{:S(2)}) collective-permute-start(bf16[1536,384]{1,0:T(8,128)(2,1)S(1)} %bitcast.18), channel_id=1, source_target_pairs={{0,2},{1,3},{2,0},{3,1},{4,6},{5,7},{6,4},{7,5}} | collective-permute-start | bytes 3538952 | tf_op jit(solution)/shard_map/ppermute | solution.py:391
  38.3 1.1 collective-permute-start.14
  39.3 23.7 %collective-permute-done.14.refs_7_.refs_3_ = bf16[1,1920]{1,0:T(2,128)(2,1)S(1)} collective-permute-done((bf16[1,1920]{1,0:T(2,128)(2,1)S(1)}, bf16[1,1920]{1,0:T(2,128)(2,1)S(1)}, u32[]{:S(2)}, u32[]{:S(2)}) %collective-permute-start.14) | collective-permute-done | bytes 3872 | tf_op jit(solution)/shard_map/ppermute | solution.py:391
  63.0 2.9 %collective-permute-start.13 = (bf16[1,1920]{1,0:T(2,128)(2,1)S(1)}, bf16[1,1920]{1,0:T(2,128)(2,1)S(1)}, u32[]{:S(2)}, u32[]{:S(2)}) collective-permute-start(bf16[1,1920]{1,0:T(2,128)(2,1)S(1)} %constant_dynamic-update-slice_fusion.refs_4_), channel_id=1, source_target_pairs={{0,3},{1,2},{2,1},{3,0},{4,7},{5,6},{6,5},{7,4}} | collective-permute-start | bytes 11528 | tf_op jit(solution)/shard_map/ppermute | solution.py:391
  66.0 1.4 collective-permute-done.13.refs_6_.refs_2_
  67.7 3.3 %collective-permute-done.12.refs_5_.refs_3_ = bf16[1,1920]{1,0:T(2,128)(2,1)S(1)} collective-permute-done((bf16[1,1920]{1,0:T(2,128)(2,1)S(1)}, bf16[1,1920]{1,0:T(2,128)(2,1)S(1)}, u32[]{:S(2)}, u32[]{:S(2)}) %collective-permute-start.12) | collective-permute-done | bytes 3872 | tf_op jit(solution)/shard_map/ppermute | solution.py:391
  71.0 1.2 collective-permute-start.11
  72.2 2.4 %collective-permute-done.11.refs_4_.refs_2_ = bf16[1,1920]{1,0:T(2,128)(2,1)S(1)} collective-permute-done((bf16[1,1920]{1,0:T(2,128)(2,1)S(1)}, bf16[1,1920]{1,0:T(2,128)(2,1)S(1)}, u32[]{:S(2)}, u32[]{:S(2)}) %collective-permute-start.11) | collective-permute-done | bytes 3872 | tf_op jit(solution)/shard_map/ppermute | solution.py:391
  74.6 10.9 %shard_map.100.h_ref = bf16[6144,1536]{1,0:T(8,128)(2,1)S(1)} custom-call(s32[16,128]{1,0:T(8,128)S(1)} %get-tuple-element.28.count_ref, s32[16,128]{1,0:T(8,128)S(1)} %get-tuple-element.29.offset_ref, s32[8,128]{1,0:T(8,128)S(1)} %get-tuple-element.32.list_ref, bf16[648,16,384]{2,1,0:T(8,128)(2,1)S(1)} %experts0.1.xs_ref, ...), custom_call_target="tpu_custom_call" | custom-call | flops 8000000000 | bytes 1000000 | tf_op jit(solution)/shard_map/pallas_call | solution.py:465
  87.7 5.8 %shard_map.101.xs_ref = bf16[648,16,384]{2,1,0:T(8,128)(2,1)S(1)} custom-call(s32[16,128]{1,0:T(8,128)S(1)} %get-tuple-element.28.count_ref, s32[16,128]{1,0:T(8,128)S(1)} %get-tuple-element.29.offset_ref, s32[8,128]{1,0:T(8,128)S(1)} %get-tuple-element.32.list_ref, bf16[648,16,384]{2,1,0:T(8,128)(2,1)S(1)} %experts0.1.xs_ref, ...), custom_call_target="tpu_custom_call", output_to_operand_aliasing={{}: (3, {})} | custom-call | flops 4000000000 | bytes 1000000 | tf_op jit(solution)/shard_map/pallas_call | solution.py:475
  93.5 5.0 %shard_map.102.ys_ref.xs_ref = bf16[648,16,384]{2,1,0:T(8,128)(2,1)S(1)} custom-call(s32[16,128]{1,0:T(8,128)S(1)} %get-tuple-element.28.count_ref, s32[16,128]{1,0:T(8,128)S(1)} %get-tuple-element.29.offset_ref, s32[8,128]{1,0:T(8,128)S(1)} %get-tuple-element.32.list_ref, ...), custom_call_target="tpu_custom_call", output_to_operand_aliasing={{}: (3, {})} | custom-call | flops 4000000000 | bytes 1000000 | tf_op jit(solution)/shard_map/pallas_call | solution.py:475
  98.5 9.7 %combine.1 = (bf16[8192,384]{1,0:T(8,128)(2,1)S(1)}, bf16[8192,256]{1,0:T(8,128)(2,1)S(1)}) custom-call(s32[16,128]{1,0:T(8,128)S(1)} %get-tuple-element.27.start_ref, bf16[648,16,384]{2,1,0:T(8,128)(2,1)S(1)} %shard_map.102.ys_ref.xs_ref, s32[64,128]{1,0:T(8,128)S(1)} %get-tuple-element.30.pos_ref, f32[64,128]{1,0:T(8,128)S(1)} %get-tuple-element.31.gate_ref, ...), custom_call_target="tpu_custom_call" | custom-call | flops 5000000000 | bytes 1000000 | tf_op jit(solution)/shard_map/combine/pallas_call | solution.py:508
  108.4 2.5 %collective-permute-start.18 = (bf16[1024,384]{1,0:T(8,128)(2,1)S(1)}, bf16[1024,384]{1,0:T(8,128)(2,1)S(1)}, u32[]{:S(2)}, u32[]{:S(2)}) collective-permute-start(bf16[1024,384]{1,0:T(8,128)(2,1)S(1)} %slice.15), channel_id=1, source_target_pairs={{0,2},{1,3},{2,0},{3,1},{4,6},{5,7},{6,4},{7,5}} | collective-permute-start | bytes 2359304 | tf_op jit(solution)/shard_map/ppermute | solution.py:391
  111.5 0.9 collective-permute-start.22
  112.4 17.4 %collective-permute-done.22.refs_5_.refs_2_ = bf16[1,1920]{1,0:T(2,128)(2,1)S(1)} collective-permute-done((bf16[1,1920]{1,0:T(2,128)(2,1)S(1)}, bf16[1,1920]{1,0:T(2,128)(2,1)S(1)}, u32[]{:S(2)}, u32[]{:S(2)}) %collective-permute-start.22) | collective-permute-done | bytes 3872 | tf_op jit(solution)/shard_map/ppermute | solution.py:391
  130.4 3.9 %collective-permute-done.21.refs_4_.refs_2_ = bf16[1,1920]{1,0:T(2,128)(2,1)S(1)} collective-permute-done((bf16[1,1920]{1,0:T(2,128)(2,1)S(1)}, bf16[1,1920]{1,0:T(2,128)(2,1)S(1)}, u32[]{:S(2)}, u32[]{:S(2)}) %collective-permute-start.21) | collective-permute-done | bytes 3872 | tf_op jit(solution)/shard_map/ppermute | solution.py:391
  134.3 5.3 %shard_map.103.h_ref = bf16[3072,1536]{1,0:T(8,128)(2,1)S(1)} custom-call(s32[16,128]{1,0:T(8,128)S(1)} %get-tuple-element.28.count_ref, s32[16,128]{1,0:T(8,128)S(1)} %get-tuple-element.29.offset_ref, s32[8,128]{1,0:T(8,128)S(1)} %get-tuple-element.32.list_ref, bf16[648,16,384]{2,1,0:T(8,128)(2,1)S(1)} %shard_map.102.ys_ref.xs_ref, ...), custom_call_target="tpu_custom_call" | custom-call | flops 4000000000 | bytes 1000000 | tf_op jit(solution)/shard_map/pallas_call | solution.py:465
  140.2 2.8 %half.1.y_ref = bf16[104,16,384]{2,1,0:T(8,128)(2,1)S(1)} custom-call(s32[16,128]{1,0:T(8,128)S(1)} %get-tuple-element.28.count_ref, s32[16,128]{1,0:T(8,128)S(1)} %get-tuple-element.29.offset_ref, bf16[3072,1536]{1,0:T(8,128)(2,1)S(1)} %shard_map.103.h_ref, bf16[512,384]{1,0:T(8,128)(2,1)S(1)} %collective-permute-done.17.refs_0_, ...), custom_call_target="tpu_custom_call" | custom-call | flops 2000000000 | bytes 1000000 | tf_op jit(solution)/shard_map/half/pallas_call | solution.py:529
  143.1 9.0 %final.1 = bf16[8192,384]{1,0:T(8,128)(2,1)} custom-call(s32[16,128]{1,0:T(8,128)S(1)} %get-tuple-element.27.start_ref, s32[16,128]{1,0:T(8,128)S(1)} %get-tuple-element.28.count_ref, s32[16,128]{1,0:T(8,128)S(1)} %get-tuple-element.29.offset_ref, s32[64,128]{1,0:T(8,128)S(1)} %get-tuple-element.30.pos_ref, f32[64,128]{1,0:T(8,128)S(1)} %get-tuple-element.31.gate_ref, ...), custom_call_target="tpu_custom_call" | custom-call | flops 5000000000 | bytes 1000000 | tf_op jit(solution)/shard_map/final/pallas_call | solution.py:538
  (47 shorter events, 6.9 us)
Async XLA Ops:
  0.0 24.4 %collective-permute-start.2 = (bf16[384,1536]{1,0:T(8,128)(2,1)}, bf16[384,1536]{1,0:T(8,128)(2,1)}, u32[]{:S(2)}, u32[]{:S(2)}) collective-permute-start(bf16[384,1536]{1,0:T(8,128)(2,1)} %bitcast.11), channel_id=1, source_target_pairs={{0,1},{1,0},{2,3},{3,2},{4,5},{5,4},{6,7},{7,6}} | collective-permute-start | bytes 3538952 | tf_op jit(solution)/shard_map/ppermute | solution.py:391
  0.8 34.5 %collective-permute-start.1 = (bf16[384,1536]{1,0:T(8,128)(2,1)}, bf16[384,1536]{1,0:T(8,128)(2,1)S(1)}, u32[]{:S(2)}, u32[]{:S(2)}) collective-permute-start(bf16[384,1536]{1,0:T(8,128)(2,1)} %bitcast.12), channel_id=1, source_target_pairs={{0,4},{1,5},{2,6},{3,7},{4,0},{5,1},{6,2},{7,3}} | collective-permute-start | bytes 3538952 | tf_op jit(solution)/shard_map/ppermute | solution.py:391
  3.3 32.0 %collective-permute-start = (bf16[384,1536]{1,0:T(8,128)(2,1)}, bf16[384,1536]{1,0:T(8,128)(2,1)S(1)}, u32[]{:S(2)}, u32[]{:S(2)}) collective-permute-start(bf16[384,1536]{1,0:T(8,128)(2,1)} %bitcast.13), channel_id=1, source_target_pairs={{0,2},{1,3},{2,0},{3,1},{4,6},{5,7},{6,4},{7,5}} | collective-permute-start | bytes 3538952 | tf_op jit(solution)/shard_map/ppermute | solution.py:391
  4.8 19.6 %collective-permute-start.3 = (bf16[1536,384]{1,0:T(8,128)(2,1)}, bf16[1536,384]{1,0:T(8,128)(2,1)}, u32[]{:S(2)}, u32[]{:S(2)}) collective-permute-start(bf16[1536,384]{1,0:T(8,128)(2,1)} %bitcast.15), channel_id=1, source_target_pairs={{0,1},{1,0},{2,3},{3,2},{4,5},{5,4},{6,7},{7,6}} | collective-permute-start | bytes 3538952 | tf_op jit(solution)/shard_map/ppermute | solution.py:391
  6.2 18.2 %collective-permute-start.4 = (bf16[1,1920]{1,0:T(2,128)(2,1)S(1)}, bf16[1,1920]{1,0:T(2,128)(2,1)S(1)}, u32[]{:S(2)}, u32[]{:S(2)}) collective-permute-start(bf16[1,1920]{1,0:T(2,128)(2,1)S(1)} %constant_dynamic-update-slice_fusion.refs_4_), channel_id=1, source_target_pairs={{0,1},{1,0},{2,3},{3,2},{4,5},{5,4},{6,7},{7,6}} | collective-permute-start | bytes 11528 | tf_op jit(solution)/shard_map/ppermute | solution.py:391
  35.3 39.3 %collective-permute-start.9 = (bf16[384,1536]{1,0:T(8,128)(2,1)S(1)}, bf16[384,1536]{1,0:T(8,128)(2,1)S(1)}, u32[]{:S(2)}, u32[]{:S(2)}) collective-permute-start(bf16[384,1536]{1,0:T(8,128)(2,1)S(1)} %collective-permute-done.refs_0_), channel_id=1, source_target_pairs={{0,1},{1,0},{2,3},{3,2},{4,5},{5,4},{6,7},{7,6}} | collective-permute-start | bytes 3538952 | tf_op jit(solution)/shard_map/ppermute | solution.py:391
  35.4 39.2 %collective-permute-start.10 = (bf16[384,1536]{1,0:T(8,128)(2,1)S(1)}, bf16[384,1536]{1,0:T(8,128)(2,1)S(1)}, u32[]{:S(2)}, u32[]{:S(2)}) collective-permute-start(bf16[384,1536]{1,0:T(8,128)(2,1)S(1)} %collective-permute-done.1.refs_1_), channel_id=1, source_target_pairs={{0,1},{1,0},{2,3},{3,2},{4,5},{5,4},{6,7},{7,6}} | collective-permute-start | bytes 3538952 | tf_op jit(solution)/shard_map/ppermute | solution.py:391
  35.9 49.7 %collective-permute-start.8 = (bf16[1536,384]{1,0:T(8,128)(2,1)S(1)}, bf16[1536,384]{1,0:T(8,128)(2,1)S(1)}, u32[]{:S(2)}, u32[]{:S(2)}) collective-permute-start(bf16[1536,384]{1,0:T(8,128)(2,1)S(1)} %bitcast.17), channel_id=1, source_target_pairs={{0,4},{1,5},{2,6},{3,7},{4,0},{5,1},{6,2},{7,3}} | collective-permute-start | bytes 3538952 | tf_op jit(solution)/shard_map/ppermute | solution.py:391
  35.9 49.7 %collective-permute-start.7 = (bf16[1536,384]{1,0:T(8,128)(2,1)S(1)}, bf16[1536,384]{1,0:T(8,128)(2,1)S(1)}, u32[]{:S(2)}, u32[]{:S(2)}) collective-permute-start(bf16[1536,384]{1,0:T(8,128)(2,1)S(1)} %bitcast.18), channel_id=1, source_target_pairs={{0,2},{1,3},{2,0},{3,1},{4,6},{5,7},{6,4},{7,5}} | collective-permute-start | bytes 3538952 | tf_op jit(solution)/shard_map/ppermute | solution.py:391
  38.3 24.8 %collective-permute-start.14 = (bf16[1,1920]{1,0:T(2,128)(2,1)S(1)}, bf16[1,1920]{1,0:T(2,128)(2,1)S(1)}, u32[]{:S(2)}, u32[]{:S(2)}) collective-permute-start(bf16[1,1920]{1,0:T(2,128)(2,1)S(1)} %constant_dynamic-update-slice_fusion.refs_4_), channel_id=1, source_target_pairs={{0,5},{1,4},{2,7},{3,6},{4,1},{5,0},{6,3},{7,2}} | collective-permute-start | bytes 11528 | tf_op jit(solution)/shard_map/ppermute | solution.py:391
  63.0 4.3 %collective-permute-start.13 = (bf16[1,1920]{1,0:T(2,128)(2,1)S(1)}, bf16[1,1920]{1,0:T(2,128)(2,1)S(1)}, u32[]{:S(2)}, u32[]{:S(2)}) collective-permute-start(bf16[1,1920]{1,0:T(2,128)(2,1)S(1)} %constant_dynamic-update-slice_fusion.refs_4_), channel_id=1, source_target_pairs={{0,3},{1,2},{2,1},{3,0},{4,7},{5,6},{6,5},{7,4}} | collective-permute-start | bytes 11528 | tf_op jit(solution)/shard_map/ppermute | solution.py:391
  67.3 3.6 %collective-permute-start.12 = (bf16[1,1920]{1,0:T(2,128)(2,1)S(1)}, bf16[1,1920]{1,0:T(2,128)(2,1)S(1)}, u32[]{:S(2)}, u32[]{:S(2)}) collective-permute-start(bf16[1,1920]{1,0:T(2,128)(2,1)S(1)} %constant_dynamic-update-slice_fusion.refs_4_), channel_id=1, source_target_pairs={{0,4},{1,5},{2,6},{3,7},{4,0},{5,1},{6,2},{7,3}} | collective-permute-start | bytes 11528 | tf_op jit(solution)/shard_map/ppermute | solution.py:391
  71.0 3.6 %collective-permute-start.11 = (bf16[1,1920]{1,0:T(2,128)(2,1)S(1)}, bf16[1,1920]{1,0:T(2,128)(2,1)S(1)}, u32[]{:S(2)}, u32[]{:S(2)}) collective-permute-start(bf16[1,1920]{1,0:T(2,128)(2,1)S(1)} %constant_dynamic-update-slice_fusion.refs_4_), channel_id=1, source_target_pairs={{0,2},{1,3},{2,0},{3,1},{4,6},{5,7},{6,4},{7,5}} | collective-permute-start | bytes 11528 | tf_op jit(solution)/shard_map/ppermute | solution.py:391
  85.5 8.0 %collective-permute-start.15 = (bf16[1536,384]{1,0:T(8,128)(2,1)S(1)}, bf16[1536,384]{1,0:T(8,128)(2,1)S(1)}, u32[]{:S(2)}, u32[]{:S(2)}) collective-permute-start(bf16[1536,384]{1,0:T(8,128)(2,1)S(1)} %collective-permute-done.7.refs_0_), channel_id=1, source_target_pairs={{0,1},{1,0},{2,3},{3,2},{4,5},{5,4},{6,7},{7,6}} | collective-permute-start | bytes 3538952 | tf_op jit(solution)/shard_map/ppermute | solution.py:391
  85.6 7.9 %collective-permute-start.16 = (bf16[1536,384]{1,0:T(8,128)(2,1)S(1)}, bf16[1536,384]{1,0:T(8,128)(2,1)S(1)}, u32[]{:S(2)}, u32[]{:S(2)}) collective-permute-start(bf16[1536,384]{1,0:T(8,128)(2,1)S(1)} %collective-permute-done.8.refs_1_), channel_id=1, source_target_pairs={{0,1},{1,0},{2,3},{3,2},{4,5},{5,4},{6,7},{7,6}} | collective-permute-start | bytes 3538952 | tf_op jit(solution)/shard_map/ppermute | solution.py:391
  86.2 22.1 %collective-permute-start.6 = (bf16[128,1536]{1,0:T(8,128)(2,1)S(1)}, bf16[128,1536]{1,0:T(8,128)(2,1)S(1)}, u32[]{:S(2)}, u32[]{:S(2)}) collective-permute-start(bf16[128,1536]{1,0:T(8,128)(2,1)S(1)} %slice.13), channel_id=1, source_target_pairs={{0,2},{1,3},{2,0},{3,1},{4,6},{5,7},{6,4},{7,5}} | collective-permute-start | bytes 1179656 | tf_op jit(solution)/shard_map/ppermute | solution.py:391
  87.0 21.3 %collective-permute-start.5 = (bf16[256,1536]{1,0:T(8,128)(2,1)S(1)}, bf16[256,1536]{1,0:T(8,128)(2,1)S(1)}, u32[]{:S(2)}, u32[]{:S(2)}) collective-permute-start(bf16[256,1536]{1,0:T(8,128)(2,1)S(1)} %slice.12), channel_id=1, source_target_pairs={{0,4},{1,5},{2,6},{3,7},{4,0},{5,1},{6,2},{7,3}} | collective-permute-start | bytes 2359304 | tf_op jit(solution)/shard_map/ppermute | solution.py:391
  108.3 26.1 %collective-permute-start.19 = (bf16[256,1536]{1,0:T(8,128)(2,1)S(1)}, bf16[256,1536]{1,0:T(8,128)(2,1)S(1)}, u32[]{:S(2)}, u32[]{:S(2)}) collective-permute-start(bf16[256,1536]{1,0:T(8,128)(2,1)S(1)} %collective-permute-done.5.refs_0_), channel_id=1, source_target_pairs={{0,1},{1,0},{2,3},{3,2},{4,5},{5,4},{6,7},{7,6}} | collective-permute-start | bytes 2359304 | tf_op jit(solution)/shard_map/ppermute | solution.py:391
  108.4 31.3 %collective-permute-start.18 = (bf16[1024,384]{1,0:T(8,128)(2,1)S(1)}, bf16[1024,384]{1,0:T(8,128)(2,1)S(1)}, u32[]{:S(2)}, u32[]{:S(2)}) collective-permute-start(bf16[1024,384]{1,0:T(8,128)(2,1)S(1)} %slice.15), channel_id=1, source_target_pairs={{0,2},{1,3},{2,0},{3,1},{4,6},{5,7},{6,4},{7,5}} | collective-permute-start | bytes 2359304 | tf_op jit(solution)/shard_map/ppermute | solution.py:391
  110.8 23.5 %collective-permute-start.20 = (bf16[128,1536]{1,0:T(8,128)(2,1)S(1)}, bf16[128,1536]{1,0:T(8,128)(2,1)S(1)}, u32[]{:S(2)}, u32[]{:S(2)}) collective-permute-start(bf16[128,1536]{1,0:T(8,128)(2,1)S(1)} %collective-permute-done.6.refs_1_), channel_id=1, source_target_pairs={{0,1},{1,0},{2,3},{3,2},{4,5},{5,4},{6,7},{7,6}} | collective-permute-start | bytes 1179656 | tf_op jit(solution)/shard_map/ppermute | solution.py:391
  110.9 28.8 %collective-permute-start.17 = (bf16[512,384]{1,0:T(8,128)(2,1)S(1)}, bf16[512,384]{1,0:T(8,128)(2,1)S(1)}, u32[]{:S(2)}, u32[]{:S(2)}) collective-permute-start(bf16[512,384]{1,0:T(8,128)(2,1)S(1)} %slice.14), channel_id=1, source_target_pairs={{0,4},{1,5},{2,6},{3,7},{4,0},{5,1},{6,2},{7,3}} | collective-permute-start | bytes 1179656 | tf_op jit(solution)/shard_map/ppermute | solution.py:391
  111.5 18.3 %collective-permute-start.22 = (bf16[1,1920]{1,0:T(2,128)(2,1)S(1)}, bf16[1,1920]{1,0:T(2,128)(2,1)S(1)}, u32[]{:S(2)}, u32[]{:S(2)}) collective-permute-start(bf16[1,1920]{1,0:T(2,128)(2,1)S(1)} %constant_dynamic-update-slice_fusion.refs_4_), channel_id=1, source_target_pairs={{0,7},{1,6},{2,5},{3,4},{4,3},{5,2},{6,1},{7,0}} | collective-permute-start | bytes 11528 | tf_op jit(solution)/shard_map/ppermute | solution.py:391
  129.8 4.5 %collective-permute-start.21 = (bf16[1,1920]{1,0:T(2,128)(2,1)S(1)}, bf16[1,1920]{1,0:T(2,128)(2,1)S(1)}, u32[]{:S(2)}, u32[]{:S(2)}) collective-permute-start(bf16[1,1920]{1,0:T(2,128)(2,1)S(1)} %constant_dynamic-update-slice_fusion.refs_4_), channel_id=1, source_target_pairs={{0,6},{1,7},{2,4},{3,5},{4,2},{5,3},{6,0},{7,1}} | collective-permute-start | bytes 11528 | tf_op jit(solution)/shard_map/ppermute | solution.py:391
  139.7 3.4 %collective-permute-start.24 = (bf16[1024,384]{1,0:T(8,128)(2,1)S(1)}, bf16[1024,384]{1,0:T(8,128)(2,1)S(1)}, u32[]{:S(2)}, u32[]{:S(2)}) collective-permute-start(bf16[1024,384]{1,0:T(8,128)(2,1)S(1)} %collective-permute-done.18.refs_1_), channel_id=1, source_target_pairs={{0,1},{1,0},{2,3},{3,2},{4,5},{5,4},{6,7},{7,6}} | collective-permute-start | bytes 2359304 | tf_op jit(solution)/shard_map/ppermute | solution.py:391
  (4 other events, 42.2 us)

commit v3 on v2

--- a/solution.py
+++ b/solution.py
@@ -13,6 +13,7 @@
 LANES = 128
 BLOCK_ROWS = 4
 GRAN = 16
+LIMIT = 5
 BF16 = jnp.bfloat16
 F32 = jnp.float32
 NT = (((1,), (1,)), ((), ()))
@@ -106,9 +107,14 @@
     wt_ref[router:, :] = tail.astype(BF16)
 
 
+def over_lanes(rows):
+    cols = [jnp.transpose(jnp.broadcast_to(rows[r : r + 1], (LANES, LANES))) for r in range(rows.shape[0])]
+    return jnp.concatenate(cols, axis=0)
+
+
 def dispatch_kernel(
     router, num_experts, capacity, slots, tau_ref, ids_ref, ord_ref, wr_ref, keys_ref, x_ref,
-    pos_ref, start_ref, count_ref, offset_ref, list_ref, gate_ref, xs_ref, wt_ref,
+    start_ref, count_ref, offset_ref, list_ref, pos_ref, gate_ref, xs_ref, wt_ref,
 ):
     grans = slots // GRAN
     spare = start_ref.shape[0] * grans
@@ -119,7 +125,7 @@
             num_experts, capacity, grans, ids_ref, ord_ref, wr_ref, keys_ref,
             pos_ref, start_ref, count_ref, offset_ref, list_ref, wt_ref,
         )
-        xs_ref[spare : spare + 2] = jnp.zeros((2,) + xs_ref.shape[1:], BF16)
+        xs_ref[spare:] = jnp.zeros((xs_ref.shape[0] - spare,) + xs_ref.shape[1:], BF16)
 
     rows = x_ref.shape[0] // LANES
     part = pl.ds(pl.multiple_of(pl.program_id(0) * rows, rows), rows)
@@ -185,7 +191,7 @@
 
 def put_rows(names, spare, y, out_ref):
     for k, name in enumerate(names):
-        out_ref[jnp.where(name == spare, spare + 1, name)] = y[k * GRAN : (k + 1) * GRAN]
+        out_ref[jnp.where(name == spare, spare + 15, name)] = y[k * GRAN : (k + 1) * GRAN]
 
 
 def expert_kernel(bits, tile, spare, count_ref, offset_ref, list_ref, xs_ref, *refs):
@@ -241,133 +247,147 @@
         lax.fori_loop(0, (granules(e, count_ref, offset_ref) + tile - 1) // tile, per_tile, 0)
 
 
-def compact_down(place, total, tile, most, window, w2_refs, b_ref, h_ref, y_ref):
+def compact_down(total, tile, window, w2_refs, b_ref, h_ref, y_ref, after=lambda t, state: state):
     width = y_ref.shape[2]
     _, b2 = split_bias(b_ref, h_ref.shape[1])
 
-    def per_tile(t, _):
-        at = pl.ds(pl.multiple_of((place * most + t * tile) * GRAN, tile * GRAN), tile * GRAN)
+    def per_tile(t, state):
+        at = pl.ds(pl.multiple_of(t * tile * GRAN, tile * GRAN), tile * GRAN)
         y = stacked_dot(h_ref[at, :], w2_refs, slice(None)) + b2
         y_ref[pl.ds(t * tile, tile)] = y.astype(BF16).reshape(tile, GRAN, width)
-        return 0
+        y_ref[pl.ds((t + 1) * tile, window)] = jnp.zeros((window, GRAN, width), BF16)
+        return after(t, state)
 
     tiles = (total + tile - 1) // tile
-    lax.fori_loop(0, tiles, per_tile, 0)
-    y_ref[pl.ds(tiles * tile, window)] = jnp.zeros((window, GRAN, width), BF16)
-
-
-def half_kernel(bits, tile, most, window, count_ref, offset_ref, h_ref, *refs):
+
+    @pl.when(tiles == 0)
+    def _():
+        y_ref[pl.ds(0, window)] = jnp.zeros((window, GRAN, width), BF16)
+
+    return lax.fori_loop(0, tiles, per_tile, jnp.int32(0))
+
+
+def half_kernel(bits, tile, window, count_ref, offset_ref, h_ref, *refs):
     total = granules(expert_names(bits)[0], count_ref, offset_ref)
-    compact_down(0, total, tile, most, window, refs[:-2], refs[-2], h_ref, refs[-1])
-
-
-def final_kernel(
-    bits, tile, most, window, start_ref, count_ref, offset_ref, pos_ref, gate_ref, ids_ref, hot_ref, h_ref, part_ref, y_ref, *refs
-):
-    count, experts = len(bits), expert_names(bits)
+    compact_down(total, tile, window, refs[:-2], refs[-2], h_ref, refs[-1])
+
+
+def final_kernel(bits, tile, window, start_ref, count_ref, offset_ref, slot_ref, gate_ref, h_ref, part_ref, y_ref, *refs):
+    experts = expert_names(bits)
     out_ref, y_buf, o_buf, o_sem = refs[-4:]
     y_refs = (y_ref, y_buf)
     blocks = start_ref.shape[0]
     width = part_ref.shape[1]
     block_tok = BLOCK_ROWS * LANES
     totals = [granules(e, count_ref, offset_ref) for e in experts]
-    compact_down(1, totals[1], tile, most, window, refs[:-5], refs[-5], h_ref, y_buf)
+
+    def rows_of(i, w, b):
+        at = jnp.minimum(offset_ref[b, experts[i]] + w * window, totals[i])
+        return y_refs[i][pl.ds(at, window)].reshape(window * GRAN, width)
 
     def out_copy(pair, slot):
         rows = pl.ds(pl.multiple_of(pair * 2 * block_tok, 2 * block_tok), 2 * block_tok)
         return pltpu.make_async_copy(o_buf.at[slot], out_ref.at[rows], o_sem.at[slot])
 
+    def add(b, w, sub, turn, slots, gates, base_ref, base_at):
+        part = slice(sub * BLOCK_ROWS, (sub + 1) * BLOCK_ROWS)
+        back = window_dot(experts, w, b, start_ref, count_ref, over_lanes(slots[part]), rows_of)
+        gate = over_lanes(gates[part])
+        for c in range(0, width, LANES):
+            base = base_ref[base_at, c : c + LANES].astype(F32)
+            o_buf[turn, sub * block_tok : (sub + 1) * block_tok, c : c + LANES] = (base + back[:, c : c + LANES] * gate).astype(BF16)
+
     def per_pair(pair, _):
-        slot = pair % 2
-        row0 = pl.multiple_of(pair * 2 * BLOCK_ROWS, 2 * BLOCK_ROWS)
-        rows8 = pl.ds(row0, 2 * BLOCK_ROWS)
-        gate_cols = jnp.transpose(gate_ref[rows8, :])
-
-        def window_rows(sub, w, hot):
-            ys = []
-            for i in range(count):
-                at = jnp.minimum(offset_ref[2 * pair + sub, experts[i]] + w * window, totals[i])
-                ys.append(y_refs[i][pl.ds(at, window)].reshape(window * GRAN, width))
-            return jnp.dot(hot, jnp.concatenate(ys, axis=0), preferred_element_type=F32)
-
-        def scaled(sub, back, r):
-            return back[r * LANES : (r + 1) * LANES] * gate_cols[:, sub * BLOCK_ROWS + r : sub * BLOCK_ROWS + r + 1]
+        turn = pair % 2
+        rows8 = pl.ds(pl.multiple_of(pair * 2 * BLOCK_ROWS, 2 * BLOCK_ROWS), 2 * BLOCK_ROWS)
+        slots, gates = slot_ref[rows8, :].astype(F32), gate_ref[rows8, :]
 
         @pl.when(pair >= 2)
         def _():
-            out_copy(pair, slot).wait()
+            out_copy(pair, turn).wait()
 
         for sub in range(2):
             b = 2 * pair + sub
-            hot = hot_ref[pl.ds(pl.multiple_of(b * block_tok, block_tok), block_tok), :]
-            back = window_rows(sub, 0, hot)
-            for r in range(BLOCK_ROWS):
-                source = pl.ds(pl.multiple_of(b * block_tok + r * LANES, LANES), LANES)
-                at = slice((sub * BLOCK_ROWS + r) * LANES, (sub * BLOCK_ROWS + r + 1) * LANES)
-                o_buf[slot, at, :] = (part_ref[source, :].astype(F32) + scaled(sub, back, r)).astype(BF16)
-
+            add(b, 0, sub, turn, slots, gates, part_ref, pl.ds(pl.multiple_of(b * block_tok, block_tok), block_tok))
         for sub in range(2):
             b = 2 * pair + sub
-            longest = count_ref[b, experts[0]]
-            for e in experts[1:]:
-                longest = jnp.maximum(longest, count_ref[b, e])
 
             def more(w, _):
-                local = local_slots(experts, pos_ref[rows8, :], ids_ref[rows8, :], [start_ref[b, e] + w * window for e in experts])
-                back = window_rows(sub, w, hot_rows(local, window, sub))
-                for r in range(BLOCK_ROWS):
-                    at = slice((sub * BLOCK_ROWS + r) * LANES, (sub * BLOCK_ROWS + r + 1) * LANES)
-                    o_buf[slot, at, :] = (o_buf[slot, at, :].astype(F32) + scaled(sub, back, r)).astype(BF16)
+                add(b, w, sub, turn, slots, gates, o_buf.at[turn], slice(sub * block_tok, (sub + 1) * block_tok))
                 return 0
 
-            lax.fori_loop(1, (longest + window - 1) // window, more, 0)
-        out_copy(pair, slot).start()
+            lax.fori_loop(1, (longest_run(experts, b, count_ref) + window - 1) // window, more, 0)
+        out_copy(pair, turn).start()
         return 0
 
-    lax.fori_loop(0, blocks // 2, per_pair, 0)
+    def ready_pairs(t, done):
+        ready = 0
+        for pair in range(blocks // 2):
+            end = offset_ref[2 * pair + 1, experts[-1]] + count_ref[2 * pair + 1, experts[-1]]
+            ready = ready + jnp.where(end <= (t + 1) * tile, 1, 0)
+        lax.fori_loop(done, ready, per_pair, 0)
+        return ready
+
+    done = compact_down(totals[-1], tile, window, refs[:-5], refs[-5], h_ref, y_buf, ready_pairs)
+    lax.fori_loop(done, blocks // 2, per_pair, 0)
     for slot in range(2):
         out_copy(0, slot).wait()
 
 
-def local_slots(experts, pos8, ids8, firsts):
-    local = []
-    for e, first in zip(experts, firsts):
-        mine = (ids8 == e) & (pos8 >= 0)
-        local.append(jnp.transpose(jnp.where(mine, pos8 - first * GRAN, -1).astype(F32)))
-    return local
-
-
-def hot_rows(local, window, sub):
-    lane = iota((LANES, window * GRAN), 1).astype(F32)
+def window_dot(experts, w, b, start_ref, count_ref, slot, rows_of):
+    lane = iota((1, LANES), 1)
     hot = []
-    for r in range(sub * BLOCK_ROWS, (sub + 1) * BLOCK_ROWS):
-        hot.append(jnp.concatenate([(lane == cols[:, r : r + 1]).astype(F32).astype(BF16) for cols in local], axis=1))
-    return jnp.concatenate(hot, axis=0)
-
-
-def combine_kernel(slots, bits, window, start_ref, ys_ref, pos_ref, gate_ref, ids_ref, out_ref, hot_ref):
+    for e in experts:
+        index = lane + w * LANES
+        name = jnp.where(index < count_ref[b, e] * GRAN, index + start_ref[b, e] * GRAN, -2)
+        hot.append((slot == name.astype(F32)).astype(F32).astype(BF16))
+    return jnp.dot(jnp.concatenate(hot, axis=1), jnp.concatenate([rows_of(e, w, b) for e in range(len(experts))], axis=0), preferred_element_type=F32)
+
+
+def longest_run(experts, b, count_ref):
+    longest = count_ref[b, experts[0]]
+    for e in experts[1:]:
+        longest = jnp.maximum(longest, count_ref[b, e])
+    return longest
+
+
+def part_kernel(bits, fresh, window, span, start_ref, count_ref, xs_ref, slot_ref, gate_ref, *refs):
     experts = expert_names(bits)
-    rows = pos_ref.shape[0]
-    pos_cols = jnp.transpose(pos_ref[...].astype(F32))
-    later = (ids_ref[...] == experts[0]) | (ids_ref[...] == experts[1])
-    gate_cols = jnp.transpose(jnp.where(later, 0.0, gate_ref[...]))
-    grans = slots // GRAN
-    upper = iota(pos_ref.shape, 0) < BLOCK_ROWS
-    pair = pl.program_id(0)
-    firsts = [jnp.where(upper, start_ref[2 * pair, e], start_ref[2 * pair + 1, e]) for e in experts]
-    local = local_slots(experts, pos_ref[...], ids_ref[...], firsts)
-    slot_iota = iota((LANES, slots), 1).astype(F32)
-    for sub in range(rows // BLOCK_ROWS):
-        row0 = sub * BLOCK_ROWS
-        y = ys_ref[pl.ds((pl.program_id(0) * (rows // BLOCK_ROWS) + sub) * grans, grans)].reshape(slots, ys_ref.shape[2])
-        hot = [(slot_iota == pos_cols[:, r : r + 1]).astype(F32).astype(BF16) for r in range(row0, row0 + BLOCK_ROWS)]
-        back = jnp.dot(jnp.concatenate(hot, axis=0), y, preferred_element_type=F32)
-        for r in range(BLOCK_ROWS):
-            at = pl.ds(pl.multiple_of(((pl.program_id(0) * rows) + row0 + r) * LANES, LANES), LANES)
-            scaled = back[r * LANES : (r + 1) * LANES] * gate_cols[:, row0 + r : row0 + r + 1]
-            out_ref[at, :] = scaled.astype(BF16)
-        block = pl.ds(pl.multiple_of((2 * pair + sub) * BLOCK_ROWS * LANES, BLOCK_ROWS * LANES), BLOCK_ROWS * LANES)
-        hot_ref[block, :] = hot_rows(local, window, sub)
+    out_ref = refs[-1]
+    width = xs_ref.shape[2]
+    block_tok = BLOCK_ROWS * LANES
+
+    def rows_of(i, w, b):
+        at = jnp.minimum(b * span + start_ref[b, experts[i]] + w * window, xs_ref.shape[0] - 1 - window)
+        return xs_ref[pl.ds(at, window)].reshape(window * GRAN, width)
+
+    def add(b, w, slot, gate, fresh):
+        back = window_dot(experts, w, b, start_ref, count_ref, slot, rows_of)
+        at = pl.ds(pl.multiple_of(b * block_tok, block_tok), block_tok)
+        for c in range(0, width, LANES):
+            scaled = back[:, c : c + LANES] * gate
+            if not fresh:
+                scaled = scaled + out_ref[at, c : c + LANES].astype(F32)
+            out_ref[at, c : c + LANES] = scaled.astype(BF16)
+
+    def per_group(group, _):
+        row0 = pl.multiple_of(group * 4 * BLOCK_ROWS, 4 * BLOCK_ROWS)
+        slots = slot_ref[pl.ds(row0, 4 * BLOCK_ROWS), :].astype(F32)
+        gates = gate_ref[pl.ds(row0, 4 * BLOCK_ROWS), :]
+        for sub in range(4):
+            part = slice(sub * BLOCK_ROWS, (sub + 1) * BLOCK_ROWS)
+            add(4 * group + sub, 0, over_lanes(slots[part]), over_lanes(gates[part]), fresh)
+        for sub in range(4):
+            part = slice(sub * BLOCK_ROWS, (sub + 1) * BLOCK_ROWS)
+
+            def more(w, _):
+                add(4 * group + sub, w, over_lanes(slots[part]), over_lanes(gates[part]), False)
+                return 0
+
+            lax.fori_loop(1, (longest_run(experts, 4 * group + sub, count_ref) + window - 1) // window, more, 0)
+        return 0
+
+    lax.fori_loop(0, start_ref.shape[0] // 4, per_group, 0)
 
 
 def vmem():
@@ -412,15 +432,15 @@
         small = functools.partial(pl.BlockSpec, index_map=lambda i: (0, 0))
         whole = small((rows, LANES))
         table = small((blocks, LANES))
-        xs_shape = (blocks * span + 8, GRAN, width)
-        pos, starts, counts, offsets, lists, gate, xs = pl.pallas_call(
+        xs_shape = (blocks * span + 16, GRAN, width)
+        starts, counts, offsets, lists, slot, gate, xs = pl.pallas_call(
             functools.partial(dispatch_kernel, router, num_experts, capacity, slots),
             out_shape=(
-                jax.ShapeDtypeStruct((rows, LANES), jnp.int32),
                 jax.ShapeDtypeStruct((blocks, LANES), jnp.int32),
                 jax.ShapeDtypeStruct((blocks, LANES), jnp.int32),
                 jax.ShapeDtypeStruct((blocks, LANES), jnp.int32),
                 jax.ShapeDtypeStruct((num_experts, LANES), jnp.int32),
+                jax.ShapeDtypeStruct((rows, LANES), jnp.int32),
                 jax.ShapeDtypeStruct((rows, LANES), F32),
                 pltpu.VMEM(xs_shape, BF16),
             ),
@@ -434,13 +454,8 @@
                 pl.BlockSpec((unit * LANES, width), lambda i: (i, 0)),
             ],
             out_specs=(
-                whole,
-                table,
-                table,
-                table,
-                small((num_experts, LANES)),
-                pl.BlockSpec((unit, LANES), lambda i: (i, 0)),
-                vmem(),
+                table, table, table, small((num_experts, LANES)),
+                whole, pl.BlockSpec((unit, LANES), lambda i: (i, 0)), vmem(),
             ),
             scratch_shapes=[pltpu.VMEM((router + 4 * num_experts, width), BF16)],
             cost_estimate=pl.CostEstimate(flops=9 * 10**9, bytes_accessed=14 * 10**6, transcendentals=0),
@@ -453,7 +468,7 @@
         held = lambda array: pltpu.with_memory_space_constraint(array, pltpu.VMEM)
 
         spare = blocks * span
-        limit = pltpu.CompilerParams(vmem_limit_bytes=8 * 2**20)
+        limit = pltpu.CompilerParams(vmem_limit_bytes=LIMIT * 2**20)
         tables = (counts, offsets, lists)
 
         def cost(flops):
@@ -482,6 +497,22 @@
                 compiler_params=limit,
             )(*tables, held(xs), held(h), *map(held, seconds), *[bias[bit] for bit in bits])
 
+        def partial(bits, xs, part):
+            held_part = [] if part is None else [held(part)]
+            return pl.pallas_call(
+                functools.partial(part_kernel, bits, part is None, window, span),
+                out_shape=pltpu.VMEM((tok_dev, width), BF16),
+                in_specs=[smem()] * 2 + [vmem()] * (3 + len(held_part)),
+                out_specs=vmem(),
+                input_output_aliases={} if part is None else {5: 0},
+                cost_estimate=cost(2 * len(bits) * 10**9),
+                compiler_params=limit,
+            )(starts, counts, held(xs), slot, gate, *held_part)
+
+        x_first, y_first, xs = lax.optimization_barrier((x_first, y_first, xs))
+        cut = width - LANES
+        d_top, d_low = swap(x_first[:cut], 4), swap(y_first[cut:], 2)
+        cx_first, cy_first = swap(x_first, 1), swap(y_first, 1)
         xs = pl.pallas_call(
             functools.partial(expert_kernel, (0, 1), tile, spare),
             out_shape=pltpu.VMEM(xs.shape, BF16),
@@ -493,52 +524,35 @@
             compiler_params=limit,
             name="experts0",
         )(*tables, held(xs), held(first), held(c_first), held(second), held(c_second), bias[0], bias[1])
-
-        x_first, y_first, xs = lax.optimization_barrier((x_first, y_first, xs))
-        cut = width - LANES
-        d_top, d_low = swap(x_first[:cut], 4), swap(y_first[cut:], 2)
-        cx_first, cy_first = swap(x_first, 1), swap(y_first, 1)
         h = up((2, 4, 3, 5), xs, ((x_first,), (y_first,), (cx_first,), (cy_first,)))
-        x_second, y_second, h = lax.optimization_barrier((x_second, y_second, h))
+        part = partial((0, 1), xs, None)
+        x_second, y_second, h, part = lax.optimization_barrier((x_second, y_second, h, part))
         edge = hidden // 3
         e_top, e_low = swap(x_second[:edge], 4), swap(y_second[edge:], 2)
         cx_second, cy_second = swap(x_second, 1), swap(y_second, 1)
         xs = down((2, 4), 0, xs, h, (x_second, y_second))
         xs = down((3, 5), 2, xs, h, (cx_second, cy_second))
-        part, hot = pl.pallas_call(
-            functools.partial(combine_kernel, slots, (6, 7), window),
-            out_shape=(pltpu.VMEM((tok_dev, width), BF16), pltpu.VMEM((tok_dev, 2 * window * GRAN), BF16)),
-            grid=(rows // unit,),
-            in_specs=[
-                smem(),
-                vmem(),
-                pl.BlockSpec((unit, LANES), lambda i: (i, 0)),
-                pl.BlockSpec((unit, LANES), lambda i: (i, 0)),
-                pl.BlockSpec((unit, LANES), lambda i: (i, 0)),
-            ],
-            out_specs=(vmem(), vmem()),
-            cost_estimate=cost(5 * 10**9),
-            compiler_params=limit,
-            name="combine",
-        )(starts, held(xs), pos, gate, ids)
-        d_top, d_low, part, hot = lax.optimization_barrier((d_top, d_low, part, hot))
-        firsts = ((d_top, d_low), (swap(d_top, 1), swap(d_low, 1)))
-        h = up((6, 7), xs, firsts)
-        e_top, e_low, h = lax.optimization_barrier((e_top, e_low, h))
+        part = partial((2, 4, 3, 5), xs, part)
+        d_top, d_low, part = lax.optimization_barrier((d_top, d_low, part))
+        cd_top, cd_low = swap(d_top, 1), swap(d_low, 1)
+        h6 = up((6,), xs, ((d_top, d_low),))
+        h6, cd_top, cd_low = lax.optimization_barrier((h6, cd_top, cd_low))
+        h7 = up((7,), xs, ((cd_top, cd_low),))
+        e_top, e_low, h6, h7 = lax.optimization_barrier((e_top, e_low, h6, h7))
         ce_top, ce_low = swap(e_top, 1), swap(e_low, 1)
         y = pl.pallas_call(
-            functools.partial(half_kernel, (6, 7), tile, most, window),
+            functools.partial(half_kernel, (6,), tile, window),
             out_shape=pltpu.VMEM((most + window, GRAN, width), BF16),
             in_specs=[smem()] * 2 + [vmem()] * 4,
             out_specs=vmem(),
             cost_estimate=cost(2 * 10**9),
             compiler_params=limit,
             name="half",
-        )(counts, offsets, held(h), held(e_top), held(e_low), bias[6])
+        )(counts, offsets, held(h6), held(e_top), held(e_low), bias[6])
         out = pl.pallas_call(
-            functools.partial(final_kernel, (6, 7), tile, most, window),
+            functools.partial(final_kernel, (6, 7), tile, window),
             out_shape=jax.ShapeDtypeStruct((tok_dev, width), BF16),
-            in_specs=[smem()] * 3 + [vmem()] * (7 + 3),
+            in_specs=[smem()] * 3 + [vmem()] * (5 + 3),
             out_specs=hbm(),
             scratch_shapes=[
                 pltpu.VMEM((most + window, GRAN, width), BF16),
@@ -546,9 +560,9 @@
                 pltpu.SemaphoreType.DMA((2,)),
             ],
             cost_estimate=cost(5 * 10**9),
-            compiler_params=limit,
+            compiler_params=pltpu.CompilerParams(vmem_limit_bytes=7 * 2**20),
             name="final",
-        )(starts, counts, offsets, pos, gate, ids, held(hot), held(h), held(part), held(y), held(ce_top), held(ce_low), bias[7])
+        )(starts, counts, offsets, slot, gate, held(h7), held(part), held(y), held(ce_top), held(ce_low), bias[7])
         return out[None]
 
     return jax.shard_map(

time: 153 us -> 143 us (0.935)
  waiting for transfers between devices: 52.1 us -> 41.3 us
    ppermute x25, waiting for transfers between devices: 52.1 us -> 41.3 us  [swap(): lax.ppermute(value, EXPERT_AXES, [(e, e ^ bit) for e in range(num_experts)])]
    pallas_call x2 -> x3, Pallas kernels: 16.2 us -> 17.3 us  [up(): pl.pallas_call(functools.partial(up_kernel, bits, pieces, tile, most), ou...]
    pallas_call x3 -> x4, Pallas kernels: 21.6 us -> 22.1 us  [the longest x2 10.6 us: partial(): pl.pallas_call(functools.partial(part_kernel, bits, part is None, window,...]
  transfers between devices with their start and end apart: 25 -> 25, of which waited for: 6 -> 9; matrix products, arithmetic and copies ran while one was open for 1% -> 0% of each run, Pallas kernels for 44% -> 49%
where the time goes in v3:
time: 143 us; the launch traced here: 142 us
  Pallas kernels  77.9 us (54%)
  waiting for transfers between devices  41.3 us (29%)
  starting transfers between devices  21.5 us (15%)
    ppermute x25, waiting for transfers between devices, swap(): lax.ppermute(value, EXPERT_AXES, [(e, e ^ bit) for e in range(num_experts)])  41.3 us
    ppermute x25, starting transfers between devices, swap(): lax.ppermute(value, EXPERT_AXES, [(e, e ^ bit) for e in range(num_experts)])  21.5 us
    pallas_call x3, Pallas kernels, up(): pl.pallas_call(functools.partial(up_kernel, bits, pieces, tile, most), ou...  17.3 us
    pallas_call x1, Pallas kernels, inner_step(): pl.pallas_call(functools.partial(dispatch_kernel, router, num_experts, ca...  17 us
    pallas_call x1, Pallas kernels, inner_step(): pl.pallas_call(functools.partial(expert_kernel, (0, 1), tile, spare), out...  10.8 us
    pallas_call x2, Pallas kernels, down(): pl.pallas_call(functools.partial(down_kernel, bits, place, tile, most, sp...  10.6 us
    pallas_call x2, Pallas kernels, partial(): pl.pallas_call(functools.partial(part_kernel, bits, part is None, window,...  10.6 us
    pallas_call x1, Pallas kernels, inner_step(): pl.pallas_call(functools.partial(final_kernel, (6, 7), tile, window), out...  8.71 us
  transfers between devices with their start and end apart: 25, of which 9 were waited for; matrix products, arithmetic and copies ran while one was open for 0% of the time, Pallas kernels for 49%

profile of v3, /device:TPU:0, one launch (start us, length us, event | category | flops | bytes accessed | tf_op | source)
XLA Modules:
  0.0 141.9 jit_solution(6272725198419155047)
XLA Ops:
  0.0 3.3 %collective-permute-start.3 = (bf16[384,1536]{1,0:T(8,128)(2,1)}, bf16[384,1536]{1,0:T(8,128)(2,1)S(1)}, u32[]{:S(2)}, u32[]{:S(2)}) collective-permute-start(bf16[384,1536]{1,0:T(8,128)(2,1)} %bitcast.8), channel_id=1, source_target_pairs={{0,4},{1,5},{2,6},{3,7},{4,0},{5,1},{6,2},{7,3}} | collective-permute-start | bytes 3538952 | tf_op jit(solution)/shard_map/ppermute | solution.py:411
  3.3 1.5 %collective-permute-start.2 = (bf16[384,1536]{1,0:T(8,128)(2,1)}, bf16[384,1536]{1,0:T(8,128)(2,1)S(1)}, u32[]{:S(2)}, u32[]{:S(2)}) collective-permute-start(bf16[384,1536]{1,0:T(8,128)(2,1)} %bitcast.9), channel_id=1, source_target_pairs={{0,2},{1,3},{2,0},{3,1},{4,6},{5,7},{6,4},{7,5}} | collective-permute-start | bytes 3538952 | tf_op jit(solution)/shard_map/ppermute | solution.py:411
  6.0 17.0 %dispatch.1 = (s32[16,128]{1,0:T(8,128)S(1)}, s32[16,128]{1,0:T(8,128)S(1)}, s32[16,128]{1,0:T(8,128)S(1)}, s32[8,128]{1,0:T(8,128)S(1)}, s32[64,128]{1,0:T(8,12...) custom-call(f32[1,1]{1,0:T(1,128)} %bitcast.7.tau_ref, s32[64,128]{1,0:T(8,128)} %bitcast.17, ...), custom_call_target="tpu_custom_call" | custom-call | flops 8999999488 | bytes 14000000 | tf_op jit(solution)/shard_map/dispatch/pallas_call | solution.py:436
  23.0 6.5 %collective-permute-done.3.refs_1_ = bf16[384,1536]{1,0:T(8,128)(2,1)S(1)} collective-permute-done((bf16[384,1536]{1,0:T(8,128)(2,1)}, bf16[384,1536]{1,0:T(8,128)(2,1)S(1)}, u32[]{:S(2)}, u32[]{:S(2)}) %collective-permute-start.3) | collective-permute-done | bytes 1179680 | tf_op jit(solution)/shard_map/ppermute | solution.py:411
  29.5 1.5 %collective-permute-done.2.refs_0_ = bf16[384,1536]{1,0:T(8,128)(2,1)S(1)} collective-permute-done((bf16[384,1536]{1,0:T(8,128)(2,1)}, bf16[384,1536]{1,0:T(8,128)(2,1)S(1)}, u32[]{:S(2)}, u32[]{:S(2)}) %collective-permute-start.2) | collective-permute-done | bytes 1179680 | tf_op jit(solution)/shard_map/ppermute | solution.py:411
  31.6 3.1 %collective-permute-done.12.refs_7_.refs_3_ = bf16[1,1920]{1,0:T(2,128)(2,1)S(1)} collective-permute-done((bf16[1,1920]{1,0:T(2,128)(2,1)S(1)}, bf16[1,1920]{1,0:T(2,128)(2,1)S(1)}, u32[]{:S(2)}, u32[]{:S(2)}) %collective-permute-start.12) | collective-permute-done | bytes 3872 | tf_op jit(solution)/shard_map/ppermute | solution.py:411
  35.8 1.9 %collective-permute-done.11.refs_6_.refs_2_ = bf16[1,1920]{1,0:T(2,128)(2,1)S(1)} collective-permute-done((bf16[1,1920]{1,0:T(2,128)(2,1)S(1)}, bf16[1,1920]{1,0:T(2,128)(2,1)S(1)}, u32[]{:S(2)}, u32[]{:S(2)}) %collective-permute-start.11) | collective-permute-done | bytes 3872 | tf_op jit(solution)/shard_map/ppermute | solution.py:411
  39.2 1.7 %collective-permute-start.1 = (bf16[1536,384]{1,0:T(8,128)(2,1)S(1)}, bf16[1536,384]{1,0:T(8,128)(2,1)S(1)}, u32[]{:S(2)}, u32[]{:S(2)}) collective-permute-start(bf16[1536,384]{1,0:T(8,128)(2,1)S(1)} %bitcast.13), channel_id=1, source_target_pairs={{0,4},{1,5},{2,6},{3,7},{4,0},{5,1},{6,2},{7,3}} | collective-permute-start | bytes 3538952 | tf_op jit(solution)/shard_map/ppermute | solution.py:411
  40.9 1.5 %collective-permute-start = (bf16[1536,384]{1,0:T(8,128)(2,1)S(1)}, bf16[1536,384]{1,0:T(8,128)(2,1)S(1)}, u32[]{:S(2)}, u32[]{:S(2)}) collective-permute-start(bf16[1536,384]{1,0:T(8,128)(2,1)S(1)} %bitcast.14), channel_id=1, source_target_pairs={{0,2},{1,3},{2,0},{3,1},{4,6},{5,7},{6,4},{7,5}} | collective-permute-start | bytes 3538952 | tf_op jit(solution)/shard_map/ppermute | solution.py:411
  42.4 10.8 %experts0.1.xs_ref = bf16[656,16,384]{2,1,0:T(8,128)(2,1)S(1)} custom-call(s32[16,128]{1,0:T(8,128)S(1)} %get-tuple-element.30.count_ref, s32[16,128]{1,0:T(8,128)S(1)} %get-tuple-element.31.offset_ref, s32[8,128]{1,0:T(8,128)S(1)} %get-tuple-element.34.list_ref, bf16[656,16,384]{2,1,0:T(8,128)(2,1)S(1)} %get-tuple-element.36.xs_ref, ...), custom_call_target="tpu_custom_call", output_to_operand_aliasing={{}: (3, {})} | custom-call | flops 6000000000 | bytes 1000000 | tf_op jit(solution)/shard_map/experts0/pallas_call | solution.py:516
  53.2 2.4 %collective-permute-start.9 = (bf16[1,1920]{1,0:T(2,128)(2,1)S(1)}, bf16[1,1920]{1,0:T(2,128)(2,1)S(1)}, u32[]{:S(2)}, u32[]{:S(2)}) collective-permute-start(bf16[1,1920]{1,0:T(2,128)(2,1)S(1)} %constant_dynamic-update-slice_fusion.refs_4_), channel_id=1, source_target_pairs={{0,2},{1,3},{2,0},{3,1},{4,6},{5,7},{6,4},{7,5}} | collective-permute-start | bytes 11528 | tf_op jit(solution)/shard_map/ppermute | solution.py:411
  55.6 4.1 %shard_map.101.refs_0_ = bf16[8192,384]{1,0:T(8,128)(2,1)S(1)} custom-call(s32[16,128]{1,0:T(8,128)S(1)} %get-tuple-element.29.start_ref, s32[16,128]{1,0:T(8,128)S(1)} %get-tuple-element.30.count_ref, bf16[656,16,384]{2,1,0:T(8,128)(2,1)S(1)} %experts0.1.xs_ref, s32[64,128]{1,0:T(8,128)S(1)} %get-tuple-element.32.slot_ref, ...), custom_call_target="tpu_custom_call" | custom-call | flops 4000000000 | bytes 1000000 | tf_op jit(solution)/shard_map/pallas_call | solution.py:502
  59.8 8.8 %collective-permute-done.9.refs_4_.refs_2_ = bf16[1,1920]{1,0:T(2,128)(2,1)S(1)} collective-permute-done((bf16[1,1920]{1,0:T(2,128)(2,1)S(1)}, bf16[1,1920]{1,0:T(2,128)(2,1)S(1)}, u32[]{:S(2)}, u32[]{:S(2)}) %collective-permute-start.9) | collective-permute-done | bytes 3872 | tf_op jit(solution)/shard_map/ppermute | solution.py:411
  68.5 11.1 %shard_map.100.h_ref = bf16[6144,1536]{1,0:T(8,128)(2,1)S(1)} custom-call(s32[16,128]{1,0:T(8,128)S(1)} %get-tuple-element.30.count_ref, s32[16,128]{1,0:T(8,128)S(1)} %get-tuple-element.31.offset_ref, s32[8,128]{1,0:T(8,128)S(1)} %get-tuple-element.34.list_ref, bf16[656,16,384]{2,1,0:T(8,128)(2,1)S(1)} %experts0.1.xs_ref, ...), custom_call_target="tpu_custom_call" | custom-call | flops 8000000000 | bytes 1000000 | tf_op jit(solution)/shard_map/pallas_call | solution.py:480
  81.7 5.8 %shard_map.102.xs_ref = bf16[656,16,384]{2,1,0:T(8,128)(2,1)S(1)} custom-call(s32[16,128]{1,0:T(8,128)S(1)} %get-tuple-element.30.count_ref, s32[16,128]{1,0:T(8,128)S(1)} %get-tuple-element.31.offset_ref, s32[8,128]{1,0:T(8,128)S(1)} %get-tuple-element.34.list_ref, bf16[656,16,384]{2,1,0:T(8,128)(2,1)S(1)} %experts0.1.xs_ref, ...), custom_call_target="tpu_custom_call", output_to_operand_aliasing={{}: (3, {})} | custom-call | flops 4000000000 | bytes 1000000 | tf_op jit(solution)/shard_map/pallas_call | solution.py:490
  87.5 4.8 %shard_map.103.xs_ref = bf16[656,16,384]{2,1,0:T(8,128)(2,1)S(1)} custom-call(s32[16,128]{1,0:T(8,128)S(1)} %get-tuple-element.30.count_ref, s32[16,128]{1,0:T(8,128)S(1)} %get-tuple-element.31.offset_ref, s32[8,128]{1,0:T(8,128)S(1)} %get-tuple-element.34.list_ref, bf16[656,16,384]{2,1,0:T(8,128)(2,1)S(1)} %shard_map.102.xs_ref, ...), custom_call_target="tpu_custom_call", output_to_operand_aliasing={{}: (3, {})} | custom-call | flops 4000000000 | bytes 1000000 | tf_op jit(solution)/shard_map/pallas_call | solution.py:490
  92.4 6.5 %shard_map.104.part_ref = bf16[8192,384]{1,0:T(8,128)(2,1)S(1)} custom-call(s32[16,128]{1,0:T(8,128)S(1)} %get-tuple-element.29.start_ref, s32[16,128]{1,0:T(8,128)S(1)} %get-tuple-element.30.count_ref, bf16[656,16,384]{2,1,0:T(8,128)(2,1)S(1)} %shard_map.103.xs_ref, s32[64,128]{1,0:T(8,128)S(1)} %get-tuple-element.32.slot_ref, ...), custom_call_target="tpu_custom_call", output_to_operand_aliasing={{}: (5, {})} | custom-call | flops 8000000000 | bytes 1000000 | tf_op jit(solution)/shard_map/pallas_call | solution.py:502
  98.9 1.9 %collective-permute-done.17.refs_0_ = bf16[256,1536]{1,0:T(8,128)(2,1)S(1)} collective-permute-done((bf16[256,1536]{1,0:T(8,128)(2,1)S(1)}, bf16[256,1536]{1,0:T(8,128)(2,1)S(1)}, u32[]{:S(2)}, u32[]{:S(2)}) %collective-permute-start.17) | collective-permute-done | bytes 786464 | tf_op jit(solution)/shard_map/ppermute | solution.py:411
  104.7 16.4 %collective-permute-done.19.refs_2_ = bf16[1,1920]{1,0:T(2,128)(2,1)S(1)} collective-permute-done((bf16[1,1920]{1,0:T(2,128)(2,1)S(1)}, bf16[1,1920]{1,0:T(2,128)(2,1)S(1)}, u32[]{:S(2)}, u32[]{:S(2)}) %collective-permute-start.19) | collective-permute-done | bytes 3872 | tf_op jit(solution)/shard_map/ppermute | solution.py:411
  121.6 3.1 %shard_map.105.h_ref = bf16[1536,1536]{1,0:T(8,128)(2,1)S(1)} custom-call(s32[16,128]{1,0:T(8,128)S(1)} %get-tuple-element.30.count_ref, s32[16,128]{1,0:T(8,128)S(1)} %get-tuple-element.31.offset_ref, s32[8,128]{1,0:T(8,128)S(1)} %get-tuple-element.34.list_ref, bf16[656,16,384]{2,1,0:T(8,128)(2,1)S(1)} %shard_map.103.xs_ref, ...), custom_call_target="tpu_custom_call" | custom-call | flops 2000000000 | bytes 1000000 | tf_op jit(solution)/shard_map/pallas_call | solution.py:480
  125.0 3.1 %shard_map.106.h_ref = bf16[1536,1536]{1,0:T(8,128)(2,1)S(1)} custom-call(s32[16,128]{1,0:T(8,128)S(1)} %get-tuple-element.30.count_ref, s32[16,128]{1,0:T(8,128)S(1)} %get-tuple-element.31.offset_ref, s32[8,128]{1,0:T(8,128)S(1)} %get-tuple-element.34.list_ref, bf16[656,16,384]{2,1,0:T(8,128)(2,1)S(1)} %shard_map.103.xs_ref, ...), custom_call_target="tpu_custom_call" | custom-call | flops 2000000000 | bytes 1000000 | tf_op jit(solution)/shard_map/pallas_call | solution.py:480
  128.1 2.0 %collective-permute-start.24 = (bf16[1024,384]{1,0:T(8,128)(2,1)S(1)}, bf16[1024,384]{1,0:T(8,128)(2,1)S(1)}, u32[]{:S(2)}, u32[]{:S(2)}) collective-permute-start(bf16[1024,384]{1,0:T(8,128)(2,1)S(1)} %collective-permute-done.14.refs_1_), channel_id=1, source_target_pairs={{0,1},{1,0},{2,3},{3,2},{4,5},{5,4},{6,7},{7,6}} | collective-permute-start | bytes 2359304 | tf_op jit(solution)/shard_map/ppermute | solution.py:411
  130.2 2.8 %half.1.y_ref = bf16[104,16,384]{2,1,0:T(8,128)(2,1)S(1)} custom-call(s32[16,128]{1,0:T(8,128)S(1)} %get-tuple-element.30.count_ref, s32[16,128]{1,0:T(8,128)S(1)} %get-tuple-element.31.offset_ref, bf16[1536,1536]{1,0:T(8,128)(2,1)S(1)} %shard_map.105.h_ref, bf16[512,384]{1,0:T(8,128)(2,1)S(1)} %collective-permute-done.13.refs_0_, ...), custom_call_target="tpu_custom_call" | custom-call | flops 2000000000 | bytes 1000000 | tf_op jit(solution)/shard_map/half/pallas_call | solution.py:543
  133.0 8.7 %final.1 = bf16[8192,384]{1,0:T(8,128)(2,1)} custom-call(s32[16,128]{1,0:T(8,128)S(1)} %get-tuple-element.29.start_ref, s32[16,128]{1,0:T(8,128)S(1)} %get-tuple-element.30.count_ref, s32[16,128]{1,0:T(8,128)S(1)} %get-tuple-element.31.offset_ref, s32[64,128]{1,0:T(8,128)S(1)} %get-tuple-element.32.slot_ref, f32[64,128]{1,0:T(8,128)S(1)} %get-tuple-element.33.gate_ref, ...), custom_call_target="tpu_custom_call" | custom-call | flops 5000000000 | bytes 1000000 | tf_op jit(solution)/shard_map/final/pallas_call | solution.py:552
  (51 shorter events, 10.6 us)
Async XLA Ops:
  0.0 29.5 %collective-permute-start.3 = (bf16[384,1536]{1,0:T(8,128)(2,1)}, bf16[384,1536]{1,0:T(8,128)(2,1)S(1)}, u32[]{:S(2)}, u32[]{:S(2)}) collective-permute-start(bf16[384,1536]{1,0:T(8,128)(2,1)} %bitcast.8), channel_id=1, source_target_pairs={{0,4},{1,5},{2,6},{3,7},{4,0},{5,1},{6,2},{7,3}} | collective-permute-start | bytes 3538952 | tf_op jit(solution)/shard_map/ppermute | solution.py:411
  3.3 27.6 %collective-permute-start.2 = (bf16[384,1536]{1,0:T(8,128)(2,1)}, bf16[384,1536]{1,0:T(8,128)(2,1)S(1)}, u32[]{:S(2)}, u32[]{:S(2)}) collective-permute-start(bf16[384,1536]{1,0:T(8,128)(2,1)} %bitcast.9), channel_id=1, source_target_pairs={{0,2},{1,3},{2,0},{3,1},{4,6},{5,7},{6,4},{7,5}} | collective-permute-start | bytes 3538952 | tf_op jit(solution)/shard_map/ppermute | solution.py:411
  4.8 34.3 %collective-permute-start.4 = (bf16[384,1536]{1,0:T(8,128)(2,1)}, bf16[384,1536]{1,0:T(8,128)(2,1)}, u32[]{:S(2)}, u32[]{:S(2)}) collective-permute-start(bf16[384,1536]{1,0:T(8,128)(2,1)} %bitcast.10), channel_id=1, source_target_pairs={{0,1},{1,0},{2,3},{3,2},{4,5},{5,4},{6,7},{7,6}} | collective-permute-start | bytes 3538952 | tf_op jit(solution)/shard_map/ppermute | solution.py:411
  4.8 36.1 %collective-permute-start.5 = (bf16[1536,384]{1,0:T(8,128)(2,1)}, bf16[1536,384]{1,0:T(8,128)(2,1)}, u32[]{:S(2)}, u32[]{:S(2)}) collective-permute-start(bf16[1536,384]{1,0:T(8,128)(2,1)} %bitcast.12), channel_id=1, source_target_pairs={{0,1},{1,0},{2,3},{3,2},{4,5},{5,4},{6,7},{7,6}} | collective-permute-start | bytes 3538952 | tf_op jit(solution)/shard_map/ppermute | solution.py:411
  31.0 37.6 %collective-permute-start.7 = (bf16[384,1536]{1,0:T(8,128)(2,1)S(1)}, bf16[384,1536]{1,0:T(8,128)(2,1)S(1)}, u32[]{:S(2)}, u32[]{:S(2)}) collective-permute-start(bf16[384,1536]{1,0:T(8,128)(2,1)S(1)} %collective-permute-done.2.refs_0_), channel_id=1, source_target_pairs={{0,1},{1,0},{2,3},{3,2},{4,5},{5,4},{6,7},{7,6}} | collective-permute-start | bytes 3538952 | tf_op jit(solution)/shard_map/ppermute | solution.py:411
  31.0 37.6 %collective-permute-start.8 = (bf16[384,1536]{1,0:T(8,128)(2,1)S(1)}, bf16[384,1536]{1,0:T(8,128)(2,1)S(1)}, u32[]{:S(2)}, u32[]{:S(2)}) collective-permute-start(bf16[384,1536]{1,0:T(8,128)(2,1)S(1)} %collective-permute-done.3.refs_1_), channel_id=1, source_target_pairs={{0,1},{1,0},{2,3},{3,2},{4,5},{5,4},{6,7},{7,6}} | collective-permute-start | bytes 3538952 | tf_op jit(solution)/shard_map/ppermute | solution.py:411
  31.5 3.1 %collective-permute-start.12 = (bf16[1,1920]{1,0:T(2,128)(2,1)S(1)}, bf16[1,1920]{1,0:T(2,128)(2,1)S(1)}, u32[]{:S(2)}, u32[]{:S(2)}) collective-permute-start(bf16[1,1920]{1,0:T(2,128)(2,1)S(1)} %constant_dynamic-update-slice_fusion.refs_4_), channel_id=1, source_target_pairs={{0,5},{1,4},{2,7},{3,6},{4,1},{5,0},{6,3},{7,2}} | collective-permute-start | bytes 11528 | tf_op jit(solution)/shard_map/ppermute | solution.py:411
  34.6 3.1 %collective-permute-start.11 = (bf16[1,1920]{1,0:T(2,128)(2,1)S(1)}, bf16[1,1920]{1,0:T(2,128)(2,1)S(1)}, u32[]{:S(2)}, u32[]{:S(2)}) collective-permute-start(bf16[1,1920]{1,0:T(2,128)(2,1)S(1)} %constant_dynamic-update-slice_fusion.refs_4_), channel_id=1, source_target_pairs={{0,3},{1,2},{2,1},{3,0},{4,7},{5,6},{6,5},{7,4}} | collective-permute-start | bytes 11528 | tf_op jit(solution)/shard_map/ppermute | solution.py:411
  38.9 14.4 %collective-permute-start.10 = (bf16[1,1920]{1,0:T(2,128)(2,1)S(1)}, bf16[1,1920]{1,0:T(2,128)(2,1)S(1)}, u32[]{:S(2)}, u32[]{:S(2)}) collective-permute-start(bf16[1,1920]{1,0:T(2,128)(2,1)S(1)} %constant_dynamic-update-slice_fusion.refs_4_), channel_id=1, source_target_pairs={{0,4},{1,5},{2,6},{3,7},{4,0},{5,1},{6,2},{7,3}} | collective-permute-start | bytes 11528 | tf_op jit(solution)/shard_map/ppermute | solution.py:411
  39.2 40.5 %collective-permute-start.1 = (bf16[1536,384]{1,0:T(8,128)(2,1)S(1)}, bf16[1536,384]{1,0:T(8,128)(2,1)S(1)}, u32[]{:S(2)}, u32[]{:S(2)}) collective-permute-start(bf16[1536,384]{1,0:T(8,128)(2,1)S(1)} %bitcast.13), channel_id=1, source_target_pairs={{0,4},{1,5},{2,6},{3,7},{4,0},{5,1},{6,2},{7,3}} | collective-permute-start | bytes 3538952 | tf_op jit(solution)/shard_map/ppermute | solution.py:411
  40.9 38.7 %collective-permute-start = (bf16[1536,384]{1,0:T(8,128)(2,1)S(1)}, bf16[1536,384]{1,0:T(8,128)(2,1)S(1)}, u32[]{:S(2)}, u32[]{:S(2)}) collective-permute-start(bf16[1536,384]{1,0:T(8,128)(2,1)S(1)} %bitcast.14), channel_id=1, source_target_pairs={{0,2},{1,3},{2,0},{3,1},{4,6},{5,7},{6,4},{7,5}} | collective-permute-start | bytes 3538952 | tf_op jit(solution)/shard_map/ppermute | solution.py:411
  53.2 15.3 %collective-permute-start.9 = (bf16[1,1920]{1,0:T(2,128)(2,1)S(1)}, bf16[1,1920]{1,0:T(2,128)(2,1)S(1)}, u32[]{:S(2)}, u32[]{:S(2)}) collective-permute-start(bf16[1,1920]{1,0:T(2,128)(2,1)S(1)} %constant_dynamic-update-slice_fusion.refs_4_), channel_id=1, source_target_pairs={{0,2},{1,3},{2,0},{3,1},{4,6},{5,7},{6,4},{7,5}} | collective-permute-start | bytes 11528 | tf_op jit(solution)/shard_map/ppermute | solution.py:411
  79.6 7.9 %collective-permute-start.15 = (bf16[1536,384]{1,0:T(8,128)(2,1)S(1)}, bf16[1536,384]{1,0:T(8,128)(2,1)S(1)}, u32[]{:S(2)}, u32[]{:S(2)}) collective-permute-start(bf16[1536,384]{1,0:T(8,128)(2,1)S(1)} %collective-permute-done.refs_0_), channel_id=1, source_target_pairs={{0,1},{1,0},{2,3},{3,2},{4,5},{5,4},{6,7},{7,6}} | collective-permute-start | bytes 3538952 | tf_op jit(solution)/shard_map/ppermute | solution.py:411
  79.7 7.9 %collective-permute-start.16 = (bf16[1536,384]{1,0:T(8,128)(2,1)S(1)}, bf16[1536,384]{1,0:T(8,128)(2,1)S(1)}, u32[]{:S(2)}, u32[]{:S(2)}) collective-permute-start(bf16[1536,384]{1,0:T(8,128)(2,1)S(1)} %collective-permute-done.1.refs_1_), channel_id=1, source_target_pairs={{0,1},{1,0},{2,3},{3,2},{4,5},{5,4},{6,7},{7,6}} | collective-permute-start | bytes 3538952 | tf_op jit(solution)/shard_map/ppermute | solution.py:411
  80.3 18.6 %collective-permute-start.18 = (bf16[128,1536]{1,0:T(8,128)(2,1)S(1)}, bf16[128,1536]{1,0:T(8,128)(2,1)S(1)}, u32[]{:S(2)}, u32[]{:S(2)}) collective-permute-start(bf16[128,1536]{1,0:T(8,128)(2,1)S(1)} %slice.15), channel_id=1, source_target_pairs={{0,2},{1,3},{2,0},{3,1},{4,6},{5,7},{6,4},{7,5}} | collective-permute-start | bytes 1179656 | tf_op jit(solution)/shard_map/ppermute | solution.py:411
  81.1 19.6 %collective-permute-start.17 = (bf16[256,1536]{1,0:T(8,128)(2,1)S(1)}, bf16[256,1536]{1,0:T(8,128)(2,1)S(1)}, u32[]{:S(2)}, u32[]{:S(2)}) collective-permute-start(bf16[256,1536]{1,0:T(8,128)(2,1)S(1)} %slice.14), channel_id=1, source_target_pairs={{0,4},{1,5},{2,6},{3,7},{4,0},{5,1},{6,2},{7,3}} | collective-permute-start | bytes 2359304 | tf_op jit(solution)/shard_map/ppermute | solution.py:411
  100.8 23.9 %collective-permute-start.20 = (bf16[256,1536]{1,0:T(8,128)(2,1)S(1)}, bf16[256,1536]{1,0:T(8,128)(2,1)S(1)}, u32[]{:S(2)}, u32[]{:S(2)}) collective-permute-start(bf16[256,1536]{1,0:T(8,128)(2,1)S(1)} %collective-permute-done.17.refs_0_), channel_id=1, source_target_pairs={{0,1},{1,0},{2,3},{3,2},{4,5},{5,4},{6,7},{7,6}} | collective-permute-start | bytes 2359304 | tf_op jit(solution)/shard_map/ppermute | solution.py:411
  100.9 27.3 %collective-permute-start.14 = (bf16[1024,384]{1,0:T(8,128)(2,1)S(1)}, bf16[1024,384]{1,0:T(8,128)(2,1)S(1)}, u32[]{:S(2)}, u32[]{:S(2)}) collective-permute-start(bf16[1024,384]{1,0:T(8,128)(2,1)S(1)} %slice.13), channel_id=1, source_target_pairs={{0,2},{1,3},{2,0},{3,1},{4,6},{5,7},{6,4},{7,5}} | collective-permute-start | bytes 2359304 | tf_op jit(solution)/shard_map/ppermute | solution.py:411
  101.6 23.1 %collective-permute-start.21 = (bf16[128,1536]{1,0:T(8,128)(2,1)S(1)}, bf16[128,1536]{1,0:T(8,128)(2,1)S(1)}, u32[]{:S(2)}, u32[]{:S(2)}) collective-permute-start(bf16[128,1536]{1,0:T(8,128)(2,1)S(1)} %collective-permute-done.18.refs_1_), channel_id=1, source_target_pairs={{0,1},{1,0},{2,3},{3,2},{4,5},{5,4},{6,7},{7,6}} | collective-permute-start | bytes 1179656 | tf_op jit(solution)/shard_map/ppermute | solution.py:411
  101.9 26.2 %collective-permute-start.13 = (bf16[512,384]{1,0:T(8,128)(2,1)S(1)}, bf16[512,384]{1,0:T(8,128)(2,1)S(1)}, u32[]{:S(2)}, u32[]{:S(2)}) collective-permute-start(bf16[512,384]{1,0:T(8,128)(2,1)S(1)} %slice.12), channel_id=1, source_target_pairs={{0,4},{1,5},{2,6},{3,7},{4,0},{5,1},{6,2},{7,3}} | collective-permute-start | bytes 1179656 | tf_op jit(solution)/shard_map/ppermute | solution.py:411
  103.3 17.7 %collective-permute-start.19 = (bf16[1,1920]{1,0:T(2,128)(2,1)S(1)}, bf16[1,1920]{1,0:T(2,128)(2,1)S(1)}, u32[]{:S(2)}, u32[]{:S(2)}) collective-permute-start(bf16[1,1920]{1,0:T(2,128)(2,1)S(1)} %constant_dynamic-update-slice_fusion.refs_4_), channel_id=1, source_target_pairs={{0,6},{1,7},{2,4},{3,5},{4,2},{5,3},{6,0},{7,1}} | collective-permute-start | bytes 11528 | tf_op jit(solution)/shard_map/ppermute | solution.py:411
  121.0 4.0 %collective-permute-start.22 = (bf16[1,1920]{1,0:T(2,128)(2,1)S(1)}, bf16[1,1920]{1,0:T(2,128)(2,1)S(1)}, u32[]{:S(2)}, u32[]{:S(2)}) collective-permute-start(bf16[1,1920]{1,0:T(2,128)(2,1)S(1)} %constant_dynamic-update-slice_fusion.refs_4_), channel_id=1, source_target_pairs={{0,7},{1,6},{2,5},{3,4},{4,3},{5,2},{6,1},{7,0}} | collective-permute-start | bytes 11528 | tf_op jit(solution)/shard_map/ppermute | solution.py:411
  128.1 4.9 %collective-permute-start.24 = (bf16[1024,384]{1,0:T(8,128)(2,1)S(1)}, bf16[1024,384]{1,0:T(8,128)(2,1)S(1)}, u32[]{:S(2)}, u32[]{:S(2)}) collective-permute-start(bf16[1024,384]{1,0:T(8,128)(2,1)S(1)} %collective-permute-done.14.refs_1_), channel_id=1, source_target_pairs={{0,1},{1,0},{2,3},{3,2},{4,5},{5,4},{6,7},{7,6}} | collective-permute-start | bytes 2359304 | tf_op jit(solution)/shard_map/ppermute | solution.py:411
  130.1 2.8 %collective-permute-start.23 = (bf16[512,384]{1,0:T(8,128)(2,1)S(1)}, bf16[512,384]{1,0:T(8,128)(2,1)S(1)}, u32[]{:S(2)}, u32[]{:S(2)}) collective-permute-start(bf16[512,384]{1,0:T(8,128)(2,1)S(1)} %collective-permute-done.13.refs_0_), channel_id=1, source_target_pairs={{0,1},{1,0},{2,3},{3,2},{4,5},{5,4},{6,7},{7,6}} | collective-permute-start | bytes 1179656 | tf_op jit(solution)/shard_map/ppermute | solution.py:411
  (5 other events, 121.7 us)

commit v4 on v3

--- a/solution.py
+++ b/solution.py
@@ -13,6 +13,8 @@
 LANES = 128
 BLOCK_ROWS = 4
 GRAN = 16
+EXTRA = 8
+TILE = 30
 LIMIT = 5
 BF16 = jnp.bfloat16
 F32 = jnp.float32
@@ -44,13 +46,17 @@
     ids = ids_ref[...]
     mask = (ids[None] == iota((num_experts, rows, LANES), 0)).astype(F32)
 
+    steps = ((rows * LANES).bit_length() + 1) // 2
+
     def narrow(step, bound):
-        trial = bound + (2 * rows * LANES >> (step + 1))
-        admitted = jnp.where(place[None] < trial, mask, 0.0)
-        total = jnp.sum(jnp.sum(admitted, axis=1, keepdims=True), axis=2, keepdims=True)
-        return jnp.where(total <= capacity, trial, bound)
-
-    steps = (rows * LANES).bit_length()
+        unit = 4 ** (steps - 1) >> (2 * step)
+        passed = jnp.zeros_like(bound)
+        for k in range(1, 4):
+            admitted = jnp.where(place[None] < bound + k * unit, mask, 0.0)
+            total = jnp.sum(jnp.sum(admitted, axis=1, keepdims=True), axis=2, keepdims=True)
+            passed = passed + jnp.where(total <= capacity, 1, 0)
+        return bound + passed * unit
+
     bound = lax.fori_loop(0, steps, narrow, jnp.zeros((num_experts, 1, 1), jnp.int32))
     kept = jnp.where(place[None] < bound, mask, 0.0)
     kept2 = kept.reshape(num_experts * rows, LANES).astype(BF16)
@@ -160,15 +166,35 @@
 def stacked_dot(left, refs, columns):
     total, at = None, 0
     for ref in refs:
-        depth = ref.shape[0]
-        part = jnp.dot(left[:, at : at + depth], ref[:, columns], preferred_element_type=F32)
+        depth = min(ref.shape[0], left.shape[1] - at)
+        part = jnp.dot(left[:, at : at + depth], ref[0:depth, columns], preferred_element_type=F32)
         total = part if total is None else total + part
         at += depth
     return total
 
 
-def split_bias(ref, hidden):
-    return ref[:, 0:hidden].astype(F32), ref[:, hidden:].astype(F32)
+def pack_kernel(w_ref, b1_ref, b2_ref, out_ref, b1_buf, b2_buf, sems):
+    depth, hidden = w_ref.shape
+    copies = [
+        pltpu.make_async_copy(b1_ref, b1_buf, sems.at[0]),
+        pltpu.make_async_copy(b2_ref, b2_buf, sems.at[1]),
+        pltpu.make_async_copy(w_ref, out_ref.at[pl.ds(0, depth)], sems.at[2]),
+    ]
+    for copy in copies:
+        copy.start()
+    for copy in copies[:2]:
+        copy.wait()
+    b2 = b2_buf[...].astype(F32)
+    b2 = jnp.concatenate([b2, jnp.zeros((1, hidden - b2.shape[1]), F32)], axis=1)
+    row = iota((EXTRA, hidden), 0)
+    lines = jnp.where(row == 0, b1_buf[...].astype(F32), jnp.where(row == 1, b2, 0.0))
+    out_ref[depth:, :] = lines.astype(BF16)
+    copies[2].wait()
+
+
+def split_bias(ref, width):
+    lines = ref[ref.shape[0] - EXTRA :, :].astype(F32)
+    return lines[0:1], lines[1:2, 0:width]
 
 
 def up_tile(x, refs, b1, h_ref, at):
@@ -185,8 +211,16 @@
     return offset_ref[last, e] + count_ref[last, e]
 
 
-def tile_names(e, t, tile, list_ref):
-    return [list_ref[e, t * tile + k] for k in range(tile)]
+def tile_names(e, start, tile, list_ref):
+    return [list_ref[e, start + k] for k in range(tile)]
+
+
+def tile_start(t, tile, most):
+    return jnp.minimum(t * tile, most - tile)
+
+
+def tile_rows(i, start, tile, most):
+    return pl.ds(pl.multiple_of((i * most + start) * GRAN, GRAN), tile * GRAN)
 
 
 def put_rows(names, spare, y, out_ref):
@@ -196,14 +230,13 @@
 
 def expert_kernel(bits, tile, spare, count_ref, offset_ref, list_ref, xs_ref, *refs):
     count = len(bits)
-    w1_refs, w2_refs, b_refs = refs[:count], refs[count : 2 * count], refs[2 * count : 3 * count]
-    out_ref, h_buf = refs[3 * count :]
-    hidden = h_buf.shape[1]
+    w1_refs, w2_refs = refs[:count], refs[count : 2 * count]
+    out_ref, h_buf = refs[2 * count :]
     for i, e in enumerate(expert_names(bits)):
-        b1, b2 = split_bias(b_refs[i], hidden)
+        b1, b2 = split_bias(w1_refs[i], xs_ref.shape[2])
 
         def per_tile(t, _):
-            names = tile_names(e, t, tile, list_ref)
+            names = tile_names(e, t * tile, tile, list_ref)
             up_tile(jnp.concatenate([xs_ref[name] for name in names], axis=0), [w1_refs[i]], b1, h_buf, slice(None))
             y = stacked_dot(h_buf[...], [w2_refs[i]], slice(None)) + b2
             put_rows(names, spare, y.astype(BF16), out_ref)
@@ -215,15 +248,16 @@
 def up_kernel(bits, pieces, tile, most, count_ref, offset_ref, list_ref, xs_ref, *refs):
     count = len(bits)
     w1_refs = [refs[i * pieces : (i + 1) * pieces] for i in range(count)]
-    b_refs = refs[count * pieces : count * pieces + count]
-    h_ref = refs[count * pieces + count]
-    hidden = h_ref.shape[1]
+    h_ref, b2_ref = refs[count * pieces :]
+    width = b2_ref.shape[1]
     for i, e in enumerate(expert_names(bits)):
-        b1, _ = split_bias(b_refs[i], hidden)
+        b1, b2 = split_bias(w1_refs[i][-1], width)
+        b2_ref[i * EXTRA : (i + 1) * EXTRA, :] = jnp.broadcast_to(b2, (EXTRA, width))
 
         def per_tile(t, _):
-            names = tile_names(e, t, tile, list_ref)
-            at = pl.ds(pl.multiple_of((i * most + t * tile) * GRAN, tile * GRAN), tile * GRAN)
+            start = tile_start(t, tile, most)
+            names = tile_names(e, start, tile, list_ref)
+            at = tile_rows(i, start, tile, most)
             up_tile(jnp.concatenate([xs_ref[name] for name in names], axis=0), w1_refs[i], b1, h_ref, at)
             return 0
 
@@ -232,14 +266,15 @@
 
 def down_kernel(bits, first, tile, most, spare, count_ref, offset_ref, list_ref, xs_ref, h_ref, *refs):
     count = len(bits)
-    w2_refs, b_refs, out_ref = refs[:count], refs[count : 2 * count], refs[2 * count]
+    b2_ref, w2_refs, out_ref = refs[0], refs[1 : count + 1], refs[count + 1]
     del xs_ref
     for i, e in enumerate(expert_names(bits)):
-        _, b2 = split_bias(b_refs[i], h_ref.shape[1])
+        b2 = b2_ref[(first + i) * EXTRA : (first + i) * EXTRA + 1, :]
 
         def per_tile(t, _):
-            names = tile_names(e, t, tile, list_ref)
-            at = pl.ds(pl.multiple_of(((first + i) * most + t * tile) * GRAN, tile * GRAN), tile * GRAN)
+            start = tile_start(t, tile, most)
+            names = tile_names(e, start, tile, list_ref)
+            at = tile_rows(first + i, start, tile, most)
             y = stacked_dot(h_ref[at, :], [w2_refs[i]], slice(None)) + b2
             put_rows(names, spare, y.astype(BF16), out_ref)
             return 0
@@ -247,15 +282,15 @@
         lax.fori_loop(0, (granules(e, count_ref, offset_ref) + tile - 1) // tile, per_tile, 0)
 
 
-def compact_down(total, tile, window, w2_refs, b_ref, h_ref, y_ref, after=lambda t, state: state):
+def compact_down(total, tile, most, window, w2_refs, b2_ref, h_ref, y_ref, after=lambda t, state: state):
     width = y_ref.shape[2]
-    _, b2 = split_bias(b_ref, h_ref.shape[1])
+    b2 = b2_ref[0:1, :]
 
     def per_tile(t, state):
-        at = pl.ds(pl.multiple_of(t * tile * GRAN, tile * GRAN), tile * GRAN)
-        y = stacked_dot(h_ref[at, :], w2_refs, slice(None)) + b2
-        y_ref[pl.ds(t * tile, tile)] = y.astype(BF16).reshape(tile, GRAN, width)
-        y_ref[pl.ds((t + 1) * tile, window)] = jnp.zeros((window, GRAN, width), BF16)
+        start = tile_start(t, tile, most)
+        y = stacked_dot(h_ref[tile_rows(0, start, tile, most), :], w2_refs, slice(None)) + b2
+        y_ref[pl.ds(start, tile)] = y.astype(BF16).reshape(tile, GRAN, width)
+        y_ref[pl.ds(start + tile, window)] = jnp.zeros((window, GRAN, width), BF16)
         return after(t, state)
 
     tiles = (total + tile - 1) // tile
@@ -267,12 +302,12 @@
     return lax.fori_loop(0, tiles, per_tile, jnp.int32(0))
 
 
-def half_kernel(bits, tile, window, count_ref, offset_ref, h_ref, *refs):
+def half_kernel(bits, tile, most, window, count_ref, offset_ref, h_ref, *refs):
     total = granules(expert_names(bits)[0], count_ref, offset_ref)
-    compact_down(total, tile, window, refs[:-2], refs[-2], h_ref, refs[-1])
-
-
-def final_kernel(bits, tile, window, start_ref, count_ref, offset_ref, slot_ref, gate_ref, h_ref, part_ref, y_ref, *refs):
+    compact_down(total, tile, most, window, refs[:-2], refs[-2], h_ref, refs[-1])
+
+
+def final_kernel(bits, tile, most, window, start_ref, count_ref, offset_ref, slot_ref, gate_ref, h_ref, part_ref, y_ref, *refs):
     experts = expert_names(bits)
     out_ref, y_buf, o_buf, o_sem = refs[-4:]
     y_refs = (y_ref, y_buf)
@@ -285,17 +320,18 @@
         at = jnp.minimum(offset_ref[b, experts[i]] + w * window, totals[i])
         return y_refs[i][pl.ds(at, window)].reshape(window * GRAN, width)
 
-    def out_copy(pair, slot):
-        rows = pl.ds(pl.multiple_of(pair * 2 * block_tok, 2 * block_tok), 2 * block_tok)
-        return pltpu.make_async_copy(o_buf.at[slot], out_ref.at[rows], o_sem.at[slot])
+    def out_copy(b, turn, sub):
+        rows = pl.ds(pl.multiple_of(b * block_tok, block_tok), block_tok)
+        part = o_buf.at[turn, pl.ds(sub * block_tok, block_tok)]
+        return pltpu.make_async_copy(part, out_ref.at[rows], o_sem.at[turn, sub])
 
     def add(b, w, sub, turn, slots, gates, base_ref, base_at):
         part = slice(sub * BLOCK_ROWS, (sub + 1) * BLOCK_ROWS)
         back = window_dot(experts, w, b, start_ref, count_ref, over_lanes(slots[part]), rows_of)
         gate = over_lanes(gates[part])
         for c in range(0, width, LANES):
-            base = base_ref[base_at, c : c + LANES].astype(F32)
-            o_buf[turn, sub * block_tok : (sub + 1) * block_tok, c : c + LANES] = (base + back[:, c : c + LANES] * gate).astype(BF16)
+            scaled = (back[:, c : c + LANES] * gate).astype(BF16)
+            o_buf[turn, sub * block_tok : (sub + 1) * block_tok, c : c + LANES] = base_ref[base_at, c : c + LANES] + scaled
 
     def per_pair(pair, _):
         turn = pair % 2
@@ -304,7 +340,8 @@
 
         @pl.when(pair >= 2)
         def _():
-            out_copy(pair, turn).wait()
+            for sub in range(2):
+                out_copy(2 * pair + sub, turn, sub).wait()
 
         for sub in range(2):
             b = 2 * pair + sub
@@ -317,7 +354,7 @@
                 return 0
 
             lax.fori_loop(1, (longest_run(experts, b, count_ref) + window - 1) // window, more, 0)
-        out_copy(pair, turn).start()
+            out_copy(b, turn, sub).start()
         return 0
 
     def ready_pairs(t, done):
@@ -328,10 +365,11 @@
         lax.fori_loop(done, ready, per_pair, 0)
         return ready
 
-    done = compact_down(totals[-1], tile, window, refs[:-5], refs[-5], h_ref, y_buf, ready_pairs)
+    done = compact_down(totals[-1], tile, most, window, refs[:-5], refs[-5], h_ref, y_buf, ready_pairs)
     lax.fori_loop(done, blocks // 2, per_pair, 0)
-    for slot in range(2):
-        out_copy(0, slot).wait()
+    for turn in range(2):
+        for sub in range(2):
+            out_copy(0, turn, sub).wait()
 
 
 def window_dot(experts, w, b, start_ref, count_ref, slot, rows_of):
@@ -365,10 +403,10 @@
         back = window_dot(experts, w, b, start_ref, count_ref, slot, rows_of)
         at = pl.ds(pl.multiple_of(b * block_tok, block_tok), block_tok)
         for c in range(0, width, LANES):
-            scaled = back[:, c : c + LANES] * gate
+            scaled = (back[:, c : c + LANES] * gate).astype(BF16)
             if not fresh:
-                scaled = scaled + out_ref[at, c : c + LANES].astype(F32)
-            out_ref[at, c : c + LANES] = scaled.astype(BF16)
+                scaled = scaled + out_ref[at, c : c + LANES]
+            out_ref[at, c : c + LANES] = scaled
 
     def per_group(group, _):
         row0 = pl.multiple_of(group * 4 * BLOCK_ROWS, 4 * BLOCK_ROWS)
@@ -420,12 +458,19 @@
         slots = -(-(BLOCK_ROWS * LANES + num_experts * (GRAN - 1)) // LANES) * LANES
         span = slots // GRAN
 
-        first, second = w_in[0], w_out[0]
+        second = w_out[0]
+        first = pl.pallas_call(
+            pack_kernel,
+            out_shape=pltpu.VMEM((width + EXTRA, hidden), BF16),
+            in_specs=[hbm()] * 3,
+            out_specs=vmem(),
+            scratch_shapes=[pltpu.VMEM((1, hidden), BF16), pltpu.VMEM((1, width), BF16), pltpu.SemaphoreType.DMA((3,))],
+            compiler_params=pltpu.CompilerParams(vmem_limit_bytes=LIMIT * 2**20),
+            name="pack",
+        )(*[pltpu.with_memory_space_constraint(array, pltpu.HBM) for array in (w_in[0], b_in, b_out)])
         x_first, y_first = swap(first, 2), swap(first, 4)
         x_second, y_second = swap(second, 2), swap(second, 4)
         c_first, c_second = swap(first, 1), swap(second, 1)
-        own_bias = jnp.concatenate([b_in, b_out], axis=1)
-        bias = [own_bias] + [swap(own_bias, bit) for bit in range(1, num_experts)]
 
         ids, order = expert_ids.reshape(rows, LANES), route_order.reshape(rows, LANES)
         unit = 2 * BLOCK_ROWS
@@ -463,8 +508,8 @@
             name="dispatch",
         )(value_a11.reshape(1, 1), *[pltpu.with_memory_space_constraint(array, pltpu.HBM) for array in (ids, order, w_route, expert_keys, tokens[0])])
 
-        most = -(-(capacity + blocks * (GRAN - 1)) // (32 * GRAN)) * 32
-        tile, window = 32, 8
+        most = -(-(capacity + blocks * (GRAN - 1)) // (16 * GRAN)) * 16
+        tile, window = TILE, 8
         held = lambda array: pltpu.with_memory_space_constraint(array, pltpu.VMEM)
 
         spare = blocks * span
@@ -479,23 +524,23 @@
             pieces = len(firsts[0])
             return pl.pallas_call(
                 functools.partial(up_kernel, bits, pieces, tile, most),
-                out_shape=pltpu.VMEM((n * most * GRAN, hidden), BF16),
-                in_specs=[smem()] * 3 + [vmem()] * (1 + n * pieces + n),
-                out_specs=vmem(),
+                out_shape=(pltpu.VMEM((n * most * GRAN, hidden), BF16), jax.ShapeDtypeStruct((n * EXTRA, width), F32)),
+                in_specs=[smem()] * 3 + [vmem()] * (1 + n * pieces),
+                out_specs=(vmem(), vmem()),
                 cost_estimate=cost(2 * n * 10**9),
                 compiler_params=limit,
-            )(*tables, held(xs), *[held(piece) for expert in firsts for piece in expert], *[bias[bit] for bit in bits])
-
-        def down(bits, place, xs, h, seconds):
+            )(*tables, held(xs), *[held(piece) for expert in firsts for piece in expert])
+
+        def down(bits, place, xs, h, b2, seconds):
             return pl.pallas_call(
                 functools.partial(down_kernel, bits, place, tile, most, spare),
                 out_shape=pltpu.VMEM(xs.shape, BF16),
-                in_specs=[smem()] * 3 + [vmem()] * (2 + 2 * len(bits)),
+                in_specs=[smem()] * 3 + [vmem()] * (3 + len(bits)),
                 out_specs=vmem(),
                 input_output_aliases={3: 0},
                 cost_estimate=cost(2 * len(bits) * 10**9),
                 compiler_params=limit,
-            )(*tables, held(xs), held(h), *map(held, seconds), *[bias[bit] for bit in bits])
+            )(*tables, held(xs), held(h), b2, *map(held, seconds))
 
         def partial(bits, xs, part):
             held_part = [] if part is None else [held(part)]
@@ -509,60 +554,60 @@
                 compiler_params=limit,
             )(starts, counts, held(xs), slot, gate, *held_part)
 
+        xs = pl.pallas_call(
+            functools.partial(expert_kernel, (0, 1), tile, spare),
+            out_shape=pltpu.VMEM(xs.shape, BF16),
+            in_specs=[smem()] * 3 + [vmem()] * 5,
+            out_specs=vmem(),
+            scratch_shapes=[pltpu.VMEM((tile * GRAN, hidden), BF16)],
+            input_output_aliases={3: 0},
+            cost_estimate=cost(6 * 10**9),
+            compiler_params=pltpu.CompilerParams(vmem_limit_bytes=2 * LIMIT * 2**20),
+            name="experts0",
+        )(*tables, held(xs), held(first), held(c_first), held(second), held(c_second))
         x_first, y_first, xs = lax.optimization_barrier((x_first, y_first, xs))
         cut = width - LANES
         d_top, d_low = swap(x_first[:cut], 4), swap(y_first[cut:], 2)
         cx_first, cy_first = swap(x_first, 1), swap(y_first, 1)
-        xs = pl.pallas_call(
-            functools.partial(expert_kernel, (0, 1), tile, spare),
-            out_shape=pltpu.VMEM(xs.shape, BF16),
-            in_specs=[smem()] * 3 + [vmem()] * 7,
-            out_specs=vmem(),
-            scratch_shapes=[pltpu.VMEM((tile * GRAN, hidden), BF16)],
-            input_output_aliases={3: 0},
-            cost_estimate=cost(6 * 10**9),
-            compiler_params=limit,
-            name="experts0",
-        )(*tables, held(xs), held(first), held(c_first), held(second), held(c_second), bias[0], bias[1])
-        h = up((2, 4, 3, 5), xs, ((x_first,), (y_first,), (cx_first,), (cy_first,)))
+        h, b2 = up((2, 4, 3, 5), xs, ((x_first,), (y_first,), (cx_first,), (cy_first,)))
         part = partial((0, 1), xs, None)
         x_second, y_second, h, part = lax.optimization_barrier((x_second, y_second, h, part))
         edge = hidden // 3
         e_top, e_low = swap(x_second[:edge], 4), swap(y_second[edge:], 2)
         cx_second, cy_second = swap(x_second, 1), swap(y_second, 1)
-        xs = down((2, 4), 0, xs, h, (x_second, y_second))
-        xs = down((3, 5), 2, xs, h, (cx_second, cy_second))
+        xs = down((2, 4), 0, xs, h, b2, (x_second, y_second))
+        xs = down((3, 5), 2, xs, h, b2, (cx_second, cy_second))
         part = partial((2, 4, 3, 5), xs, part)
         d_top, d_low, part = lax.optimization_barrier((d_top, d_low, part))
         cd_top, cd_low = swap(d_top, 1), swap(d_low, 1)
-        h6 = up((6,), xs, ((d_top, d_low),))
+        h6, b6 = up((6,), xs, ((d_top, d_low),))
         h6, cd_top, cd_low = lax.optimization_barrier((h6, cd_top, cd_low))
-        h7 = up((7,), xs, ((cd_top, cd_low),))
+        h7, b7 = up((7,), xs, ((cd_top, cd_low),))
         e_top, e_low, h6, h7 = lax.optimization_barrier((e_top, e_low, h6, h7))
         ce_top, ce_low = swap(e_top, 1), swap(e_low, 1)
         y = pl.pallas_call(
-            functools.partial(half_kernel, (6,), tile, window),
+            functools.partial(half_kernel, (6,), tile, most, window),
             out_shape=pltpu.VMEM((most + window, GRAN, width), BF16),
             in_specs=[smem()] * 2 + [vmem()] * 4,
             out_specs=vmem(),
             cost_estimate=cost(2 * 10**9),
             compiler_params=limit,
             name="half",
-        )(counts, offsets, held(h6), held(e_top), held(e_low), bias[6])
+        )(counts, offsets, held(h6), held(e_top), held(e_low), b6)
         out = pl.pallas_call(
-            functools.partial(final_kernel, (6, 7), tile, window),
+            functools.partial(final_kernel, (6, 7), tile, most, window),
             out_shape=jax.ShapeDtypeStruct((tok_dev, width), BF16),
             in_specs=[smem()] * 3 + [vmem()] * (5 + 3),
             out_specs=hbm(),
             scratch_shapes=[
                 pltpu.VMEM((most + window, GRAN, width), BF16),
                 pltpu.VMEM((2, 2 * BLOCK_ROWS * LANES, width), BF16),
-                pltpu.SemaphoreType.DMA((2,)),
+                pltpu.SemaphoreType.DMA((2, 2)),
             ],
             cost_estimate=cost(5 * 10**9),
             compiler_params=pltpu.CompilerParams(vmem_limit_bytes=7 * 2**20),
             name="final",
-        )(starts, counts, offsets, slot, gate, held(h7), held(part), held(y), held(ce_top), held(ce_low), bias[7])
+        )(starts, counts, offsets, slot, gate, held(h7), held(part), held(y), held(ce_top), held(ce_low), b7)
         return out[None]
 
     return jax.shard_map(

time: 143 us -> 119 us (0.83)
  waiting for transfers between devices: 41.3 us -> 23.5 us
  starting transfers between devices: 21.5 us -> 15 us
    ppermute x25 -> x18, waiting for transfers between devices: 41.3 us -> 23.5 us  [swap(): lax.ppermute(value, EXPERT_AXES, [(e, e ^ bit) for e in range(num_experts)])]
    ppermute x25 -> x18, starting transfers between devices: 21.5 us -> 15 us  [swap(): lax.ppermute(value, EXPERT_AXES, [(e, e ^ bit) for e in range(num_experts)])]
    pallas_call x2 -> x3, Pallas kernels: 11.5 us -> 12.6 us  [the longest x1 8.56 us: inner_step(): pl.pallas_call(functools.partial(final_kernel, (6, 7), tile, most, window...]
  transfers between devices with their start and end apart: 25 -> 18, of which waited for: 9 -> 5; matrix products, arithmetic and copies ran while one was open for 0% -> 1% of each run, Pallas kernels for 49% -> 57%
where the time goes in v4:
time: 119 us
  Pallas kernels  77.8 us (65%)
  waiting for transfers between devices  23.5 us (20%)
  starting transfers between devices  15 us (13%)
  local copies, waits for them, and re-layouts  1.2 us (1%)
    ppermute x18, waiting for transfers between devices, swap(): lax.ppermute(value, EXPERT_AXES, [(e, e ^ bit) for e in range(num_experts)])  23.5 us
    pallas_call x3, Pallas kernels, up(): pl.pallas_call(functools.partial(up_kernel, bits, pieces, tile, most), ou...  16.9 us
    pallas_call x1, Pallas kernels, inner_step(): pl.pallas_call(functools.partial(dispatch_kernel, router, num_experts, ca...  16.5 us
    ppermute x18, starting transfers between devices, swap(): lax.ppermute(value, EXPERT_AXES, [(e, e ^ bit) for e in range(num_experts)])  15 us
    pallas_call x1, Pallas kernels, inner_step(): pl.pallas_call(functools.partial(expert_kernel, (0, 1), tile, spare), out...  10.8 us
    pallas_call x2, Pallas kernels, partial(): pl.pallas_call(functools.partial(part_kernel, bits, part is None, window,...  10.6 us
    pallas_call x2, Pallas kernels, down(): pl.pallas_call(functools.partial(down_kernel, bits, place, tile, most, sp...  10.3 us
    pallas_call x1, Pallas kernels, inner_step(): pl.pallas_call(functools.partial(final_kernel, (6, 7), tile, most, window...  8.56 us
  transfers between devices with their start and end apart: 18, of which 5 were waited for; matrix products, arithmetic and copies ran while one was open for 1% of the time, Pallas kernels for 57%

profile of v4, /device:TPU:0, one launch (start us, length us, event | category | flops | bytes accessed | tf_op | source)
XLA Modules:
  0.0 118.5 jit_solution(16534179315826712093)
XLA Ops:
  0.0 1.3 %pack.1.refs_0_ = bf16[392,1536]{1,0:T(8,128)(2,1)S(1)} custom-call(bf16[384,1536]{1,0:T(8,128)(2,1)} %bitcast.8, bf16[1,1536]{1,0:T(2,128)(2,1)} %b1_ref.1, bf16[1,384]{1,0:T(2,128)(2,1)} %b2_ref.1), custom_call_target="tpu_custom_call" | custom-call | tf_op jit(solution)/shard_map/pack/pallas_call | solution.py:462
  1.3 0.9 collective-permute-start.4
  2.2 3.0 %collective-permute-start.3 = (bf16[392,1536]{1,0:T(8,128)(2,1)S(1)}, bf16[392,1536]{1,0:T(8,128)(2,1)}, u32[]{:S(2)}, u32[]{:S(2)}) collective-permute-start(bf16[392,1536]{1,0:T(8,128)(2,1)S(1)} %pack.1.refs_0_), channel_id=1, source_target_pairs={{0,4},{1,5},{2,6},{3,7},{4,0},{5,1},{6,2},{7,3}} | collective-permute-start | bytes 3612680 | tf_op jit(solution)/shard_map/ppermute | solution.py:449
  5.2 1.5 %collective-permute-start.2 = (bf16[392,1536]{1,0:T(8,128)(2,1)S(1)}, bf16[392,1536]{1,0:T(8,128)(2,1)S(1)}, u32[]{:S(2)}, u32[]{:S(2)}) collective-permute-start(bf16[392,1536]{1,0:T(8,128)(2,1)S(1)} %pack.1.refs_0_), channel_id=1, source_target_pairs={{0,2},{1,3},{2,0},{3,1},{4,6},{5,7},{6,4},{7,5}} | collective-permute-start | bytes 3612680 | tf_op jit(solution)/shard_map/ppermute | solution.py:449
  7.3 16.5 %dispatch.1 = (s32[16,128]{1,0:T(8,128)S(1)}, s32[16,128]{1,0:T(8,128)S(1)}, s32[16,128]{1,0:T(8,128)S(1)}, s32[8,128]{1,0:T(8,128)S(1)}, s32[64,128]{1,0:T(8,12...) custom-call(f32[1,1]{1,0:T(1,128)} %bitcast.7.tau_ref, s32[64,128]{1,0:T(8,128)} %bitcast.10, ...), custom_call_target="tpu_custom_call" | custom-call | flops 8999999488 | bytes 14000000 | tf_op jit(solution)/shard_map/dispatch/pallas_call | solution.py:481
  23.9 10.8 %experts0.1.xs_ref = bf16[656,16,384]{2,1,0:T(8,128)(2,1)S(1)} custom-call(s32[16,128]{1,0:T(8,128)S(1)} %get-tuple-element.36.count_ref, s32[16,128]{1,0:T(8,128)S(1)} %get-tuple-element.37.offset_ref, s32[8,128]{1,0:T(8,128)S(1)} %get-tuple-element.40.list_ref, bf16[656,16,384]{2,1,0:T(8,128)(2,1)S(1)} %get-tuple-element.41.xs_ref, ...), custom_call_target="tpu_custom_call", output_to_operand_aliasing={{}: (3, {})} | custom-call | flops 6000000000 | bytes 1000000 | tf_op jit(solution)/shard_map/experts0/pallas_call | solution.py:557
  35.3 2.3 %collective-permute-start = (bf16[1536,384]{1,0:T(8,128)(2,1)}, bf16[1536,384]{1,0:T(8,128)(2,1)S(1)}, u32[]{:S(2)}, u32[]{:S(2)}) collective-permute-start(bf16[1536,384]{1,0:T(8,128)(2,1)} %bitcast.4.refs_2_), channel_id=1, source_target_pairs={{0,2},{1,3},{2,0},{3,1},{4,6},{5,7},{6,4},{7,5}} | collective-permute-start | bytes 3538952 | tf_op jit(solution)/shard_map/ppermute | solution.py:449
  37.6 4.1 %shard_map.101.refs_0_ = bf16[8192,384]{1,0:T(8,128)(2,1)S(1)} custom-call(s32[16,128]{1,0:T(8,128)S(1)} %get-tuple-element.35.start_ref, s32[16,128]{1,0:T(8,128)S(1)} %get-tuple-element.36.count_ref, bf16[656,16,384]{2,1,0:T(8,128)(2,1)S(1)} %experts0.1.xs_ref, s32[64,128]{1,0:T(8,128)S(1)} %get-tuple-element.38.slot_ref, ...), custom_call_target="tpu_custom_call" | custom-call | flops 4000000000 | bytes 1000000 | tf_op jit(solution)/shard_map/pallas_call | solution.py:547
  41.7 10.8 %shard_map.100 = (bf16[6144,1536]{1,0:T(8,128)(2,1)S(1)}, f32[32,384]{1,0:T(8,128)S(1)}) custom-call(s32[16,128]{1,0:T(8,128)S(1)} %get-tuple-element.36.count_ref, s32[16,128]{1,0:T(8,128)S(1)} %get-tuple-element.37.offset_ref, s32[8,128]{1,0:T(8,128)S(1)} %get-tuple-element.40.list_ref, bf16[656,16,384]{2,1,0:T(8,128)(2,1)S(1)} %experts0.1.xs_ref, ...), custom_call_target="tpu_custom_call" | custom-call | flops 8000000000 | bytes 1000000 | tf_op jit(solution)/shard_map/pallas_call | solution.py:525
  52.6 10.8 %collective-permute-done.1.refs_2_ = bf16[1536,384]{1,0:T(8,128)(2,1)S(1)} collective-permute-done((bf16[1536,384]{1,0:T(8,128)(2,1)}, bf16[1536,384]{1,0:T(8,128)(2,1)S(1)}, u32[]{:S(2)}, u32[]{:S(2)}) %collective-permute-start.1) | collective-permute-done | bytes 1179680 | tf_op jit(solution)/shard_map/ppermute | solution.py:449
  63.4 0.6 collective-permute-done.refs_1_
  64.5 1.0 slice.15
  65.6 1.7 %collective-permute-start.13 = (bf16[136,1536]{1,0:T(8,128)(2,1)S(1)}, bf16[136,1536]{1,0:T(8,128)(2,1)S(1)}, u32[]{:S(2)}, u32[]{:S(2)}) collective-permute-start(bf16[136,1536]{1,0:T(8,128)(2,1)S(1)} %slice.15), channel_id=1, source_target_pairs={{0,2},{1,3},{2,0},{3,1},{4,6},{5,7},{6,4},{7,5}} | collective-permute-start | bytes 1253384 | tf_op jit(solution)/shard_map/ppermute | solution.py:449
  67.3 1.7 %collective-permute-start.12 = (bf16[256,1536]{1,0:T(8,128)(2,1)S(1)}, bf16[256,1536]{1,0:T(8,128)(2,1)S(1)}, u32[]{:S(2)}, u32[]{:S(2)}) collective-permute-start(bf16[256,1536]{1,0:T(8,128)(2,1)S(1)} %slice.14), channel_id=1, source_target_pairs={{0,4},{1,5},{2,6},{3,7},{4,0},{5,1},{6,2},{7,3}} | collective-permute-start | bytes 2359304 | tf_op jit(solution)/shard_map/ppermute | solution.py:449
  69.0 5.7 %shard_map.102.xs_ref = bf16[656,16,384]{2,1,0:T(8,128)(2,1)S(1)} custom-call(s32[16,128]{1,0:T(8,128)S(1)} %get-tuple-element.36.count_ref, s32[16,128]{1,0:T(8,128)S(1)} %get-tuple-element.37.offset_ref, s32[8,128]{1,0:T(8,128)S(1)} %get-tuple-element.40.list_ref, bf16[656,16,384]{2,1,0:T(8,128)(2,1)S(1)} %experts0.1.xs_ref, ...), custom_call_target="tpu_custom_call", output_to_operand_aliasing={{}: (3, {})} | custom-call | flops 4000000000 | bytes 1000000 | tf_op jit(solution)/shard_map/pallas_call | solution.py:535
  74.8 4.6 %shard_map.103.xs_ref = bf16[656,16,384]{2,1,0:T(8,128)(2,1)S(1)} custom-call(s32[16,128]{1,0:T(8,128)S(1)} %get-tuple-element.36.count_ref, s32[16,128]{1,0:T(8,128)S(1)} %get-tuple-element.37.offset_ref, s32[8,128]{1,0:T(8,128)S(1)} %get-tuple-element.40.list_ref, bf16[656,16,384]{2,1,0:T(8,128)(2,1)S(1)} %shard_map.102.xs_ref, ...), custom_call_target="tpu_custom_call", output_to_operand_aliasing={{}: (3, {})} | custom-call | flops 4000000000 | bytes 1000000 | tf_op jit(solution)/shard_map/pallas_call | solution.py:535
  79.4 6.5 %shard_map.104.part_ref = bf16[8192,384]{1,0:T(8,128)(2,1)S(1)} custom-call(s32[16,128]{1,0:T(8,128)S(1)} %get-tuple-element.35.start_ref, s32[16,128]{1,0:T(8,128)S(1)} %get-tuple-element.36.count_ref, bf16[656,16,384]{2,1,0:T(8,128)(2,1)S(1)} %shard_map.103.xs_ref, s32[64,128]{1,0:T(8,128)S(1)} %get-tuple-element.38.slot_ref, ...), custom_call_target="tpu_custom_call", output_to_operand_aliasing={{}: (5, {})} | custom-call | flops 8000000000 | bytes 1000000 | tf_op jit(solution)/shard_map/pallas_call | solution.py:547
  87.2 1.8 %collective-permute-start.8 = (bf16[512,384]{1,0:T(8,128)(2,1)S(1)}, bf16[512,384]{1,0:T(8,128)(2,1)S(1)}, u32[]{:S(2)}, u32[]{:S(2)}) collective-permute-start(bf16[512,384]{1,0:T(8,128)(2,1)S(1)} %slice.12), channel_id=1, source_target_pairs={{0,4},{1,5},{2,6},{3,7},{4,0},{5,1},{6,2},{7,3}} | collective-permute-start | bytes 1179656 | tf_op jit(solution)/shard_map/ppermute | solution.py:449
  88.9 3.0 %shard_map.105 = (bf16[1536,1536]{1,0:T(8,128)(2,1)S(1)}, f32[8,384]{1,0:T(8,128)S(1)}) custom-call(s32[16,128]{1,0:T(8,128)S(1)} %get-tuple-element.36.count_ref, s32[16,128]{1,0:T(8,128)S(1)} %get-tuple-element.37.offset_ref, s32[8,128]{1,0:T(8,128)S(1)} %get-tuple-element.40.list_ref, bf16[656,16,384]{2,1,0:T(8,128)(2,1)S(1)} %shard_map.103.xs_ref, ...), custom_call_target="tpu_custom_call" | custom-call | flops 2000000000 | bytes 1000000 | tf_op jit(solution)/shard_map/pallas_call | solution.py:525
  92.0 3.0 %shard_map.106 = (bf16[1536,1536]{1,0:T(8,128)(2,1)S(1)}, f32[8,384]{1,0:T(8,128)S(1)}) custom-call(s32[16,128]{1,0:T(8,128)S(1)} %get-tuple-element.36.count_ref, s32[16,128]{1,0:T(8,128)S(1)} %get-tuple-element.37.offset_ref, s32[8,128]{1,0:T(8,128)S(1)} %get-tuple-element.40.list_ref, bf16[656,16,384]{2,1,0:T(8,128)(2,1)S(1)} %shard_map.103.xs_ref, ...), custom_call_target="tpu_custom_call" | custom-call | flops 2000000000 | bytes 1000000 | tf_op jit(solution)/shard_map/pallas_call | solution.py:525
  95.0 3.5 %collective-permute-done.8.refs_0_ = bf16[512,384]{1,0:T(8,128)(2,1)S(1)} collective-permute-done((bf16[512,384]{1,0:T(8,128)(2,1)S(1)}, bf16[512,384]{1,0:T(8,128)(2,1)S(1)}, u32[]{:S(2)}, u32[]{:S(2)}) %collective-permute-start.8) | collective-permute-done | bytes 393248 | tf_op jit(solution)/shard_map/ppermute | solution.py:449
  98.5 8.0 %collective-permute-done.9.refs_1_ = bf16[1024,384]{1,0:T(8,128)(2,1)S(1)} collective-permute-done((bf16[1024,384]{1,0:T(8,128)(2,1)S(1)}, bf16[1024,384]{1,0:T(8,128)(2,1)S(1)}, u32[]{:S(2)}, u32[]{:S(2)}) %collective-permute-start.9) | collective-permute-done | bytes 786464 | tf_op jit(solution)/shard_map/ppermute | solution.py:449
  107.0 2.7 %half.1.y_ref = bf16[104,16,384]{2,1,0:T(8,128)(2,1)S(1)} custom-call(s32[16,128]{1,0:T(8,128)S(1)} %get-tuple-element.36.count_ref, s32[16,128]{1,0:T(8,128)S(1)} %get-tuple-element.37.offset_ref, bf16[1536,1536]{1,0:T(8,128)(2,1)S(1)} %get-tuple-element.60.h_ref, bf16[512,384]{1,0:T(8,128)(2,1)S(1)} %collective-permute-done.8.refs_0_, ...), custom_call_target="tpu_custom_call" | custom-call | flops 2000000000 | bytes 1000000 | tf_op jit(solution)/shard_map/half/pallas_call | solution.py:588
  109.8 8.6 %final.1 = bf16[8192,384]{1,0:T(8,128)(2,1)} custom-call(s32[16,128]{1,0:T(8,128)S(1)} %get-tuple-element.35.start_ref, s32[16,128]{1,0:T(8,128)S(1)} %get-tuple-element.36.count_ref, s32[16,128]{1,0:T(8,128)S(1)} %get-tuple-element.37.offset_ref, s32[64,128]{1,0:T(8,128)S(1)} %get-tuple-element.38.slot_ref, f32[64,128]{1,0:T(8,128)S(1)} %get-tuple-element.39.gate_ref, ...), custom_call_target="tpu_custom_call" | custom-call | flops 5000000000 | bytes 1000000 | tf_op jit(solution)/shard_map/final/pallas_call | solution.py:597
  (28 shorter events, 2.9 us)
Async XLA Ops:
  1.3 22.5 %collective-permute-start.4 = (bf16[392,1536]{1,0:T(8,128)(2,1)S(1)}, bf16[392,1536]{1,0:T(8,128)(2,1)}, u32[]{:S(2)}, u32[]{:S(2)}) collective-permute-start(bf16[392,1536]{1,0:T(8,128)(2,1)S(1)} %pack.1.refs_0_), channel_id=1, source_target_pairs={{0,1},{1,0},{2,3},{3,2},{4,5},{5,4},{6,7},{7,6}} | collective-permute-start | bytes 3612680 | tf_op jit(solution)/shard_map/ppermute | solution.py:449
  2.2 21.7 %collective-permute-start.5 = (bf16[1536,384]{1,0:T(8,128)(2,1)}, bf16[1536,384]{1,0:T(8,128)(2,1)}, u32[]{:S(2)}, u32[]{:S(2)}) collective-permute-start(bf16[1536,384]{1,0:T(8,128)(2,1)} %bitcast.4.refs_2_), channel_id=1, source_target_pairs={{0,1},{1,0},{2,3},{3,2},{4,5},{5,4},{6,7},{7,6}} | collective-permute-start | bytes 3538952 | tf_op jit(solution)/shard_map/ppermute | solution.py:449
  2.2 32.5 %collective-permute-start.3 = (bf16[392,1536]{1,0:T(8,128)(2,1)S(1)}, bf16[392,1536]{1,0:T(8,128)(2,1)}, u32[]{:S(2)}, u32[]{:S(2)}) collective-permute-start(bf16[392,1536]{1,0:T(8,128)(2,1)S(1)} %pack.1.refs_0_), channel_id=1, source_target_pairs={{0,4},{1,5},{2,6},{3,7},{4,0},{5,1},{6,2},{7,3}} | collective-permute-start | bytes 3612680 | tf_op jit(solution)/shard_map/ppermute | solution.py:449
  5.2 29.5 %collective-permute-start.2 = (bf16[392,1536]{1,0:T(8,128)(2,1)S(1)}, bf16[392,1536]{1,0:T(8,128)(2,1)S(1)}, u32[]{:S(2)}, u32[]{:S(2)}) collective-permute-start(bf16[392,1536]{1,0:T(8,128)(2,1)S(1)} %pack.1.refs_0_), channel_id=1, source_target_pairs={{0,2},{1,3},{2,0},{3,1},{4,6},{5,7},{6,4},{7,5}} | collective-permute-start | bytes 3612680 | tf_op jit(solution)/shard_map/ppermute | solution.py:449
  34.7 7.0 %collective-permute-start.6 = (bf16[392,1536]{1,0:T(8,128)(2,1)S(1)}, bf16[392,1536]{1,0:T(8,128)(2,1)S(1)}, u32[]{:S(2)}, u32[]{:S(2)}) collective-permute-start(bf16[392,1536]{1,0:T(8,128)(2,1)S(1)} %collective-permute-done.2.refs_0_), channel_id=1, source_target_pairs={{0,1},{1,0},{2,3},{3,2},{4,5},{5,4},{6,7},{7,6}} | collective-permute-start | bytes 3612680 | tf_op jit(solution)/shard_map/ppermute | solution.py:449
  34.8 6.9 %collective-permute-start.7 = (bf16[392,1536]{1,0:T(8,128)(2,1)}, bf16[392,1536]{1,0:T(8,128)(2,1)S(1)}, u32[]{:S(2)}, u32[]{:S(2)}) collective-permute-start(bf16[392,1536]{1,0:T(8,128)(2,1)} %collective-permute-done.3.refs_1_), channel_id=1, source_target_pairs={{0,1},{1,0},{2,3},{3,2},{4,5},{5,4},{6,7},{7,6}} | collective-permute-start | bytes 3612680 | tf_op jit(solution)/shard_map/ppermute | solution.py:449
  35.3 28.1 %collective-permute-start.1 = (bf16[1536,384]{1,0:T(8,128)(2,1)}, bf16[1536,384]{1,0:T(8,128)(2,1)S(1)}, u32[]{:S(2)}, u32[]{:S(2)}) collective-permute-start(bf16[1536,384]{1,0:T(8,128)(2,1)} %bitcast.4.refs_2_), channel_id=1, source_target_pairs={{0,4},{1,5},{2,6},{3,7},{4,0},{5,1},{6,2},{7,3}} | collective-permute-start | bytes 3538952 | tf_op jit(solution)/shard_map/ppermute | solution.py:449
  35.3 28.7 %collective-permute-start = (bf16[1536,384]{1,0:T(8,128)(2,1)}, bf16[1536,384]{1,0:T(8,128)(2,1)S(1)}, u32[]{:S(2)}, u32[]{:S(2)}) collective-permute-start(bf16[1536,384]{1,0:T(8,128)(2,1)} %bitcast.4.refs_2_), channel_id=1, source_target_pairs={{0,2},{1,3},{2,0},{3,1},{4,6},{5,7},{6,4},{7,5}} | collective-permute-start | bytes 3538952 | tf_op jit(solution)/shard_map/ppermute | solution.py:449
  64.0 10.8 %collective-permute-start.10 = (bf16[1536,384]{1,0:T(8,128)(2,1)S(1)}, bf16[1536,384]{1,0:T(8,128)(2,1)S(1)}, u32[]{:S(2)}, u32[]{:S(2)}) collective-permute-start(bf16[1536,384]{1,0:T(8,128)(2,1)S(1)} %collective-permute-done.refs_1_), channel_id=1, source_target_pairs={{0,1},{1,0},{2,3},{3,2},{4,5},{5,4},{6,7},{7,6}} | collective-permute-start | bytes 3538952 | tf_op jit(solution)/shard_map/ppermute | solution.py:449
  64.0 10.8 %collective-permute-start.11 = (bf16[1536,384]{1,0:T(8,128)(2,1)S(1)}, bf16[1536,384]{1,0:T(8,128)(2,1)S(1)}, u32[]{:S(2)}, u32[]{:S(2)}) collective-permute-start(bf16[1536,384]{1,0:T(8,128)(2,1)S(1)} %collective-permute-done.1.refs_2_), channel_id=1, source_target_pairs={{0,1},{1,0},{2,3},{3,2},{4,5},{5,4},{6,7},{7,6}} | collective-permute-start | bytes 3538952 | tf_op jit(solution)/shard_map/ppermute | solution.py:449
  65.6 20.4 %collective-permute-start.13 = (bf16[136,1536]{1,0:T(8,128)(2,1)S(1)}, bf16[136,1536]{1,0:T(8,128)(2,1)S(1)}, u32[]{:S(2)}, u32[]{:S(2)}) collective-permute-start(bf16[136,1536]{1,0:T(8,128)(2,1)S(1)} %slice.15), channel_id=1, source_target_pairs={{0,2},{1,3},{2,0},{3,1},{4,6},{5,7},{6,4},{7,5}} | collective-permute-start | bytes 1253384 | tf_op jit(solution)/shard_map/ppermute | solution.py:449
  67.3 19.2 %collective-permute-start.12 = (bf16[256,1536]{1,0:T(8,128)(2,1)S(1)}, bf16[256,1536]{1,0:T(8,128)(2,1)S(1)}, u32[]{:S(2)}, u32[]{:S(2)}) collective-permute-start(bf16[256,1536]{1,0:T(8,128)(2,1)S(1)} %slice.14), channel_id=1, source_target_pairs={{0,4},{1,5},{2,6},{3,7},{4,0},{5,1},{6,2},{7,3}} | collective-permute-start | bytes 2359304 | tf_op jit(solution)/shard_map/ppermute | solution.py:449
  86.5 5.5 %collective-permute-start.14 = (bf16[256,1536]{1,0:T(8,128)(2,1)S(1)}, bf16[256,1536]{1,0:T(8,128)(2,1)S(1)}, u32[]{:S(2)}, u32[]{:S(2)}) collective-permute-start(bf16[256,1536]{1,0:T(8,128)(2,1)S(1)} %collective-permute-done.12.refs_0_), channel_id=1, source_target_pairs={{0,1},{1,0},{2,3},{3,2},{4,5},{5,4},{6,7},{7,6}} | collective-permute-start | bytes 2359304 | tf_op jit(solution)/shard_map/ppermute | solution.py:449
  86.6 20.0 %collective-permute-start.9 = (bf16[1024,384]{1,0:T(8,128)(2,1)S(1)}, bf16[1024,384]{1,0:T(8,128)(2,1)S(1)}, u32[]{:S(2)}, u32[]{:S(2)}) collective-permute-start(bf16[1024,384]{1,0:T(8,128)(2,1)S(1)} %slice.13), channel_id=1, source_target_pairs={{0,2},{1,3},{2,0},{3,1},{4,6},{5,7},{6,4},{7,5}} | collective-permute-start | bytes 2359304 | tf_op jit(solution)/shard_map/ppermute | solution.py:449
  86.9 5.1 %collective-permute-start.15 = (bf16[136,1536]{1,0:T(8,128)(2,1)S(1)}, bf16[136,1536]{1,0:T(8,128)(2,1)S(1)}, u32[]{:S(2)}, u32[]{:S(2)}) collective-permute-start(bf16[136,1536]{1,0:T(8,128)(2,1)S(1)} %collective-permute-done.13.refs_1_), channel_id=1, source_target_pairs={{0,1},{1,0},{2,3},{3,2},{4,5},{5,4},{6,7},{7,6}} | collective-permute-start | bytes 1253384 | tf_op jit(solution)/shard_map/ppermute | solution.py:449
  87.2 11.3 %collective-permute-start.8 = (bf16[512,384]{1,0:T(8,128)(2,1)S(1)}, bf16[512,384]{1,0:T(8,128)(2,1)S(1)}, u32[]{:S(2)}, u32[]{:S(2)}) collective-permute-start(bf16[512,384]{1,0:T(8,128)(2,1)S(1)} %slice.12), channel_id=1, source_target_pairs={{0,4},{1,5},{2,6},{3,7},{4,0},{5,1},{6,2},{7,3}} | collective-permute-start | bytes 1179656 | tf_op jit(solution)/shard_map/ppermute | solution.py:449
  106.5 3.2 %collective-permute-start.17 = (bf16[1024,384]{1,0:T(8,128)(2,1)S(1)}, bf16[1024,384]{1,0:T(8,128)(2,1)S(1)}, u32[]{:S(2)}, u32[]{:S(2)}) collective-permute-start(bf16[1024,384]{1,0:T(8,128)(2,1)S(1)} %collective-permute-done.9.refs_1_), channel_id=1, source_target_pairs={{0,1},{1,0},{2,3},{3,2},{4,5},{5,4},{6,7},{7,6}} | collective-permute-start | bytes 2359304 | tf_op jit(solution)/shard_map/ppermute | solution.py:449
  106.5 3.2 %collective-permute-start.16 = (bf16[512,384]{1,0:T(8,128)(2,1)S(1)}, bf16[512,384]{1,0:T(8,128)(2,1)S(1)}, u32[]{:S(2)}, u32[]{:S(2)}) collective-permute-start(bf16[512,384]{1,0:T(8,128)(2,1)S(1)} %collective-permute-done.8.refs_0_), channel_id=1, source_target_pairs={{0,1},{1,0},{2,3},{3,2},{4,5},{5,4},{6,7},{7,6}} | collective-permute-start | bytes 1179656 | tf_op jit(solution)/shard_map/ppermute | solution.py:449
